TPU v7x, 32 devices: a whole 2x2x4 slice. The times are simulated.
32 devices in a mesh: fsdp: 8 (over y, x, core), ctx: 4 (over z).
Axes of the slice: x: 2, y: 2, z: 4, core: 2. Of those that a mesh axis runs over, the one named last changes fastest.
Arguments:
- tokens: bfloat16 [8, 1024, 1024], P('fsdp', 'ctx'), may hold values from -6 to 6
- segments: int32 [8, 1024], P('fsdp', 'ctx'), may hold values from 0 to 7, never falling along the last dimension, each value on 1 to 512 neighbouring positions
- cotangent: bfloat16 [8, 1024, 1024], P('fsdp', 'ctx'), may hold values from -6 to 6
- attn_gain: bfloat16 [1024], P('fsdp'), may hold values from 0.5 to 1.5
- w_query: bfloat16 [1024, 2048], P('fsdp'), may hold values from -0.1875 to 0.1875
- key_matrix: bfloat16 [1024, 1024], P('fsdp'), may hold values from -0.1875 to 0.1875
- value_matrix: bfloat16 [1024, 1024], P('fsdp'), may hold values from -0.1875 to 0.1875
- w_out: bfloat16 [2048, 1024], P('fsdp'), may hold values from -1 to 1
- query_gain: bfloat16 [128], replicated, may hold values from 0.099609375 to 1.8984375
- key_gain: bfloat16 [128], replicated, may hold values from 0.099609375 to 1.8984375
- ffn_gain: bfloat16 [1024], P('fsdp'), may hold values from 0.5 to 1.5
- w_gate: bfloat16 [1024, 3072], P('fsdp'), may hold values from -0.1875 to 0.1875
- w_up: bfloat16 [1024, 3072], P('fsdp'), may hold values from -0.1875 to 0.1875
- w_down: bfloat16 [3072, 1024], P('fsdp'), may hold values from -0.109375 to 0.109375
Outputs:
- output: bfloat16 [8, 1024, 1024], P('fsdp', 'ctx')
- input_grad: float32 [8, 1024, 1024], P('fsdp', 'ctx')
- attn_gain_grad: float32 [1024], P('fsdp')
- w_query_grad: float32 [1024, 2048], P('fsdp')
- w_key_grad: float32 [1024, 1024], P('fsdp')
- w_value_grad: float32 [1024, 1024], P('fsdp')
- w_out_grad: float32 [2048, 1024], P('fsdp')
- query_gain_grad: float32 [128], replicated
- key_gain_grad: float32 [128], replicated
- ffn_gain_grad: float32 [1024], P('fsdp')
- w_gate_grad: float32 [1024, 3072], P('fsdp')
- w_up_grad: float32 [1024, 3072], P('fsdp')
- w_down_grad: float32 [3072, 1024], P('fsdp')
Inputs may be any that keep to these rules, and one draw needn't show every extreme that they name: `segments`: along each sequence the segment numbers never fall; each number names one document of 1 to 512 tokens, and one document has exactly 512.
All inputs are finite; a program needn't handle non-finite values.
Results may differ from a plain program's by a relative error of at most 0.019.
Values may be sent and summed in bfloat16 or wider, within the bound.
No kernel may reach another device: no remote copies, remote signals or barrier semaphores. Data moves between devices by JAX's collectives and lax.ppermute only.
A program may use at most 192 MiB of HBM per device.

v0:
```python
import math

import jax
import jax.numpy as jnp
from jax import lax
from jax.sharding import PartitionSpec as P

EPS = 1e-06
ROPE_BASE = 1000000.0
NEG = -1e30


def for_sending(x):

    def short(part):
        return part.astype(jnp.bfloat16) if part.dtype == jnp.float32 else part

    return jax.tree.map(short, x)


def norm_forward(values, gain):
    scale = lax.rsqrt(jnp.mean(values * values, axis=-1, keepdims=True) + EPS)
    return (values * scale * gain, scale)


def norm_backward(values, scale, gain, upstream):
    weighted = upstream * gain
    leading = tuple(range(values.ndim - 1))
    gain_grad = jnp.sum(upstream * values * scale, axis=leading)
    inner = jnp.mean(weighted * values, axis=-1, keepdims=True)
    return (scale * weighted - values * scale * scale * scale * inner, gain_grad)


def rotate(values, cosine, sine):
    half = values.shape[-1] // 2
    first = values[..., :half]
    second = values[..., half:]
    return jnp.concatenate(
        [first * cosine - second * sine, second * cosine + first * sine], axis=-1
    )


def rotate_back(upstream, cosine, sine):
    half = upstream.shape[-1] // 2
    first = upstream[..., :half]
    second = upstream[..., half:]
    return jnp.concatenate(
        [first * cosine + second * sine, second * cosine - first * sine], axis=-1
    )


def reduce_grads(terms):
    shares = jax.tree.map(
        lambda part: part.astype(jnp.float32),
        lax.psum_scatter(for_sending(terms), "fsdp", scatter_dimension=0, tiled=True),
    )
    return jax.tree.map(lambda part: part.astype(jnp.float32), lax.psum(for_sending(shares), "ctx"))


def body(
    tokens,
    segments,
    cotangent,
    attn_gain,
    w_query,
    key_matrix,
    value_matrix,
    w_out,
    query_gain,
    key_gain,
    ffn_gain,
    w_gate,
    w_up,
    w_down,
):
    f32 = jnp.float32
    bf16 = jnp.bfloat16
    resid = tokens[0].astype(f32)
    rows = resid.shape[0]
    head_dim = query_gain.shape[0]
    heads = w_query.shape[1] // head_dim
    kv_heads = key_matrix.shape[1] // head_dim
    head_group = heads // kv_heads
    scale = 1.0 / math.sqrt(head_dim)
    offset = lax.axis_index("ctx") * rows
    seg_all = lax.all_gather(segments, "ctx", axis=1, tiled=True)[0]
    span_length = seg_all.shape[0]
    index = jnp.arange(span_length, dtype=jnp.int32)
    begins = jnp.concatenate([jnp.ones((1,), dtype=bool), seg_all[1:] != seg_all[:-1]])
    start = lax.cummax(jnp.where(begins, index, jnp.zeros_like(index)), axis=0)
    place = lax.dynamic_slice_in_dim(index - start, offset, rows).astype(f32)
    seg_mine = lax.dynamic_slice_in_dim(seg_all, offset, rows)
    query_index = offset + jnp.arange(rows, dtype=jnp.int32)
    allowed = (index[None, :] <= query_index[:, None]) & (seg_mine[:, None] == seg_all[None, :])
    half = head_dim // 2
    freq = 1.0 / ROPE_BASE ** (jnp.arange(half, dtype=f32) * 2.0 / head_dim)
    angle = place[:, None] * freq[None, :]
    cosine = jnp.cos(angle)[:, None, :]
    sine = jnp.sin(angle)[:, None, :]
    query_gain_f = query_gain.astype(f32)
    key_gain_f = key_gain.astype(f32)
    attn_parts = (
        lax.all_gather(attn_gain, "fsdp", axis=0, tiled=True),
        lax.all_gather(w_query, "fsdp", axis=0, tiled=True),
        lax.all_gather(key_matrix, "fsdp", axis=0, tiled=True),
        lax.all_gather(value_matrix, "fsdp", axis=0, tiled=True),
        lax.all_gather(w_out, "fsdp", axis=0, tiled=True),
    )
    gain_attn, full_query, full_key, full_value, full_out = attn_parts
    normed, scale_attn = norm_forward(resid, gain_attn.astype(f32))
    attention_normed = normed.astype(bf16)
    query_raw = jnp.dot(attention_normed, full_query, preferred_element_type=f32).reshape(
        rows, heads, head_dim
    )
    key_unnormed = jnp.dot(attention_normed, full_key, preferred_element_type=f32).reshape(
        rows, kv_heads, head_dim
    )
    value_raw = jnp.dot(attention_normed, full_value, preferred_element_type=f32)
    query_normed, query_scale = norm_forward(query_raw, query_gain_f)
    key_normed, key_scale = norm_forward(key_unnormed, key_gain_f)
    query_reduced = rotate(query_normed, cosine, sine).astype(bf16)
    key_low = rotate(key_normed, cosine, sine).reshape(rows, kv_heads * head_dim).astype(bf16)
    value_reduced = value_raw.astype(bf16)
    key_all, value_all = (
        lax.all_gather(key_low, "ctx", axis=0, tiled=True),
        lax.all_gather(value_reduced, "ctx", axis=0, tiled=True),
    )
    key_heads = key_all.reshape(span_length, kv_heads, head_dim).transpose(1, 0, 2)
    value_heads = value_all.reshape(span_length, kv_heads, head_dim).transpose(1, 0, 2)
    query_heads = query_reduced.reshape(rows, kv_heads, head_group, head_dim).transpose(1, 2, 0, 3)

    def scores_of(query_block, key_block):
        raw = jnp.einsum("gtd,sd->gts", query_block, key_block, preferred_element_type=f32) * scale
        return jnp.where(allowed[None], raw, NEG)

    def attend(item):
        query_block, key_block, value_block = item
        scores = scores_of(query_block, key_block)
        peak = jnp.max(scores, axis=-1, keepdims=True)
        exponent = jnp.exp(scores - peak)
        total = jnp.sum(exponent, axis=-1, keepdims=True)
        probs = (exponent / total).astype(bf16)
        context = jnp.einsum("gts,sd->gtd", probs, value_block, preferred_element_type=f32)
        return (context, peak[..., 0] + jnp.log(total[..., 0]))

    context, log_total = lax.map(attend, (query_heads, key_heads, value_heads))
    context_low = context.transpose(2, 0, 1, 3).reshape(rows, heads * head_dim).astype(bf16)
    middle = resid + jnp.dot(context_low, full_out, preferred_element_type=f32)
    ffn_parts = (
        lax.all_gather(ffn_gain, "fsdp", axis=0, tiled=True),
        lax.all_gather(w_gate, "fsdp", axis=0, tiled=True),
        lax.all_gather(w_up, "fsdp", axis=0, tiled=True),
        lax.all_gather(w_down, "fsdp", axis=0, tiled=True),
    )
    gain_ffn, full_gate, full_up, full_down = ffn_parts
    gain_ffn_f = gain_ffn.astype(f32)
    normed, scale_ffn = norm_forward(middle, gain_ffn_f)
    normed_ffn = normed.astype(bf16)
    gate = jnp.dot(normed_ffn, full_gate, preferred_element_type=f32)
    upper = jnp.dot(normed_ffn, full_up, preferred_element_type=f32)
    sigma = jax.nn.sigmoid(gate)
    active = gate * sigma
    hidden = (active * upper).astype(bf16)
    output = middle + jnp.dot(hidden, full_down, preferred_element_type=f32)
    upstream = cotangent[0].astype(f32)
    upstream_low = upstream.astype(bf16)
    down_shares = reduce_grads(
        (jnp.einsum("tf,td->fd", hidden, upstream_low, preferred_element_type=f32),)
    )
    hidden_grad = jnp.einsum("td,fd->tf", upstream_low, full_down, preferred_element_type=f32)
    gate_grad = (hidden_grad * upper * sigma * (1.0 + gate * (1.0 - sigma))).astype(bf16)
    upper_grad = (hidden_grad * active).astype(bf16)
    normed_grad = jnp.einsum("tf,df->td", gate_grad, full_gate, preferred_element_type=f32)
    normed_grad = normed_grad + jnp.einsum(
        "tf,df->td", upper_grad, full_up, preferred_element_type=f32
    )
    middle_part, ffn_gain_term = norm_backward(middle, scale_ffn, gain_ffn_f, normed_grad)
    middle_grad = upstream + middle_part
    gate_term = jnp.einsum("td,tf->df", normed_ffn, gate_grad, preferred_element_type=f32)
    gate_shares = reduce_grads((ffn_gain_term, gate_term))
    upper_term = jnp.einsum("td,tf->df", normed_ffn, upper_grad, preferred_element_type=f32)
    upper_shares = reduce_grads((upper_term,))
    back_parts = (
        lax.all_gather(attn_gain, "fsdp", axis=0, tiled=True),
        lax.all_gather(w_query, "fsdp", axis=0, tiled=True),
        lax.all_gather(key_matrix, "fsdp", axis=0, tiled=True),
        lax.all_gather(value_matrix, "fsdp", axis=0, tiled=True),
        lax.all_gather(w_out, "fsdp", axis=0, tiled=True),
    )
    gain_back, query_back_w, key_back_w, value_back_w, out_back_w = back_parts
    middle_low = middle_grad.astype(bf16)
    out_term = jnp.einsum("ti,td->id", context_low, middle_low, preferred_element_type=f32)
    context_grad = jnp.einsum(
        "td,id->ti", middle_low, out_back_w, preferred_element_type=f32
    ).astype(bf16)
    context_heads = context_grad.reshape(rows, kv_heads, head_group, head_dim).transpose(1, 2, 0, 3)

    def attend_back(item):
        query_block, key_block, value_block, context_block, log_block = item
        scores = scores_of(query_block, key_block)
        probs = jnp.exp(scores - log_block[..., None])
        probs_grad = jnp.einsum(
            "gtd,sd->gts", context_block, value_block, preferred_element_type=f32
        )
        inner = jnp.sum(probs * probs_grad, axis=-1, keepdims=True)
        scores_grad = (probs * (probs_grad - inner)).astype(bf16)
        query_part = (
            jnp.einsum("gts,sd->gtd", scores_grad, key_block, preferred_element_type=f32) * scale
        )
        key_part = (
            jnp.einsum("gts,gtd->sd", scores_grad, query_block, preferred_element_type=f32) * scale
        )
        value_part = jnp.einsum(
            "gts,gtd->sd", probs.astype(bf16), context_block, preferred_element_type=f32
        )
        return (query_part, key_part, value_part)

    query_parts, key_parts, value_parts = lax.map(
        attend_back, (query_heads, key_heads, value_heads, context_heads, log_total)
    )
    key_terms = key_parts.transpose(1, 0, 2).reshape(span_length, kv_heads * head_dim)
    value_terms = value_parts.transpose(1, 0, 2).reshape(span_length, kv_heads * head_dim)
    key_back, value_back = (
        lax.psum_scatter(key_terms, "ctx", scatter_dimension=0, tiled=True),
        lax.psum_scatter(value_terms, "ctx", scatter_dimension=0, tiled=True),
    )
    query_grad = query_parts.transpose(2, 0, 1, 3).reshape(rows, heads, head_dim)
    query_rot = rotate_back(query_grad, cosine, sine)
    query_raw_grad, query_gain_term = norm_backward(query_raw, query_scale, query_gain_f, query_rot)
    key_rot = rotate_back(key_back.reshape(rows, kv_heads, head_dim), cosine, sine)
    key_raw_grad, key_gain_term = norm_backward(key_unnormed, key_scale, key_gain_f, key_rot)
    query_raw_low = query_raw_grad.reshape(rows, heads * head_dim).astype(bf16)
    key_raw_low = key_raw_grad.reshape(rows, kv_heads * head_dim).astype(bf16)
    value_grad_low = value_back.astype(bf16)
    attn_normed_grad = jnp.einsum(
        "ti,di->td", query_raw_low, query_back_w, preferred_element_type=f32
    )
    attn_normed_grad = attn_normed_grad + jnp.einsum(
        "ti,di->td", key_raw_low, key_back_w, preferred_element_type=f32
    )
    attn_normed_grad = attn_normed_grad + jnp.einsum(
        "ti,di->td", value_grad_low, value_back_w, preferred_element_type=f32
    )
    resid_part, attn_gain_term = norm_backward(
        resid, scale_attn, gain_back.astype(f32), attn_normed_grad
    )
    input_grad = middle_grad + resid_part
    query_term = jnp.einsum(
        "td,ti->di", attention_normed, query_raw_low, preferred_element_type=f32
    )
    key_term = jnp.einsum("td,ti->di", attention_normed, key_raw_low, preferred_element_type=f32)
    value_term = jnp.einsum(
        "td,ti->di", attention_normed, value_grad_low, preferred_element_type=f32
    )
    attn_shares = reduce_grads((attn_gain_term, query_term, key_term, value_term, out_term))
    head_gains = lax.psum((query_gain_term, key_gain_term), ("fsdp", "ctx"))
    return (
        output.astype(bf16)[None],
        input_grad[None],
        attn_shares[0],
        attn_shares[1],
        attn_shares[2],
        attn_shares[3],
        attn_shares[4],
        head_gains[0],
        head_gains[1],
        gate_shares[0],
        gate_shares[1],
        upper_shares[0],
        down_shares[0],
    )


def solution(mesh):
    in_specs = (
        P("fsdp", "ctx", None),
        P("fsdp", "ctx"),
        P("fsdp", "ctx", None),
        P("fsdp"),
        P("fsdp", None),
        P("fsdp", None),
        P("fsdp", None),
        P("fsdp", None),
        P(),
        P(),
        P("fsdp"),
        P("fsdp", None),
        P("fsdp", None),
        P("fsdp", None),
    )
    out_specs = (
        P("fsdp", "ctx", None),
        P("fsdp", "ctx", None),
        P("fsdp"),
        P("fsdp", None),
        P("fsdp", None),
        P("fsdp", None),
        P("fsdp", None),
        P(),
        P(),
        P("fsdp"),
        P("fsdp", None),
        P("fsdp", None),
        P("fsdp", None),
    )
    return jax.shard_map(body, mesh=mesh, in_specs=in_specs, out_specs=out_specs, check_vma=False)
```

profile of v0, /device:TPU:0, one launch (start us, length us, event | category | flops | bytes accessed | tf_op | source)
XLA Modules:
  0.0 1235.1 jit_solution(1702905229145286098)
XLA Ops:
  8.7 10.4 all-gather
  19.8 11.4 all_gather.41
  33.6 6.8 all-gather.14.cloned.1.call-done
  40.4 2.9 copy.55
  45.5 24.6 %all-gather.18.cloned.1.call-done = bf16[1024,1024]{1,0:T(8,128)(2,1)} async-done(((bf16[128,1024]{1,0:T(8,128)(2,1)}), bf16[1024,1024]{1,0:T(8,128)(2,1)}) %all-gather.18.cloned.1.call-update) | async-done | bytes 2097168 | tf_op jit(solution)/shard_map/all_gather | solution.py:106
  70.1 3.1 convolution_convert_fusion.8
  76.8 8.9 all-gather.1
  85.8 32.8 %all-gather.16.cloned.1.call-done = bf16[1024,1024]{0,1:T(8,128)(2,1)} async-done(((bf16[256,1024]{0,1:T(8,128)(2,1)}), bf16[1024,1024]{0,1:T(8,128)(2,1)}) %all-gather.16.cloned.1.call-update) | async-done | bytes 2097168 | tf_op jit(solution)/shard_map/all_gather | solution.py:125
  118.5 3.9 copy.57
  122.4 42.0 %all-gather.20.cloned.1.call-done = bf16[1024,1024]{1,0:T(8,128)(2,1)} async-done(((bf16[256,1024]{1,0:T(8,128)(2,1)}), bf16[1024,1024]{1,0:T(8,128)(2,1)}) %all-gather.20.cloned.1.call-update) | async-done | bytes 2097168 | tf_op jit(solution)/shard_map/all_gather | solution.py:126
  164.4 3.3 bitcast_bitcast_fusion
  167.7 33.9 %all-gather.12.cloned.1.call-done = bf16[1024,2048]{1,0:T(8,128)(2,1)} async-done(((bf16[128,2048]{1,0:T(8,128)(2,1)}), bf16[1024,2048]{1,0:T(8,128)(2,1)}) %all-gather.12.cloned.1.call-update) | async-done | bytes 4194320 | tf_op jit(solution)/shard_map/all_gather | solution.py:104
  201.6 6.4 copy.52
  208.0 3.7 multiply_reduce_fusion.3
  216.0 40.5 %while.28 = (s32[]{:T(128)}, bf16[8,2,256,128]{2,3,1,0:T(8,128)(2,1)}, f32[8,2,256]{2,1,0:T(2,128)S(1)}, bf16[8,2,256,128]{3,2,1,0:T(8,128)(2,1)}, bf16[8,1024,1...) while((s32[]{:T(128)}, ...), condition=%wide.region_8.9_spmd.clone, body=%wide.region_5.8_spmd.clone.sunk | while | flops 275512832 | bytes 8282217 | solution.py:146
  223.6 2.4 fusion.152
  248.9 2.5 fusion.152
  256.4 3.9 multiply_reduce_fusion.8
  260.5 26.7 %all-gather.24.cloned.1.call-done = bf16[1024,3072]{1,0:T(8,128)(2,1)} async-done(((bf16[128,3072]{1,0:T(8,128)(2,1)}), bf16[1024,3072]{1,0:T(8,128)(2,1)}) %all-gather.24.cloned.1.call-update) | async-done | bytes 6291472 | tf_op jit(solution)/shard_map/all_gather | solution.py:151
  287.2 6.2 fusion.92
  293.4 41.1 %all-gather.26.cloned.1.call-done = bf16[1024,3072]{1,0:T(8,128)(2,1)} async-done(((bf16[128,3072]{1,0:T(8,128)(2,1)}), bf16[1024,3072]{1,0:T(8,128)(2,1)}) %all-gather.26.cloned.1.call-update) | async-done | bytes 6291472 | tf_op jit(solution)/shard_map/all_gather | solution.py:152
  334.5 6.3 fusion.93
  340.8 41.0 %all-gather.28.cloned.1.call-done = bf16[3072,1024]{1,0:T(8,128)(2,1)} async-done(((bf16[384,1024]{1,0:T(8,128)(2,1)}), bf16[3072,1024]{1,0:T(8,128)(2,1)}) %all-gather.28.cloned.1.call-update) | async-done | bytes 6291472 | tf_op jit(solution)/shard_map/all_gather | solution.py:153
  381.8 9.8 multiply_convert_fusion.1
  391.6 5.8 fusion.94
  404.4 114.4 %while.29 = (s32[]{:T(128)}, f32[8,2,256,128]{3,2,1,0:T(8,128)}, f32[8,1024,128]{1,2,0:T(8,128)}, f32[8,1024,128]{1,2,0:T(8,128)}, bf16[8,2,256,128]{3,2,1,0:T(8...) while((s32[]{:T(128)}, f32[8,2,256,128]{3,2,1,0:T(8,128)}, ...), condition=%wide.region_13.14_spmd.clone, body=%wide.region_11.13_spmd.clone.sunk | while | flops 676789760 | bytes 20993152 | solution.py:218
  526.0 3.4 convolution_convert_fusion.4
  531.0 3.2 convolution_convert_fusion.3
  535.3 5.9 convolution_convert_fusion.2
  541.2 5.8 convolution_convert_fusion.1
  548.5 5.5 convolution_convert_fusion
  554.0 41.7 %reduce-scatter.10.cloned.1.call-done = f32[256,1024]{0,1:T(8,128)} async-done(((f32[1024,1024]{0,1:T(8,128)}), f32[256,1024]{0,1:T(8,128)}) %reduce-scatter.10.cloned.1.call-update) | async-done | bytes 1048592 | tf_op jit(solution)/shard_map/reduce_scatter | solution.py:224
  600.3 75.1 %reduce-scatter.12.cloned.1.call-done = f32[256,1024]{0,1:T(8,128)} async-done(((f32[1024,1024]{0,1:T(8,128)}), f32[256,1024]{0,1:T(8,128)}) %reduce-scatter.12.cloned.1.call-update) | async-done | bytes 1048592 | tf_op jit(solution)/shard_map/reduce_scatter | solution.py:225
  675.4 3.4 convolution_convert_fusion.6
  678.9 51.4 %reduce-scatter.14.cloned.1.call-done = bf16[128,2048]{1,0:T(8,128)(2,1)} async-done(((bf16[1024,2048]{1,0:T(8,128)(2,1)}), bf16[128,2048]{1,0:T(8,128)(2,1)}) %reduce-scatter.14.cloned.1.call-update) | async-done | bytes 524304 | tf_op jit(solution)/shard_map/reduce_scatter | solution.py:55
  730.3 54.6 %reduce-scatter.20.cloned.1.call-done = bf16[256,1024]{1,0:T(8,128)(2,1)} async-done(((bf16[2048,1024]{1,0:T(8,128)(2,1)}), bf16[256,1024]{1,0:T(8,128)(2,1)}) %reduce-scatter.20.cloned.1.call-update) | async-done | bytes 524304 | tf_op jit(solution)/shard_map/reduce_scatter | solution.py:55
  784.8 65.0 %reduce-scatter.22.cloned.1.call-done = bf16[128,3072]{1,0:T(8,128)(2,1)} async-done(((bf16[1024,3072]{1,0:T(8,128)(2,1)}), bf16[128,3072]{1,0:T(8,128)(2,1)}) %reduce-scatter.22.cloned.1.call-update) | async-done | bytes 786448 | tf_op jit(solution)/shard_map/reduce_scatter | solution.py:55
  849.9 65.0 %reduce-scatter.24.cloned.1.call-done = bf16[128,3072]{1,0:T(8,128)(2,1)} async-done(((bf16[1024,3072]{1,0:T(8,128)(2,1)}), bf16[128,3072]{1,0:T(8,128)(2,1)}) %reduce-scatter.24.cloned.1.call-update) | async-done | bytes 786448 | tf_op jit(solution)/shard_map/reduce_scatter | solution.py:55
  914.9 65.0 %reduce-scatter.26.cloned.1.call-done = bf16[384,1024]{1,0:T(8,128)(2,1)} async-done(((bf16[3072,1024]{1,0:T(8,128)(2,1)}), bf16[384,1024]{1,0:T(8,128)(2,1)}) %reduce-scatter.26.cloned.1.call-update) | async-done | bytes 786448 | tf_op jit(solution)/shard_map/reduce_scatter | solution.py:55
  979.9 44.3 %reduce-scatter.16.cloned.1.call-done = bf16[128,1024]{1,0:T(8,128)(2,1)} async-done(((bf16[1024,1024]{1,0:T(8,128)(2,1)}), bf16[128,1024]{1,0:T(8,128)(2,1)}) %reduce-scatter.16.cloned.1.call-update) | async-done | bytes 262160 | tf_op jit(solution)/shard_map/reduce_scatter | solution.py:55
  1024.2 44.3 %reduce-scatter.18.cloned.1.call-done = bf16[128,1024]{1,0:T(8,128)(2,1)} async-done(((bf16[1024,1024]{1,0:T(8,128)(2,1)}), bf16[128,1024]{1,0:T(8,128)(2,1)}) %reduce-scatter.18.cloned.1.call-update) | async-done | bytes 262160 | tf_op jit(solution)/shard_map/reduce_scatter | solution.py:55
  1069.8 3.6 fusion.95
  1073.4 5.6 fusion.60
  1082.0 13.4 %all-reduce.3 = (bf16[1024]{0:T(1024)(128)(2,1)S(1)}, bf16[1024]{0:T(1024)(128)(2,1)S(1)}) all-reduce(bf16[1024]{0:T(1024)(128)(2,1)S(1)} %get-tuple-element.210, bf16[1024]{0:T(1024)(128)(2,1)S(1)} %get-tuple-element.206), channel_id=4, replica_groups=mesh['fsdp'=8,'ctx'=4] {'fsdp'}, use_global_device_ids=true, to_apply=%region_20.21.clone | all-reduce | flops 2048 | bytes 8192
  1095.6 12.2 all-reduce.4
  1108.8 42.5 %all-reduce.2 = (f32[128]{0:T(128)}, f32[128]{0:T(128)}) all-reduce(f32[128]{0:T(128)S(1)} %get-tuple-element.204, f32[128]{0:T(128)S(1)} %get-tuple-element.208), channel_id=1, replica_groups=mesh['fsdp'=8,'ctx'=4] {'fsdp','ctx'}, use_global_device_ids=true, to_apply=%region_31.32 | all-reduce | flops 256 | bytes 2048 | tf_op jit(solution)/shard_map/psum | solution.py:256
  1152.7 66.7 %all-reduce.8.cloned.1.call-done = (bf16[128,2048]{1,0:T(8,128)(2,1)}, bf16[128,1024]{1,0:T(8,128)(2,1)}, bf16[128,1024]{1,0:T(8,128)(2,1)}, bf16[256,1024]{1,0:...) async-done(((bf16[128,2048]{1,0:T(8,128)(2,1)}, bf16[128,1024]{1,0:T(8,128)(2,1)}, bf16[128,1024]{1,0:T(8,128)(2,1)}, ...) | async-done | bytes 3932176 | tf_op jit(solution)/shard_map/psum | solution.py:57
  1219.4 2.5 convert_element_type.222
  (292 shorter events, 199.2 us)
Async XLA Ops:
  7.2 33.2 %all-gather.14.cloned.1.call-start = ((), (), s32[]{:S(2)}) async-start(), calls=%async_computation.10 | async-start | bytes 2359296 | tf_op jit(solution)/shard_map/all_gather | solution.py:105
  7.9 62.2 %all-gather.18.cloned.1.call-start = ((), (), s32[]{:S(2)}) async-start(), calls=%async_computation.12 | async-start | bytes 2359296 | tf_op jit(solution)/shard_map/all_gather | solution.py:106
  8.7 109.9 %all-gather.16.cloned.1.call-start = ((), (), s32[]{:S(2)}) async-start(), calls=%async_computation.11 | async-start | bytes 2621440 | tf_op jit(solution)/shard_map/all_gather | solution.py:125
  40.4 2.9 copy-start
  45.4 119.0 %all-gather.20.cloned.1.call-start = ((), (), s32[]{:S(2)}) async-start(), calls=%async_computation.13 | async-start | bytes 2621440 | tf_op jit(solution)/shard_map/all_gather | solution.py:126
  73.2 3.6 copy-start.32
  73.2 3.6 copy-start.29
  73.3 128.3 %all-gather.12.cloned.1.call-start = ((), (), s32[]{:S(2)}) async-start(), calls=%async_computation.9 | async-start | bytes 4718592 | tf_op jit(solution)/shard_map/all_gather | solution.py:104
  73.9 182.5 %all-gather.22.cloned.1.call-start = ((), (), s32[]{:S(2)}) async-start(), calls=%async_computation.14 | async-start | bytes 4718592 | tf_op jit(solution)/shard_map/all_gather | solution.py:107
  74.4 212.8 %all-gather.24.cloned.1.call-start = ((), (), s32[]{:S(2)}) async-start(), calls=%async_computation.15 | async-start | bytes 7077888 | tf_op jit(solution)/shard_map/all_gather | solution.py:151
  75.2 259.3 %all-gather.26.cloned.1.call-start = ((), (), s32[]{:S(2)}) async-start(), calls=%async_computation.16 | async-start | bytes 7077888 | tf_op jit(solution)/shard_map/all_gather | solution.py:152
  75.9 305.9 %all-gather.28.cloned.1.call-start = ((), (), s32[]{:S(2)}) async-start(), calls=%async_computation.17 | async-start | bytes 7077888 | tf_op jit(solution)/shard_map/all_gather | solution.py:153
  76.7 519.1 %reduce-scatter.10.cloned.1.call-start = ((), (), s32[]{:S(2)}) async-start(), calls=%async_computation.18 | async-start | bytes 5242880 | tf_op jit(solution)/shard_map/reduce_scatter | solution.py:224
  211.7 1.4 copy-start.2
  260.3 139.3 %copy-start.14 = (f32[256,1024]{1,0:T(8,128)}, f32[256,1024]{1,0:T(8,128)S(1)}, u32[]{:S(2)}) copy-start(f32[256,1024]{1,0:T(8,128)S(1)} %get-tuple-element.289) | copy-start | bytes 3145732
  260.5 74.1 %copy-start.9 = (bf16[256,1024]{1,0:T(8,128)(2,1)}, bf16[256,1024]{1,0:T(8,128)(2,1)S(1)}, u32[]{:S(2)}) copy-start(bf16[256,1024]{1,0:T(8,128)(2,1)S(1)} %multiply_convert_fusion.4) | copy-start | bytes 1572868
  293.4 88.4 %copy-start.20 = (bf16[1,256,1024]{2,1,0:T(8,128)(2,1)S(1)}, bf16[1,256,1024]{2,1,0:T(8,128)(2,1)}, u32[]{:S(2)}) copy-start(bf16[1,256,1024]{2,1,0:T(8,128)(2,1)} %param.20) | copy-start | bytes 1572868
  391.6 5.8 copy-start.22
  391.6 5.8 copy-start.21
  391.6 5.8 copy-start.30
  397.5 3.5 copy-start.31
  518.8 156.6 %reduce-scatter.12.cloned.1.call-start = ((), (), s32[]{:S(2)}) async-start(), calls=%async_computation.19 | async-start | bytes 5242880 | tf_op jit(solution)/shard_map/reduce_scatter | solution.py:225
  519.5 210.7 %reduce-scatter.14.cloned.1.call-start = ((), (), s32[]{:S(2)}) async-start(), calls=%async_computation.20 | async-start | bytes 4718592 | tf_op jit(solution)/shard_map/reduce_scatter | solution.py:55
  521.9 1.6 copy-start.3
  524.4 1.7 copy-start.1
  529.5 1.5 copy-start.18
  529.5 255.4 %reduce-scatter.20.cloned.1.call-start = ((), (), s32[]{:S(2)}) async-start(), calls=%async_computation.23 | async-start | bytes 4718592 | tf_op jit(solution)/shard_map/reduce_scatter | solution.py:55
  534.2 315.6 %reduce-scatter.22.cloned.1.call-start = ((), (), s32[]{:S(2)}) async-start(), calls=%async_computation.24 | async-start | bytes 7077888 | tf_op jit(solution)/shard_map/reduce_scatter | solution.py:55
  541.2 373.7 %reduce-scatter.24.cloned.1.call-start = ((), (), s32[]{:S(2)}) async-start(), calls=%async_computation.25 | async-start | bytes 7077888 | tf_op jit(solution)/shard_map/reduce_scatter | solution.py:55
  547.1 1.4 copy-start.16
  547.1 432.8 %reduce-scatter.26.cloned.1.call-start = ((), (), s32[]{:S(2)}) async-start(), calls=%async_computation.26 | async-start | bytes 7077888 | tf_op jit(solution)/shard_map/reduce_scatter | solution.py:55
  554.0 43.1 %copy-start.5 = (f32[256,8,128]{0,2,1:T(8,128)S(1)}, f32[256,8,128]{0,2,1:T(8,128)}, u32[]{:S(2)}) copy-start(f32[256,8,128]{0,2,1:T(8,128)} %copy-done.4) | copy-start | bytes 3145732
  554.0 470.2 %reduce-scatter.16.cloned.1.call-start = ((), (), s32[]{:S(2)}) async-start(), calls=%async_computation.21 | async-start | bytes 2359296 | tf_op jit(solution)/shard_map/reduce_scatter | solution.py:55
  600.0 468.4 %reduce-scatter.18.cloned.1.call-start = ((), (), s32[]{:S(2)}) async-start(), calls=%async_computation.22 | async-start | bytes 2359296 | tf_op jit(solution)/shard_map/reduce_scatter | solution.py:55
  678.8 389.7 %copy-start.33 = (u32[32]{0:T(128)S(1)}, u32[32]{0:T(128)}, u32[]{:S(2)}) copy-start(u32[32]{0:T(128)} %constant.101) | copy-start | bytes 388
  678.8 390.9 %copy-start.13 = (bf16[256,16,128]{0,2,1:T(8,128)(2,1)S(1)}, bf16[256,16,128]{0,2,1:T(8,128)(2,1)}, u32[]{:S(2)}) copy-start(bf16[256,16,128]{0,2,1:T(8,128)(2,1)} %copy-done.12) | copy-start | bytes 3145732
  678.8 540.6 %all-reduce.8.cloned.1.call-start = ((), (), s32[]{:S(2)}) async-start(), calls=%async_computation.27 | async-start | bytes 7864320 | tf_op jit(solution)/shard_map/psum | solution.py:57
  1069.7 3.7 copy-start.15
  1069.8 3.7 copy-start.17
  1073.4 5.6 copy-start.8
  1079.0 1.2 copy-start.11
  1079.0 1.9 copy-start.19
  1219.4 2.6 copy-start.24
  1219.4 3.9 copy-start.23
  1221.9 2.6 copy-start.26
  1223.2 2.4 copy-start.25
  1224.5 2.2 copy-start.28
  1224.5 3.0 copy-start.27
  (5 other events, 5.4 us)
Sparse Core Ops, SparseCore 0:
  9.9 30.4 all-gather.13
  42.3 27.7 all-gather.17
  72.2 46.2 all-gather.15
  120.5 43.8 all-gather.19
  166.1 35.3 all-gather.11
  203.3 36.5 all-gather.21
  241.8 45.3 all-gather.23
  289.1 45.3 all-gather.25
  336.4 45.3 all-gather.27
  518.9 76.7 reduce-scatter.9
  598.1 77.2 reduce-scatter.11
  678.6 51.6 reduce-scatter.13
  733.6 51.1 reduce-scatter.19
  788.1 61.7 reduce-scatter.21
  853.1 61.7 reduce-scatter.23
  918.1 61.7 reduce-scatter.25
  983.1 41.0 reduce-scatter.15
  1027.3 41.0 reduce-scatter.17
  1071.4 147.9 all-reduce.7
where the time goes:
time: 1240 us
  waiting for transfers between devices  827 us (67%)
  matrix products  194 us (16%)
  blocking collectives  98.9 us (8%)
  local copies, waits for them, and re-layouts  63.6 us (5%)
  other arithmetic  34.1 us (3%)
  between operations  15.4 us (1%)
    reduce_scatter x7, waiting for transfers between devices, reduce_grads(): lax.psum_scatter(for_sending(terms), 'fsdp', scatter_dimension=0, tiled=T...  390 us
    reduce_scatter x1, waiting for transfers between devices, body(): lax.psum_scatter(value_terms, 'ctx', scatter_dimension=0, tiled=True)  75.1 us
    psum x1, waiting for transfers between devices, reduce_grads(): lax.psum(for_sending(shares), 'ctx')  66.7 us
    psum x1, blocking collectives, body(): head_gains = lax.psum((query_gain_term, key_gain_term), ('fsdp', 'ctx'))  42.5 us
    all_gather x1, waiting for transfers between devices, body(): lax.all_gather(value_reduced, 'ctx', axis=0, tiled=True)  42 us
    reduce_scatter x1, waiting for transfers between devices, body(): lax.psum_scatter(key_terms, 'ctx', scatter_dimension=0, tiled=True)  41.7 us
    all_gather x1, waiting for transfers between devices, body(): lax.all_gather(w_up, 'fsdp', axis=0, tiled=True)  41.1 us
    all_gather x1, waiting for transfers between devices, body(): lax.all_gather(w_down, 'fsdp', axis=0, tiled=True)  41 us
  transfers between devices with their start and end apart: 19, of which 18 were waited for; matrix products, arithmetic and copies ran while one was open for 11% of the time, Pallas kernels for 0%

commit v1 on v0

v1 whole, which is shorter than its diff:
```python
import functools
import math

import jax
import jax.numpy as jnp
from jax import lax
from jax.experimental import pallas as pl
from jax.experimental.pallas import tpu as pltpu
from jax.sharding import PartitionSpec as P

EPS = 1e-06
ROPE_BASE = 1000000.0
NEG = -1e30
DOC_MAX = 512
QB = 128

f32 = jnp.float32
bf16 = jnp.bfloat16


def mm(a, b, ca, cb):
    return lax.dot_general(a, b, (((ca,), (cb,)), ((), ())), preferred_element_type=f32)


def head_norm(x, gain):
    scale = lax.rsqrt(jnp.mean(x * x, axis=-1, keepdims=True) + EPS)
    return x * scale * gain, scale


def rotate(u, cosine, sine):
    return u * cosine + pltpu.roll(u, u.shape[-1] // 2, axis=1) * sine


def rotate_back(r, cosine, sine):
    return r * cosine - pltpu.roll(r, r.shape[-1] // 2, axis=1) * sine


def mask_bias(segc, segr, lo, halo, width):
    row = lax.broadcasted_iota(jnp.int32, (QB, width), 0)
    col = lax.broadcasted_iota(jnp.int32, (QB, width), 1)
    same = segc[lo : lo + QB, :] == segr[:, lo : lo + width]
    return jnp.where(same & (col <= row + halo), 0.0, NEG)


def attend_kernel(group, halo, q_ref, kv_ref, cos_ref, sin_ref, segc_ref, segr_ref, qg_ref, kg_ref, ctx_ref):
    hd = cos_ref.shape[1]
    rows = q_ref.shape[0]
    width = halo + QB
    scale = 1.0 / math.sqrt(hd)
    cosine, sine = cos_ref[...], sin_ref[...]
    kn, _ = head_norm(kv_ref[:, :hd], kg_ref[...])
    k_low = rotate(kn, cosine, sine).astype(bf16)
    v_low = kv_ref[:, hd:].astype(bf16)
    for i in range(rows // QB):
        lo = i * QB
        bias = mask_bias(segc_ref[0], segr_ref[0], lo, halo, width)
        qs = []
        for h in range(group):
            qn, _ = head_norm(q_ref[lo : lo + QB, h * hd : (h + 1) * hd], qg_ref[...])
            at = halo + lo
            qs.append(rotate(qn, cosine[at : at + QB], sine[at : at + QB]).astype(bf16))
        q_low = jnp.concatenate(qs, axis=0)
        s = mm(q_low, k_low[lo : lo + width], 1, 1)
        e = jnp.exp(s * scale + jnp.concatenate([bias] * group, axis=0))
        p = (e * (1.0 / jnp.sum(e, axis=-1, keepdims=True))).astype(bf16)
        c = mm(p, v_low[lo : lo + width], 1, 0).astype(bf16)
        for h in range(group):
            ctx_ref[lo : lo + QB, h * hd : (h + 1) * hd] = c[h * QB : (h + 1) * QB]


def attend_back_kernel(
    group, halo, q_ref, kv_ref, dc_ref, cos_ref, sin_ref, segc_ref, segr_ref, qg_ref, kg_ref,
    dq_ref, dkv_ref, qgg_ref, kgg_ref, dk_ref, dv_ref,
):
    hd = cos_ref.shape[1]
    rows = q_ref.shape[0]
    width = halo + QB
    scale = 1.0 / math.sqrt(hd)
    cosine, sine = cos_ref[...], sin_ref[...]
    q_gain, k_gain = qg_ref[...], kg_ref[...]

    @pl.when((pl.program_id(0) == 0) & (pl.program_id(1) == 0))
    def _():
        qgg_ref[...] = jnp.zeros_like(qgg_ref)
        kgg_ref[...] = jnp.zeros_like(kgg_ref)

    k_raw = kv_ref[:, :hd]
    kn, k_scale = head_norm(k_raw, k_gain)
    k_low = rotate(kn, cosine, sine).astype(bf16)
    v_low = kv_ref[:, hd:].astype(bf16)
    dk_ref[...] = jnp.zeros_like(dk_ref)
    dv_ref[...] = jnp.zeros_like(dv_ref)
    q_gain_grad = jnp.zeros((1, hd), f32)
    for i in range(rows // QB):
        lo = i * QB
        at = halo + lo
        cq, sq = cosine[at : at + QB], sine[at : at + QB]
        bias = mask_bias(segc_ref[0], segr_ref[0], lo, halo, width)
        raws, scales, lows, dcs = [], [], [], []
        for h in range(group):
            raw = q_ref[lo : lo + QB, h * hd : (h + 1) * hd]
            qn, q_scale = head_norm(raw, q_gain)
            raws.append(raw)
            scales.append(q_scale)
            lows.append(rotate(qn, cq, sq).astype(bf16))
            dcs.append(dc_ref[lo : lo + QB, h * hd : (h + 1) * hd])
        q_low = jnp.concatenate(lows, axis=0)
        dc = jnp.concatenate(dcs, axis=0)
        kw, vw = k_low[lo : lo + width], v_low[lo : lo + width]
        s = mm(q_low, kw, 1, 1)
        e = jnp.exp(s * scale + jnp.concatenate([bias] * group, axis=0))
        p = e * (1.0 / jnp.sum(e, axis=-1, keepdims=True))
        dp = mm(dc, vw, 1, 1)
        inner = jnp.sum(p * dp, axis=-1, keepdims=True)
        ds = (p * (dp - inner)).astype(bf16)
        dq = mm(ds, kw, 1, 0) * scale
        dk_ref[lo : lo + width, :] += mm(ds, q_low, 0, 0)
        dv_ref[lo : lo + width, :] += mm(p.astype(bf16), dc, 0, 0)
        for h in range(group):
            rot = rotate_back(dq[h * QB : (h + 1) * QB], cq, sq)
            raw, sc = raws[h], scales[h]
            b = rot * q_gain
            q_gain_grad += jnp.sum(rot * raw * sc, axis=0, keepdims=True)
            grad = sc * b - raw * (sc * sc * sc * jnp.mean(b * raw, axis=-1, keepdims=True))
            dq_ref[lo : lo + QB, h * hd : (h + 1) * hd] = grad.astype(bf16)
    qgg_ref[...] += q_gain_grad
    rot = rotate_back(dk_ref[...] * scale, cosine, sine)
    b = rot * k_gain
    kgg_ref[...] += jnp.sum(rot * k_raw * k_scale, axis=0, keepdims=True)
    grad = k_scale * b - k_raw * (k_scale * k_scale * k_scale * jnp.mean(b * k_raw, axis=-1, keepdims=True))
    dkv_ref[:, :hd] = grad.astype(bf16)
    dkv_ref[:, hd:] = dv_ref[...].astype(bf16)


def attention_specs(seqs, rows, keys, group, hd):
    return [
        pl.BlockSpec((rows, group * hd), lambda j, g: (j, g)),
        pl.BlockSpec((keys, 2 * hd), lambda j, g: (j, g)),
    ], [
        pl.BlockSpec((keys, hd), lambda j, g: (0, 0)),
        pl.BlockSpec((keys, hd), lambda j, g: (0, 0)),
        pl.BlockSpec((1, rows, 1), lambda j, g: (j, 0, 0)),
        pl.BlockSpec((1, 1, keys), lambda j, g: (j, 0, 0)),
        pl.BlockSpec((1, hd), lambda j, g: (0, 0)),
        pl.BlockSpec((1, hd), lambda j, g: (0, 0)),
    ]


def attend(q_raw, kv_raw, tables, seqs, rows, keys, group, hd):
    heads = kv_raw.shape[1] // (2 * hd)
    first, rest = attention_specs(seqs, rows, keys, group, hd)
    pairs = seqs * heads * group * rows * (keys - rows + QB)
    return pl.pallas_call(
        functools.partial(attend_kernel, group, keys - rows),
        grid=(seqs, heads),
        in_specs=first + rest,
        out_specs=pl.BlockSpec((rows, group * hd), lambda j, g: (j, g)),
        out_shape=jax.ShapeDtypeStruct(q_raw.shape, bf16),
        cost_estimate=pl.CostEstimate(
            flops=4 * pairs * hd, bytes_accessed=q_raw.size * 6 + kv_raw.size * 4, transcendentals=pairs
        ),
        name="attend",
    )(q_raw, kv_raw, *tables)


def attend_back(q_raw, kv_raw, context_grad, tables, seqs, rows, keys, group, hd):
    heads = kv_raw.shape[1] // (2 * hd)
    first, rest = attention_specs(seqs, rows, keys, group, hd)
    pairs = seqs * heads * group * rows * (keys - rows + QB)
    gain_spec = pl.BlockSpec((1, hd), lambda j, g: (0, 0))
    return pl.pallas_call(
        functools.partial(attend_back_kernel, group, keys - rows),
        grid=(seqs, heads),
        in_specs=first + [first[0]] + rest,
        out_specs=[first[0], first[1], gain_spec, gain_spec],
        out_shape=[
            jax.ShapeDtypeStruct(q_raw.shape, bf16),
            jax.ShapeDtypeStruct(kv_raw.shape, bf16),
            jax.ShapeDtypeStruct((1, hd), f32),
            jax.ShapeDtypeStruct((1, hd), f32),
        ],
        scratch_shapes=[pltpu.VMEM((keys, hd), f32), pltpu.VMEM((keys, hd), f32)],
        cost_estimate=pl.CostEstimate(
            flops=10 * pairs * hd, bytes_accessed=q_raw.size * 8 + kv_raw.size * 6, transcendentals=pairs
        ),
        name="attend_back",
    )(q_raw, kv_raw, context_grad, *tables)


def feed_kernel(x_ref, u_ref, wgu_ref, wd_ref, hid_ref, gug_ref, ng_ref, out_ref):
    n = wd_ref.shape[0]
    wgu, wd, u = wgu_ref[...], wd_ref[...], u_ref[...]
    gu = mm(x_ref[...], wgu, 1, 0)
    hg = mm(u, wd, 1, 1)
    gate, upper = gu[:, :n], gu[:, n:]
    sig = 1.0 / (1.0 + jnp.exp(-gate))
    act = gate * sig
    hidden = (act * upper).astype(bf16)
    hid_ref[...] = hidden
    gg = (hg * upper * sig * (1.0 + gate * (1.0 - sig))).astype(bf16)
    ug = (hg * act).astype(bf16)
    gug_ref[:, :n] = gg
    gug_ref[:, n:] = ug
    ng_ref[...] = (mm(gg, wgu[:, :n], 1, 1) + mm(ug, wgu[:, n:], 1, 1)).astype(bf16)
    out_ref[...] = mm(hidden, wd, 1, 0).astype(bf16)


def feed(x, u, wgu, wd, block):
    t, d = x.shape
    n = wd.shape[0]
    row = lambda cols: pl.BlockSpec((block, cols), lambda i: (i, 0))
    whole = lambda a: pl.BlockSpec(a.shape, lambda i: (0, 0), pipeline_mode=pl.Buffered(1))
    return pl.pallas_call(
        feed_kernel,
        grid=(t // block,),
        in_specs=[row(d), row(d), whole(wgu), whole(wd)],
        out_specs=[row(n), row(2 * n), row(d), row(d)],
        out_shape=[
            jax.ShapeDtypeStruct((t, n), bf16),
            jax.ShapeDtypeStruct((t, 2 * n), bf16),
            jax.ShapeDtypeStruct((t, d), bf16),
            jax.ShapeDtypeStruct((t, d), bf16),
        ],
        cost_estimate=pl.CostEstimate(
            flops=14 * t * d * n, bytes_accessed=2 * (4 * t * d + 3 * t * n + 3 * d * n), transcendentals=t * n
        ),
        name="feed",
    )(x, u, wgu, wd)


def row_norm(values, gain):
    scale = lax.rsqrt(jnp.mean(values * values, axis=-1, keepdims=True) + EPS)
    return (values * scale * gain).astype(bf16), scale


def row_norm_back(values, scale, gain, upstream):
    weighted = upstream * gain
    inner = jnp.mean(weighted * values, axis=-1, keepdims=True)
    return scale * weighted - values * (scale * scale * scale * inner)


def build(mesh):
    F, Z = mesh.shape["fsdp"], mesh.shape["ctx"]
    C = F // 2
    assert F == 2 * C and F & (F - 1) == 0 and Z & (Z - 1) == 0 and Z > 1
    chip_bits = [2 << i for i in range(C.bit_length() - 1)]
    z_bits = [1 << i for i in range(Z.bit_length() - 1)]
    sizes = {"fsdp": F, "ctx": Z}

    def hop(x, axis, bit):
        return lax.ppermute(x, axis, [(i, i ^ bit) for i in range(sizes[axis])])

    def shift(x, by):
        return lax.ppermute(x, "ctx", [(i, i + by) for i in range(Z) if 0 <= i + by < Z])

    def gather_chips(piece, c):
        r, n = piece.shape
        out = jnp.zeros((C * r, n), piece.dtype)
        place = lambda buf, part, rel, off=0: lax.dynamic_update_slice(buf, part, ((c ^ rel) * r + off, 0))
        if C == 4:
            x, y = hop(piece, "fsdp", 2), hop(piece, "fsdp", 4)
            h = r // 2
            da, db = hop(x[:h], "fsdp", 4), hop(y[h:], "fsdp", 2)
            for part, rel, off in ((piece, 0, 0), (x, 1, 0), (y, 2, 0), (da, 3, 0), (db, 3, h)):
                out = place(out, part, rel, off)
            return out
        parts = [piece]
        for bit in chip_bits:
            parts = parts + [hop(p, "fsdp", bit) for p in parts]
        for rel, part in enumerate(parts):
            out = place(out, part, rel)
        return out

    def scatter_chips(full, c):
        r = full.shape[0] // C
        parts = [lax.dynamic_slice_in_dim(full, (c ^ rel) * r, r) for rel in range(C)]
        if C == 4:
            h = r // 2
            ra, rb = hop(parts[3][:h], "fsdp", 4), hop(parts[3][h:], "fsdp", 2)
            add = lambda a, b: (a.astype(f32) + b.astype(f32)).astype(bf16)
            px = jnp.concatenate([add(parts[1][:h], ra), parts[1][h:]], axis=0)
            py = jnp.concatenate([parts[2][:h], add(parts[2][h:], rb)], axis=0)
            rx, ry = hop(px, "fsdp", 2), hop(py, "fsdp", 4)
            return parts[0].astype(f32) + rx.astype(f32) + ry.astype(f32)
        parts = [p.astype(f32) for p in parts]
        for bit in reversed(chip_bits):
            half = len(parts) // 2
            got = [hop(p.astype(bf16), "fsdp", bit) for p in parts[half:]]
            parts = [p + g.astype(f32) for p, g in zip(parts[:half], got)]
        return parts[0]

    def z_sum(b, bits):
        for bit in bits:
            b = (b.astype(f32) + hop(b, "ctx", bit).astype(f32)).astype(bf16)
        return b

    def z_sum_split(own, zb):
        h = own.shape[0] // 2
        top, bottom = own[:h], own[h:]
        mine, theirs = jnp.where(zb == 0, top, bottom), jnp.where(zb == 0, bottom, top)
        mine = mine.astype(f32) + hop(theirs.astype(bf16), "ctx", 1).astype(f32)
        b = z_sum(mine.astype(bf16), z_bits[1:])
        o = hop(b, "ctx", 1)
        return jnp.where(zb == 0, jnp.concatenate([b, o]), jnp.concatenate([o, b]))

    def body(
        tokens, segments, cotangent, attn_gain, w_query, key_matrix, value_matrix, w_out,
        query_gain, key_gain, ffn_gain, w_gate, w_up, w_down,
    ):
        me = lax.axis_index("fsdp")
        core, c = me % 2, me // 2
        zb = lax.axis_index("ctx") % 2
        R, D = tokens.shape[1:]
        hd = query_gain.shape[0]
        heads, kv_heads = w_query.shape[1] // hd, key_matrix.shape[1] // hd
        group = heads // F
        kv_split = kv_heads == F
        assert heads % F == 0 and (kv_split or (kv_heads == C and heads == F))
        halos = -(-(DOC_MAX - 1) // R)
        K = (halos + 1) * R
        qc = group * hd
        dr = w_query.shape[0]
        FB = w_down.shape[0]
        FS = FB // 2
        swap = lambda x: hop(x, "fsdp", 1)
        by_core = lambda a, b: jnp.where(core == 0, a, b)

        gains = jnp.stack([attn_gain, ffn_gain])[None]
        other = swap(gains)
        gains = by_core(jnp.concatenate([gains, other]), jnp.concatenate([other, gains]))
        for bit in chip_bits:
            other = hop(gains, "fsdp", bit)
            gains = jnp.where(
                me & bit == 0, jnp.concatenate([gains, other]), jnp.concatenate([other, gains])
            )
        gain_attn = gains[:, 0].reshape(1, D).astype(f32)
        gain_ffn = gains[:, 1].reshape(1, D).astype(f32)

        def columns(w, blocks):
            return jnp.concatenate([w[:, s : s + n] for s, n in blocks], axis=1)

        def qkv_of(k):
            q = columns(w_query, [((2 * i + k) * qc, qc) for i in range(C)])
            kv = []
            for i in range(C):
                b = (2 * i + k if kv_split else i) * hd
                kv += [key_matrix[:, b : b + hd], value_matrix[:, b : b + hd]]
            return jnp.concatenate([q] + kv, axis=1)

        def gu_of(k):
            pick = lambda w, z: columns(w, [((2 * i + k) * FB + z * FS, FS) for i in range(C)])
            return jnp.concatenate(
                [jnp.where(zb == 0, pick(w, 0), pick(w, 1)) for w in (w_gate, w_up)], axis=1
            )

        def chip_rows(of):
            even, odd = of(0), of(1)
            mine, got = by_core(even, odd), swap(by_core(odd, even))
            return by_core(jnp.concatenate([mine, got]), jnp.concatenate([got, mine]))

        w_qkv = gather_chips(chip_rows(qkv_of), c)
        wq, wkv = w_qkv[:, : C * qc], w_qkv[:, C * qc :]

        pad = 16
        seg_rows = jnp.zeros((pad, D), bf16).at[0, :R].set((segments[0] + 1).astype(bf16))
        cur = jnp.concatenate([tokens[0], seg_rows])
        window = [cur]
        for _ in range(halos):
            cur = shift(cur, 1)
            window.insert(0, cur)
        window = jnp.stack(window)
        window = jnp.stack([window, swap(window)])
        seg = window[:, :, R, :R].reshape(2, K).astype(jnp.int32)
        resid = window[:, :, :R].reshape(2, K, D).astype(f32)

        upstream = cotangent[0].astype(f32)
        u = jnp.stack([cotangent[0], hop(cotangent[0], "ctx", 1)])
        u4 = jnp.concatenate([u, swap(u)]).reshape(4 * R, D)

        half = hd // 2
        freq = 1.0 / ROPE_BASE ** (jnp.arange(half, dtype=f32) * 2.0 / hd)
        angle = jnp.arange(K, dtype=f32)[:, None] * freq[None, :]
        cosine, sine = jnp.cos(angle), jnp.sin(angle)
        tables = (
            jnp.concatenate([cosine, cosine], axis=1),
            jnp.concatenate([-sine, sine], axis=1),
            seg[:, K - R :, None],
            seg[:, None, :],
            query_gain.astype(f32)[None],
            key_gain.astype(f32)[None],
        )

        normed, scale_attn = row_norm(resid, gain_attn)
        normed_own = normed[:, K - R :].reshape(2 * R, D)
        normed_all = normed.reshape(2 * K, D)
        q_raw = mm(normed_own, wq, 1, 0)
        kv_raw = mm(normed_all, wkv, 1, 0)
        context = attend(q_raw, kv_raw, tables, 2, R, K, group, hd)
        w_o = gather_chips(w_out, c)
        part = mm(context, w_o, 1, 0)
        middle = resid[0, K - R :] + part[:R] + swap(part[R:].astype(bf16)).astype(f32)

        w_gu = gather_chips(chip_rows(gu_of), c)
        w_d = gather_chips(jnp.where(zb == 0, w_down[:FS], w_down[FS:]), c)
        nf, scale_ffn = row_norm(middle, gain_ffn)
        x = jnp.stack([nf, hop(nf, "ctx", 1)])
        x4 = jnp.concatenate([x, swap(x)]).reshape(4 * R, D)
        hidden, gug, ng, out = feed(x4, u4, w_gu, w_d, R)

        def token_sum(parts):
            parts = parts.reshape(4, R, D)
            s = parts[:2].astype(f32) + swap(parts[2:]).astype(f32)
            return s[0] + hop(s[1].astype(bf16), "ctx", 1).astype(f32)

        normed_grad = token_sum(ng)
        output = (middle + token_sum(out)).astype(bf16)
        ffn_gain_term = jnp.sum(normed_grad * middle * scale_ffn, axis=0)
        middle_grad = upstream + row_norm_back(middle, scale_ffn, gain_ffn, normed_grad)

        d_down = scatter_chips(mm(hidden, u4, 0, 0).astype(bf16), c)
        d_down = z_sum(d_down.astype(bf16), z_bits[1:])
        o = hop(d_down, "ctx", 1)
        d_down = jnp.where(zb == 0, jnp.concatenate([d_down, o]), jnp.concatenate([o, d_down])).astype(f32)

        def core_rows(rows):
            top, bottom = rows[:dr], rows[dr:]
            mine, theirs = by_core(top, bottom), by_core(bottom, top)
            return mine, swap(theirs.astype(bf16)).astype(f32)

        def by_parity(mine, other):
            return by_core(mine, other), by_core(other, mine)

        mine, got = core_rows(scatter_chips(mm(x4, gug, 0, 0).astype(bf16), c))
        mine = z_sum(jnp.concatenate([mine, got]).astype(bf16), z_bits[1:])
        o = hop(mine, "ctx", 1)
        z0, z1 = jnp.where(zb == 0, mine, o), jnp.where(zb == 0, o, mine)
        quarters = [by_parity(q[:dr], q[dr:]) for q in (z0, z1)]

        def unit_columns(base):
            cols = []
            for i in range(C):
                for k in range(2):
                    for z in range(2):
                        s = base + i * FS
                        cols.append(quarters[z][k][:, s : s + FS])
            return jnp.concatenate(cols, axis=1).astype(f32)

        d_gate, d_up = unit_columns(0), unit_columns(C * FS)

        ml = middle_grad.astype(bf16)
        ml2 = jnp.concatenate([ml, swap(ml)])
        context_grad = mm(ml2, w_o, 1, 1).astype(bf16)
        d_out = z_sum_split(scatter_chips(mm(context, ml2, 0, 0).astype(bf16), c), zb).astype(f32)
        dq, dkv, q_gain_term, k_gain_term = attend_back(
            q_raw, kv_raw, context_grad, tables, 2, R, K, group, hd
        )
        d_qkv = jnp.concatenate(
            [mm(normed_own, dq, 0, 0).astype(bf16), mm(normed_all, dkv, 0, 0).astype(bf16)], axis=1
        )
        own_rows = mm(dq, wq, 1, 1).reshape(2, R, D)
        attn_grad = mm(dkv, wkv, 1, 1).reshape(2, K, D)
        attn_grad = attn_grad + jnp.pad(own_rows, ((0, 0), (K - R, 0), (0, 0)))
        attn_grad = attn_grad[0] + swap(attn_grad[1].astype(bf16)).astype(f32)
        attn_gain_term = jnp.sum(attn_grad * resid[0] * scale_attn[0], axis=0)
        carry = attn_grad[:R]
        for i in range(1, halos + 1):
            carry = attn_grad[i * R : (i + 1) * R] + shift(carry.astype(bf16), -1).astype(f32)
        input_grad = middle_grad + row_norm_back(
            resid[0, K - R :], scale_attn[0, K - R :], gain_attn, carry
        )

        mine, got = core_rows(scatter_chips(d_qkv, c))
        if kv_split:
            full = z_sum_split(jnp.concatenate([mine, got]), zb).astype(f32)
            even, odd = by_parity(full[:dr], full[dr:])
        else:
            kv = mine[:, C * qc :] + got[:, C * qc :]
            full = z_sum_split(jnp.concatenate([mine[:, : C * qc], got[:, : C * qc], kv], axis=1), zb).astype(f32)
            even, odd = by_parity(full[:, : C * qc], full[:, C * qc : 2 * C * qc])
            kv = full[:, 2 * C * qc :]
        d_query = jnp.concatenate(
            [p[:, i * qc : (i + 1) * qc] for i in range(C) for p in (even, odd)], axis=1
        )
        if kv_split:
            pick = lambda off: jnp.concatenate(
                [
                    p[:, C * qc + 2 * i * hd + off : C * qc + 2 * i * hd + off + hd]
                    for i in range(C)
                    for p in (even, odd)
                ],
                axis=1,
            )
        else:
            pick = lambda off: jnp.concatenate(
                [kv[:, 2 * i * hd + off : 2 * i * hd + off + hd] for i in range(C)], axis=1
            )
        d_key, d_value = pick(0), pick(hd)

        small = jnp.concatenate([q_gain_term[0], k_gain_term[0], ffn_gain_term, attn_gain_term])
        small = small.reshape(-1, 128)
        for axis, bits in (("fsdp", [1] + chip_bits), ("ctx", z_bits)):
            for bit in bits:
                small = small + hop(small, axis, bit)
        small = small.reshape(-1)
        own_gain = lambda base: lax.dynamic_slice_in_dim(small, base + me * dr, dr)
        return (
            output[None],
            input_grad[None],
            own_gain(2 * hd + D),
            d_query,
            d_key,
            d_value,
            d_out,
            small[:hd],
            small[hd : 2 * hd],
            own_gain(2 * hd),
            d_gate,
            d_up,
            d_down,
        )

    return body


def solution(mesh):
    row = P("fsdp", None)
    token = P("fsdp", "ctx", None)
    in_specs = (token, P("fsdp", "ctx"), token, P("fsdp"), row, row, row, row, P(), P(), P("fsdp"), row, row, row)
    out_specs = (token, token, P("fsdp"), row, row, row, row, P(), P(), P("fsdp"), row, row, row)
    return jax.shard_map(build(mesh), mesh=mesh, in_specs=in_specs, out_specs=out_specs, check_vma=False)
```

time: 1240 us -> 516 us (0.42)
  waiting for transfers between devices: 827 us -> 193 us
  matrix products: 194 us -> 47.5 us
  blocking collectives: 98.9 us -> 0 us
  starting transfers between devices: 0.93 us -> 73.4 us
  Pallas kernels: 0 us -> 58.2 us
  other arithmetic: 34.1 us -> 70.3 us
  between operations: 15.4 us -> 2.64 us
    reduce_scatter x9 -> x0, waiting for transfers between devices: 506 us -> none  [the longest x7 390 us: reduce_grads(): lax.psum_scatter(for_sending(terms), 'fsdp', scatter_dimension=0, tiled=T...]
    all_gather x9 -> x0, waiting for transfers between devices: 249 us -> none  [the longest x1 42 us: body(): lax.all_gather(value_reduced, 'ctx', axis=0, tiled=True)]
    ppermute x0 -> x70, waiting for transfers between devices: none -> 193 us  [the longest x66 187 us: hop(): return lax.ppermute(x, axis, [(i, i ^ bit) for i in range(sizes[axis])])]
    dot_general x77 -> x11, matrix products: 194 us -> 47.5 us  [mm(): lax.dot_general(a, b, (((ca,), (cb,)), ((), ())), preferred_element_type=...]
    ppermute x0 -> x70, starting transfers between devices: none -> 73.4 us  [the longest x66 63 us: hop(): return lax.ppermute(x, axis, [(i, i ^ bit) for i in range(sizes[axis])])]
    psum x1 -> x0, waiting for transfers between devices: 66.7 us -> none  [reduce_grads(): lax.psum(for_sending(shares), 'ctx')]
    pallas_call x0 -> x3, Pallas kernels: none -> 58.2 us  [the longest x1 26.5 us: attend_back(): pl.pallas_call(functools.partial(attend_back_kernel, group, keys - rows),...]
    psum x2 -> x0, blocking collectives: 54.7 us -> none  [the longest x1 42.5 us: body(): head_gains = lax.psum((query_gain_term, key_gain_term), ('fsdp', 'ctx'))]
  transfers between devices with their start and end apart: 19 -> 70, of which waited for: 18 -> 24; matrix products, arithmetic and copies ran while one was open for 11% -> 31% of each run, Pallas kernels for 0% -> 8%
where the time goes in v1:
time: 516 us; the launch traced here: 507 us
  waiting for transfers between devices  193 us (37%)
  starting transfers between devices  73.4 us (14%)
  other arithmetic  70.3 us (14%)
  local copies, waits for them, and re-layouts  62.2 us (12%)
  Pallas kernels  58.2 us (11%)
  matrix products  47.5 us (9%)
    ppermute x66, waiting for transfers between devices, hop(): return lax.ppermute(x, axis, [(i, i ^ bit) for i in range(sizes[axis])])  187 us
    ppermute x66, starting transfers between devices, hop(): return lax.ppermute(x, axis, [(i, i ^ bit) for i in range(sizes[axis])])  63 us
    dot_general x11, matrix products, mm(): lax.dot_general(a, b, (((ca,), (cb,)), ((), ())), preferred_element_type=...  47.5 us
    pallas_call x1, Pallas kernels, attend_back(): pl.pallas_call(functools.partial(attend_back_kernel, group, keys - rows),...  26.5 us
    unnamed x185, local copies, waits for them, and re-layouts  16.8 us
    pallas_call x1, Pallas kernels, attend(): pl.pallas_call(functools.partial(attend_kernel, group, keys - rows), grid...  16 us
    pallas_call x1, Pallas kernels, feed(): pl.pallas_call(feed_kernel, grid=(t // block,), in_specs=[row(d), row(d),...  15.8 us
    dynamic_update_slice x17, local copies, waits for them, and re-layouts, gather_chips(): lax.dynamic_update_slice(buf, part, ((c ^ rel) * r + off, 0))  14.2 us
  transfers between devices with their start and end apart: 70, of which 24 were waited for; matrix products, arithmetic and copies ran while one was open for 31% of the time, Pallas kernels for 8%

profile of v1, /device:TPU:0, one launch (start us, length us, event | category | flops | bytes accessed | tf_op | source)
XLA Modules:
  0.0 507.4 jit_solution(5618815974299016297)
XLA Ops:
  0.7 3.0 collective-permute-start.11
  13.1 4.3 collective-permute-start
  33.4 3.5 collective-permute-start.1
  36.9 2.5 broadcast_in_dim.46
  39.4 2.9 constant_dynamic-update-slice_fusion.59
  55.6 18.6 %collective-permute-done.13 = bf16[128,1024]{1,0:T(8,128)(2,1)S(1)} collective-permute-done((bf16[128,1024]{1,0:T(8,128)(2,1)S(1)}, bf16[128,1024]{1,0:T(8,128)(2,1)S(1)}, u32[]{:S(2)}, u32[]{:S(2)}) %collective-permute-start.13) | collective-permute-done | bytes 262176 | tf_op jit(solution)/shard_map/ppermute | solution.py:251
  82.2 13.2 %collective-permute-done.9 = bf16[128,2048]{0,1:T(8,128)(2,1)S(1)} collective-permute-done((bf16[128,2048]{0,1:T(8,128)(2,1)S(1)}, bf16[128,2048]{0,1:T(8,128)(2,1)S(1)}, u32[]{:S(2)}, u32[]{:S(2)}) %collective-permute-start.9) | collective-permute-done | bytes 524320 | tf_op jit(solution)/shard_map/ppermute | solution.py:251
  98.2 3.1 fusion.3
  101.3 3.4 fusion.1
  104.7 8.2 %fusion.11.kv_ref = f32[1536,1024]{1,0:T(8,128)} fusion(bf16[1536,1024]{1,0:T(8,128)(2,1)S(1)} %fusion.1, bf16[1024,2048]{0,1:T(8,128)(2,1)} %constant_dynamic-update-slice_fusion.55), kind=kOutput, calls=%fused_computation.37 | convolution fusion | flops 3221225472 | bytes 11534336 | tf_op jit(solution)/shard_map/dot_general | solution.py:22
  115.7 4.3 fusion.15.q_ref
  121.5 16.0 %attend.1 = bf16[512,1024]{1,0:T(8,128)(2,1)} custom-call(f32[512,1024]{1,0:T(8,128)} %fusion.15.q_ref, f32[1536,1024]{1,0:T(8,128)} %fusion.11.kv_ref, f32[768,128]{1,0:T(8,128)} %pad_maximum_fusion.15.cos_ref, f32[768,128]{1,0:T(8,128)} %pad_maximum_fusion.16.sin_ref, s32[2,256,1]{2,1,0:T(8,128)} %copy.78.segc_ref, s32[2,1,768]{2,1,0:T(1,128)} %convert.37.segr_ref, ...), custom_call_target="tpu_custom_call" | custom-call | flops 1342177280 | bytes 9437184 | tf_op jit(solution)/shard_map/attend/pallas_call | solution.py:153
  137.5 3.2 fusion.69
  153.0 3.4 collective-permute-done.18
  157.3 12.5 %collective-permute-done.27 = bf16[96,1024]{1,0:T(8,128)(2,1)S(1)} collective-permute-done((bf16[96,1024]{1,0:T(8,128)(2,1)S(1)}, bf16[96,1024]{1,0:T(8,128)(2,1)S(1)}, u32[]{:S(2)}, u32[]{:S(2)}) %collective-permute-start.27) | collective-permute-done | bytes 196640 | tf_op jit(solution)/shard_map/ppermute | solution.py:251
  175.5 7.3 %collective-permute-done.23 = bf16[128,1536]{1,0:T(8,128)(2,1)S(1)} collective-permute-done((bf16[128,1536]{1,0:T(8,128)(2,1)S(1)}, bf16[128,1536]{1,0:T(8,128)(2,1)S(1)}, u32[]{:S(2)}, u32[]{:S(2)}) %collective-permute-start.23) | collective-permute-done | bytes 393248 | tf_op jit(solution)/shard_map/ppermute | solution.py:251
  186.5 15.8 %feed.1 = (bf16[1024,768]{1,0:T(8,128)(2,1)}, bf16[1024,1536]{1,0:T(8,128)(2,1)}, bf16[1024,1024]{1,0:T(8,128)(2,1)}, bf16[1024,1024]{1,0:T(8,128)(2,1)}) custom-call(bf16[1024,1024]{1,0:T(8,128)(2,1)} %bitcast.152, bf16[1024,1024]{1,0:T(8,128)(2,1)} %bitcast.150, bf16[1024,1536]{1,0:T(8,128)(2,1)} %copy-done.6, ...), custom_call_target="tpu_custom_call" | custom-call | flops 11274289152 | bytes 17825792 | tf_op jit(solution)/shard_map/feed/pallas_call | solution.py:213
  202.3 4.0 convolution_convert_fusion.4
  207.5 4.2 convolution_convert_fusion
  216.8 5.0 collective-permute-done.57
  223.3 2.1 collective-permute-done.59
  225.7 5.8 %collective-permute-done.65 = bf16[192,1024]{1,0:T(8,128)(2,1)S(1)} collective-permute-done((bf16[192,1024]{1,0:T(8,128)(2,1)S(1)}, bf16[192,1024]{1,0:T(8,128)(2,1)S(1)}, u32[]{:S(2)}, u32[]{:S(2)}) %collective-permute-start.65) | collective-permute-done | bytes 393248 | tf_op jit(solution)/shard_map/ppermute | solution.py:251
  234.6 15.1 %collective-permute-done.68 = bf16[192,1024]{1,0:T(8,128)(2,1)S(1)} collective-permute-done((bf16[192,1024]{1,0:T(8,128)(2,1)S(1)}, bf16[192,1024]{1,0:T(8,128)(2,1)S(1)}, u32[]{:S(2)}, u32[]{:S(2)}) %collective-permute-start.68) | collective-permute-done | bytes 393248 | tf_op jit(solution)/shard_map/ppermute | solution.py:251
  254.9 28.8 %collective-permute-done.32 = bf16[256,1024]{1,0:T(8,128)(2,1)S(1)} collective-permute-done((bf16[256,1024]{1,0:T(8,128)(2,1)S(1)}, bf16[256,1024]{1,0:T(8,128)(2,1)S(1)}, u32[]{:S(2)}, u32[]{:S(2)}) %collective-permute-start.32) | collective-permute-done | bytes 524320 | tf_op jit(solution)/shard_map/ppermute | solution.py:251
  287.2 2.1 slice.821
  291.9 2.8 fusion.34
  297.3 4.2 convolution_convert_fusion.5.dc_ref
  301.5 26.5 %attend_back.1 = (bf16[512,1024]{1,0:T(8,128)(2,1)}, bf16[1536,1024]{1,0:T(8,128)(2,1)}, f32[1,128]{1,0:T(1,128)}, f32[1,128]{1,0:T(1,128)}) custom-call(f32[512,1024]{1,0:T(8,128)} %fusion.15.q_ref, f32[1536,1024]{1,0:T(8,128)} %fusion.11.kv_ref, bf16[512,1024]{1,0:T(8,128)(2,1)} %convolution_convert_fusion.5.dc_ref, ...), custom_call_target="tpu_custom_call" | custom-call | flops 3355443200 | bytes 13631488 | tf_op jit(solution)/shard_map/attend_back/pallas_call | solution.py:171
  327.9 2.9 convolution_convert_fusion.3
  330.9 3.0 fusion.13
  334.3 3.9 convolution_convert_fusion.2
  338.3 7.0 %fusion.9 = f32[1536,1024]{1,0:T(8,128)} fusion(bf16[1536,1024]{1,0:T(8,128)(2,1)S(1)} %copy-done.57, bf16[1024,2048]{0,1:T(8,128)(2,1)} %constant_dynamic-update-slice_fusion.55), kind=kOutput, calls=%fused_computation.35 | convolution fusion | flops 3221225472 | bytes 11534336 | tf_op jit(solution)/shard_map/dot_general | solution.py:22
  345.3 2.5 convolution_convert_fusion.1
  356.0 3.7 pad_add_fusion
  366.5 2.4 collective-permute-done.42
  370.7 9.5 %collective-permute-done.51 = bf16[256,1024]{1,0:T(8,128)(2,1)S(1)} collective-permute-done((bf16[256,1024]{1,0:T(8,128)(2,1)S(1)}, bf16[256,1024]{1,0:T(8,128)(2,1)S(1)}, u32[]{:S(2)}, u32[]{:S(2)}) %collective-permute-start.51) | collective-permute-done | bytes 524320 | tf_op jit(solution)/shard_map/ppermute | solution.py:251
  386.8 2.4 collective-permute-done.54
  389.3 2.3 collective-permute-start.55
  394.3 10.2 %collective-permute-done.43 = bf16[256,2048]{0,1:T(8,128)(2,1)S(1)} collective-permute-done((bf16[256,2048]{0,1:T(8,128)(2,1)S(1)}, bf16[256,2048]{0,1:T(8,128)(2,1)S(1)}, u32[]{:S(2)}, u32[]{:S(2)}) %collective-permute-start.43) | collective-permute-done | bytes 1048608 | tf_op jit(solution)/shard_map/ppermute | solution.py:251
  404.6 4.3 collective-permute-done.45
  418.2 2.7 collective-permute-start.40
  428.4 8.2 %collective-permute-done.40 = f32[18,128]{1,0:T(8,128)} collective-permute-done((f32[18,128]{1,0:T(8,128)S(1)}, f32[18,128]{1,0:T(8,128)}, u32[]{:S(2)}, u32[]{:S(2)}) %collective-permute-start.40) | collective-permute-done | bytes 9248 | tf_op jit(solution)/shard_map/ppermute | solution.py:251
  437.7 2.3 fusion.39
  447.5 5.4 %collective-permute-start.48 = (bf16[128,2048]{0,1:T(8,128)(2,1)S(1)}, bf16[128,2048]{0,1:T(8,128)(2,1)S(1)}, u32[]{:S(2)}, u32[]{:S(2)}) collective-permute-start(bf16[128,2048]{0,1:T(8,128)(2,1)S(1)} %fusion.20), channel_id=1, source_target_pairs={{0,2},{1,3},{2,0},{3,1},{4,6},{5,7},{6,4},{7,5},{8,10},{9,11},{10,... | collective-permute-start | bytes 1572872 | tf_op jit(solution)/shard_map/ppermute | solution.py:251
  454.0 6.6 %collective-permute-done.36 = bf16[256,1024]{1,0:T(8,128)(2,1)S(1)} collective-permute-done((bf16[256,1024]{1,0:T(8,128)(2,1)S(1)}, bf16[256,1024]{1,0:T(8,128)(2,1)S(1)}, u32[]{:S(2)}, u32[]{:S(2)}) %collective-permute-start.36) | collective-permute-done | bytes 524320 | tf_op jit(solution)/shard_map/ppermute | solution.py:254
  462.1 22.1 %collective-permute-done.48 = bf16[128,2048]{0,1:T(8,128)(2,1)S(1)} collective-permute-done((bf16[128,2048]{0,1:T(8,128)(2,1)S(1)}, bf16[128,2048]{0,1:T(8,128)(2,1)S(1)}, u32[]{:S(2)}, u32[]{:S(2)}) %collective-permute-start.48) | collective-permute-done | bytes 524320 | tf_op jit(solution)/shard_map/ppermute | solution.py:251
  484.4 2.5 add_bitcast_fusion
  486.9 8.8 %collective-permute-done.49 = bf16[128,2048]{0,1:T(8,128)(2,1)S(1)} collective-permute-done((bf16[128,2048]{0,1:T(8,128)(2,1)S(1)}, bf16[128,2048]{0,1:T(8,128)(2,1)S(1)}, u32[]{:S(2)}, u32[]{:S(2)}) %collective-permute-start.49) | collective-permute-done | bytes 524320 | tf_op jit(solution)/shard_map/ppermute | solution.py:251
  (450 shorter events, 166.1 us)
Async XLA Ops:
  0.7 46.6 %collective-permute-start.11 = (bf16[256,1024]{1,0:T(8,128)(2,1)}, bf16[256,1024]{1,0:T(8,128)(2,1)}, u32[]{:S(2)}, u32[]{:S(2)}) collective-permute-start(bf16[256,1024]{1,0:T(8,128)(2,1)} %param.23), channel_id=1, source_target_pairs={{0,8},{4,12},{8,0},{12,4},{16,24},{20,28},{24,16},{28,20},{1,9},{5... | collective-permute-start | bytes 1572872 | tf_op jit(solution)/shard_map/ppermute | solution.py:251
  3.7 46.6 %collective-permute-start.12 = (bf16[256,1024]{1,0:T(8,128)(2,1)}, bf16[256,1024]{1,0:T(8,128)(2,1)}, u32[]{:S(2)}, u32[]{:S(2)}) collective-permute-start(bf16[256,1024]{1,0:T(8,128)(2,1)} %param.23), channel_id=1, source_target_pairs={{0,16},{4,20},{8,24},{12,28},{16,0},{20,4},{24,8},{28,12},{1,17},{... | collective-permute-start | bytes 1572872 | tf_op jit(solution)/shard_map/ppermute | solution.py:251
  11.6 25.3 %collective-permute-start.6 = (bf16[128,2048]{0,1:T(8,128)(2,1)}, bf16[128,2048]{0,1:T(8,128)(2,1)}, u32[]{:S(2)}, u32[]{:S(2)}) collective-permute-start(bf16[128,2048]{0,1:T(8,128)(2,1)} %get-tuple-element.133), channel_id=1, source_target_pairs={{0,4},{4,0},{8,12},{12,8},{16,20},{20,16},{24,28},{28,24},{1,5},{5... | collective-permute-start | bytes 1572872 | tf_op jit(solution)/shard_map/ppermute | solution.py:251
  11.6 17.2 %collective-permute-start.3 = (bf16[1,2,128]{2,1,0:T(2,128)(2,1)S(1)}, bf16[1,2,128]{2,1,0:T(2,128)(2,1)S(1)}, u32[]{:S(2)}, u32[]{:S(2)}) collective-permute-start(bf16[1,2,128]{2,1,0:T(2,128)(2,1)S(1)} %maximum_bitcast_fusion.1), channel_id=1, source_target_pairs={{0,4},{4,0},{8,12},{12,8},{16,20},{20,16},{24,28},{28,24},{1,5},{5... | collective-permute-start | bytes 1544 | tf_op jit(solution)/shard_map/ppermute | solution.py:251
  13.1 20.3 %collective-permute-start = (bf16[272,1024]{1,0:T(8,128)(2,1)}, bf16[272,1024]{1,0:T(8,128)(2,1)}, u32[]{:S(2)}, u32[]{:S(2)}) collective-permute-start(bf16[272,1024]{1,0:T(8,128)(2,1)} %get-tuple-element.175), channel_id=1, source_target_pairs={{0,1},{1,2},{2,3},{4,5},{5,6},{6,7},{8,9},{9,10},{10,11},{12,13},{... | collective-permute-start | bytes 1671176 | tf_op jit(solution)/shard_map/ppermute | solution.py:254
  33.4 15.3 %collective-permute-start.1 = (bf16[272,1024]{1,0:T(8,128)(2,1)}, bf16[272,1024]{1,0:T(8,128)(2,1)}, u32[]{:S(2)}, u32[]{:S(2)}) collective-permute-start(bf16[272,1024]{1,0:T(8,128)(2,1)} %collective-permute-done), channel_id=1, source_target_pairs={{0,1},{1,2},{2,3},{4,5},{5,6},{6,7},{8,9},{9,10},{10,11},{12,13},{... | collective-permute-start | bytes 1671176 | tf_op jit(solution)/shard_map/ppermute | solution.py:254
  42.3 33.2 %collective-permute-start.7 = (bf16[256,2048]{0,1:T(8,128)(2,1)}, bf16[256,2048]{0,1:T(8,128)(2,1)S(1)}, u32[]{:S(2)}, u32[]{:S(2)}) collective-permute-start(bf16[256,2048]{0,1:T(8,128)(2,1)} %get-tuple-element.82), channel_id=1, source_target_pairs={{0,8},{4,12},{8,0},{12,4},{16,24},{20,28},{24,16},{28,20},{1,9},{5... | collective-permute-start | bytes 3145736 | tf_op jit(solution)/shard_map/ppermute | solution.py:251
  44.7 33.6 %collective-permute-start.8 = (bf16[256,2048]{0,1:T(8,128)(2,1)}, bf16[256,2048]{0,1:T(8,128)(2,1)S(1)}, u32[]{:S(2)}, u32[]{:S(2)}) collective-permute-start(bf16[256,2048]{0,1:T(8,128)(2,1)} %get-tuple-element.82), channel_id=1, source_target_pairs={{0,16},{4,20},{8,24},{12,28},{16,0},{20,4},{24,8},{28,12},{1,17},{... | collective-permute-start | bytes 3145736 | tf_op jit(solution)/shard_map/ppermute | solution.py:251
  48.2 26.0 %collective-permute-start.13 = (bf16[128,1024]{1,0:T(8,128)(2,1)S(1)}, bf16[128,1024]{1,0:T(8,128)(2,1)S(1)}, u32[]{:S(2)}, u32[]{:S(2)}) collective-permute-start(bf16[128,1024]{1,0:T(8,128)(2,1)S(1)} %slice.802), channel_id=1, source_target_pairs={{0,16},{4,20},{8,24},{12,28},{16,0},{20,4},{24,8},{28,12},{1,17},{... | collective-permute-start | bytes 786440 | tf_op jit(solution)/shard_map/ppermute | solution.py:251
  50.2 47.0 %collective-permute-start.2 = (bf16[3,272,1024]{2,1,0:T(8,128)(2,1)S(1)}, bf16[3,272,1024]{2,1,0:T(8,128)(2,1)S(1)}, u32[]{:S(2)}, u32[]{:S(2)}) collective-permute-start(bf16[3,272,1024]{2,1,0:T(8,128)(2,1)S(1)} %get-tuple-element.104), channel_id=1, source_target_pairs={{0,4},{4,0},{8,12},{12,8},{16,20},{20,16},{24,28},{28,24},{1,5},{5... | collective-permute-start | bytes 5013512 | tf_op jit(solution)/shard_map/ppermute | solution.py:251
  51.3 25.8 %collective-permute-start.14 = (bf16[128,1024]{1,0:T(8,128)(2,1)S(1)}, bf16[128,1024]{1,0:T(8,128)(2,1)S(1)}, u32[]{:S(2)}, u32[]{:S(2)}) collective-permute-start(bf16[128,1024]{1,0:T(8,128)(2,1)S(1)} %slice.803), channel_id=1, source_target_pairs={{0,8},{4,12},{8,0},{12,4},{16,24},{20,28},{24,16},{28,20},{1,9},{5... | collective-permute-start | bytes 786440 | tf_op jit(solution)/shard_map/ppermute | solution.py:251
  74.2 71.9 %collective-permute-start.25 = (bf16[192,1024]{1,0:T(8,128)(2,1)}, bf16[192,1024]{1,0:T(8,128)(2,1)S(1)}, u32[]{:S(2)}, u32[]{:S(2)}) collective-permute-start(bf16[192,1024]{1,0:T(8,128)(2,1)} %get-tuple-element.74), channel_id=1, source_target_pairs={{0,8},{4,12},{8,0},{12,4},{16,24},{20,28},{24,16},{28,20},{1,9},{5... | collective-permute-start | bytes 1179656 | tf_op jit(solution)/shard_map/ppermute | solution.py:251
  75.5 72.2 %collective-permute-start.26 = (bf16[192,1024]{1,0:T(8,128)(2,1)}, bf16[192,1024]{1,0:T(8,128)(2,1)S(1)}, u32[]{:S(2)}, u32[]{:S(2)}) collective-permute-start(bf16[192,1024]{1,0:T(8,128)(2,1)} %get-tuple-element.74), channel_id=1, source_target_pairs={{0,16},{4,20},{8,24},{12,28},{16,0},{20,4},{24,8},{28,12},{1,17},{... | collective-permute-start | bytes 1179656 | tf_op jit(solution)/shard_map/ppermute | solution.py:251
  77.1 18.4 %collective-permute-start.9 = (bf16[128,2048]{0,1:T(8,128)(2,1)S(1)}, bf16[128,2048]{0,1:T(8,128)(2,1)S(1)}, u32[]{:S(2)}, u32[]{:S(2)}) collective-permute-start(bf16[128,2048]{0,1:T(8,128)(2,1)S(1)} %slice.797), channel_id=1, source_target_pairs={{0,16},{4,20},{8,24},{12,28},{16,0},{20,4},{24,8},{28,12},{1,17},{... | collective-permute-start | bytes 1572872 | tf_op jit(solution)/shard_map/ppermute | solution.py:251
  78.4 18.0 %collective-permute-start.10 = (bf16[128,2048]{0,1:T(8,128)(2,1)S(1)}, bf16[128,2048]{0,1:T(8,128)(2,1)S(1)}, u32[]{:S(2)}, u32[]{:S(2)}) collective-permute-start(bf16[128,2048]{0,1:T(8,128)(2,1)S(1)} %slice.798), channel_id=1, source_target_pairs={{0,8},{4,12},{8,0},{12,4},{16,24},{20,28},{24,16},{28,20},{1,9},{5... | collective-permute-start | bytes 1572872 | tf_op jit(solution)/shard_map/ppermute | solution.py:251
  95.4 47.4 %collective-permute-start.20 = (bf16[128,1536]{1,0:T(8,128)(2,1)}, bf16[128,1536]{1,0:T(8,128)(2,1)}, u32[]{:S(2)}, u32[]{:S(2)}) collective-permute-start(bf16[128,1536]{1,0:T(8,128)(2,1)} %get-tuple-element.141), channel_id=1, source_target_pairs={{0,4},{4,0},{8,12},{12,8},{16,20},{20,16},{24,28},{28,24},{1,5},{5... | collective-permute-start | bytes 1179656 | tf_op jit(solution)/shard_map/ppermute | solution.py:251
  142.1 14.3 %collective-permute-start.18 = (bf16[256,1024]{1,0:T(8,128)(2,1)S(1)}, bf16[256,1024]{1,0:T(8,128)(2,1)S(1)}, u32[]{:S(2)}, u32[]{:S(2)}) collective-permute-start(bf16[256,1024]{1,0:T(8,128)(2,1)S(1)} %bitcast.146), channel_id=1, source_target_pairs={{0,1},{1,0},{2,3},{3,2},{4,5},{5,4},{6,7},{7,6},{8,9},{9,8},{10,11... | collective-permute-start | bytes 1572872 | tf_op jit(solution)/shard_map/ppermute | solution.py:251
  144.6 26.6 %collective-permute-start.21 = (bf16[256,1536]{1,0:T(8,128)(2,1)S(1)}, bf16[256,1536]{1,0:T(8,128)(2,1)S(1)}, u32[]{:S(2)}, u32[]{:S(2)}) collective-permute-start(bf16[256,1536]{1,0:T(8,128)(2,1)S(1)} %get-tuple-element.76), channel_id=1, source_target_pairs={{0,8},{4,12},{8,0},{12,4},{16,24},{20,28},{24,16},{28,20},{1,9},{5... | collective-permute-start | bytes 2359304 | tf_op jit(solution)/shard_map/ppermute | solution.py:251
  146.2 26.6 %collective-permute-start.22 = (bf16[256,1536]{1,0:T(8,128)(2,1)S(1)}, bf16[256,1536]{1,0:T(8,128)(2,1)S(1)}, u32[]{:S(2)}, u32[]{:S(2)}) collective-permute-start(bf16[256,1536]{1,0:T(8,128)(2,1)S(1)} %get-tuple-element.76), channel_id=1, source_target_pairs={{0,16},{4,20},{8,24},{12,28},{16,0},{20,4},{24,8},{28,12},{1,17},{... | collective-permute-start | bytes 2359304 | tf_op jit(solution)/shard_map/ppermute | solution.py:251
  147.7 22.1 %collective-permute-start.27 = (bf16[96,1024]{1,0:T(8,128)(2,1)S(1)}, bf16[96,1024]{1,0:T(8,128)(2,1)S(1)}, u32[]{:S(2)}, u32[]{:S(2)}) collective-permute-start(bf16[96,1024]{1,0:T(8,128)(2,1)S(1)} %slice.809), channel_id=1, source_target_pairs={{0,16},{4,20},{8,24},{12,28},{16,0},{20,4},{24,8},{28,12},{1,17},{... | collective-permute-start | bytes 589832 | tf_op jit(solution)/shard_map/ppermute | solution.py:251
  150.7 19.8 %collective-permute-start.28 = (bf16[96,1024]{1,0:T(8,128)(2,1)S(1)}, bf16[96,1024]{1,0:T(8,128)(2,1)S(1)}, u32[]{:S(2)}, u32[]{:S(2)}) collective-permute-start(bf16[96,1024]{1,0:T(8,128)(2,1)S(1)} %slice.810), channel_id=1, source_target_pairs={{0,8},{4,12},{8,0},{12,4},{16,24},{20,28},{24,16},{28,20},{1,9},{5... | collective-permute-start | bytes 589832 | tf_op jit(solution)/shard_map/ppermute | solution.py:251
  156.4 17.2 %collective-permute-start.16 = (bf16[256,1024]{1,0:T(8,128)(2,1)S(1)}, bf16[256,1024]{1,0:T(8,128)(2,1)S(1)}, u32[]{:S(2)}, u32[]{:S(2)}) collective-permute-start(bf16[256,1024]{1,0:T(8,128)(2,1)S(1)} %multiply_convert_fusion), channel_id=1, source_target_pairs={{0,1},{1,0},{2,3},{3,2},{4,5},{5,4},{6,7},{7,6},{8,9},{9,8},{10,11... | collective-permute-start | bytes 1572872 | tf_op jit(solution)/shard_map/ppermute | solution.py:251
  215.4 35.2 %collective-permute-start.29 = (bf16[2,256,1024]{2,1,0:T(8,128)(2,1)S(1)}, bf16[2,256,1024]{2,1,0:T(8,128)(2,1)S(1)}, u32[]{:S(2)}, u32[]{:S(2)}) collective-permute-start(bf16[2,256,1024]{2,1,0:T(8,128)(2,1)S(1)} %bitcast.161), channel_id=1, source_target_pairs={{0,4},{4,0},{8,12},{12,8},{16,20},{20,16},{24,28},{28,24},{1,5},{5... | collective-permute-start | bytes 3145736 | tf_op jit(solution)/shard_map/ppermute | solution.py:251
  215.5 37.7 %collective-permute-start.31 = (bf16[2,256,1024]{2,1,0:T(8,128)(2,1)S(1)}, bf16[2,256,1024]{2,1,0:T(8,128)(2,1)S(1)}, u32[]{:S(2)}, u32[]{:S(2)}) collective-permute-start(bf16[2,256,1024]{2,1,0:T(8,128)(2,1)S(1)} %bitcast.160), channel_id=1, source_target_pairs={{0,4},{4,0},{8,12},{12,8},{16,20},{20,16},{24,28},{28,24},{1,5},{5... | collective-permute-start | bytes 3145736 | tf_op jit(solution)/shard_map/ppermute | solution.py:251
  216.2 15.3 %collective-permute-start.65 = (bf16[192,1024]{1,0:T(8,128)(2,1)S(1)}, bf16[192,1024]{1,0:T(8,128)(2,1)S(1)}, u32[]{:S(2)}, u32[]{:S(2)}) collective-permute-start(bf16[192,1024]{1,0:T(8,128)(2,1)S(1)} %pad_maximum_fusion.19), channel_id=1, source_target_pairs={{0,8},{4,12},{8,0},{12,4},{16,24},{20,28},{24,16},{28,20},{1,9},{5... | collective-permute-start | bytes 1179656 | tf_op jit(solution)/shard_map/ppermute | solution.py:251
  231.7 18.1 %collective-permute-start.68 = (bf16[192,1024]{1,0:T(8,128)(2,1)S(1)}, bf16[192,1024]{1,0:T(8,128)(2,1)S(1)}, u32[]{:S(2)}, u32[]{:S(2)}) collective-permute-start(bf16[192,1024]{1,0:T(8,128)(2,1)S(1)} %add_convert_fusion.5), channel_id=1, source_target_pairs={{0,2},{1,3},{2,0},{3,1},{4,6},{5,7},{6,4},{7,5},{8,10},{9,11},{10,... | collective-permute-start | bytes 1179656 | tf_op jit(solution)/shard_map/ppermute | solution.py:251
  232.1 21.7 %collective-permute-start.58 = (bf16[256,1536]{1,0:T(8,128)(2,1)S(1)}, bf16[256,1536]{1,0:T(8,128)(2,1)S(1)}, u32[]{:S(2)}, u32[]{:S(2)}) collective-permute-start(bf16[256,1536]{1,0:T(8,128)(2,1)S(1)} %pad_maximum_fusion.8), channel_id=1, source_target_pairs={{0,8},{4,12},{8,0},{12,4},{16,24},{20,28},{24,16},{28,20},{1,9},{5... | collective-permute-start | bytes 2359304 | tf_op jit(solution)/shard_map/ppermute | solution.py:251
  233.7 20.0 %collective-permute-start.60 = (bf16[256,1536]{1,0:T(8,128)(2,1)S(1)}, bf16[256,1536]{1,0:T(8,128)(2,1)S(1)}, u32[]{:S(2)}, u32[]{:S(2)}) collective-permute-start(bf16[256,1536]{1,0:T(8,128)(2,1)S(1)} %pad_maximum_fusion.9), channel_id=1, source_target_pairs={{0,16},{4,20},{8,24},{12,28},{16,0},{20,4},{24,8},{28,12},{1,17},{... | collective-permute-start | bytes 2359304 | tf_op jit(solution)/shard_map/ppermute | solution.py:251
  250.6 41.2 %collective-permute-start.69 = (bf16[192,1024]{1,0:T(8,128)(2,1)}, bf16[192,1024]{1,0:T(8,128)(2,1)}, u32[]{:S(2)}, u32[]{:S(2)}) collective-permute-start(bf16[192,1024]{1,0:T(8,128)(2,1)} %add_convert_fusion.4), channel_id=1, source_target_pairs={{0,1},{1,0},{2,3},{3,2},{4,5},{5,4},{6,7},{7,6},{8,9},{9,8},{10,11... | collective-permute-start | bytes 1179656 | tf_op jit(solution)/shard_map/ppermute | solution.py:251
  251.1 33.6 %collective-permute-start.30 = (bf16[256,1024]{1,0:T(8,128)(2,1)S(1)}, bf16[256,1024]{1,0:T(8,128)(2,1)S(1)}, u32[]{:S(2)}, u32[]{:S(2)}) collective-permute-start(bf16[256,1024]{1,0:T(8,128)(2,1)S(1)} %fusion.37), channel_id=1, source_target_pairs={{0,1},{1,0},{2,3},{3,2},{4,5},{5,4},{6,7},{7,6},{8,9},{9,8},{10,11... | collective-permute-start | bytes 1572872 | tf_op jit(solution)/shard_map/ppermute | solution.py:251
  253.7 30.0 %collective-permute-start.32 = (bf16[256,1024]{1,0:T(8,128)(2,1)S(1)}, bf16[256,1024]{1,0:T(8,128)(2,1)S(1)}, u32[]{:S(2)}, u32[]{:S(2)}) collective-permute-start(bf16[256,1024]{1,0:T(8,128)(2,1)S(1)} %fusion.38), channel_id=1, source_target_pairs={{0,1},{1,0},{2,3},{3,2},{4,5},{5,4},{6,7},{7,6},{8,9},{9,8},{10,11... | collective-permute-start | bytes 1572872 | tf_op jit(solution)/shard_map/ppermute | solution.py:251
  254.9 39.7 %collective-permute-start.61 = (bf16[128,1536]{1,0:T(8,128)(2,1)}, bf16[128,1536]{1,0:T(8,128)(2,1)}, u32[]{:S(2)}, u32[]{:S(2)}) collective-permute-start(bf16[128,1536]{1,0:T(8,128)(2,1)} %get-tuple-element.140), channel_id=1, source_target_pairs={{0,4},{4,0},{8,12},{12,8},{16,20},{20,16},{24,28},{28,24},{1,5},{5... | collective-permute-start | bytes 1179656 | tf_op jit(solution)/shard_map/ppermute | solution.py:251
  296.6 63.4 %collective-permute-start.62 = (bf16[256,1536]{1,0:T(8,128)(2,1)}, bf16[256,1536]{1,0:T(8,128)(2,1)}, u32[]{:S(2)}, u32[]{:S(2)}) collective-permute-start(bf16[256,1536]{1,0:T(8,128)(2,1)} %pad_maximum_fusion.10), channel_id=1, source_target_pairs={{0,2},{1,3},{2,0},{3,1},{4,6},{5,7},{6,4},{7,5},{8,10},{9,11},{10,... | collective-permute-start | bytes 2359304 | tf_op jit(solution)/shard_map/ppermute | solution.py:251
  352.3 16.5 %collective-permute-start.42 = (bf16[128,2048]{0,1:T(8,128)(2,1)}, bf16[128,2048]{0,1:T(8,128)(2,1)}, u32[]{:S(2)}, u32[]{:S(2)}) collective-permute-start(bf16[128,2048]{0,1:T(8,128)(2,1)} %get-tuple-element.130), channel_id=1, source_target_pairs={{0,16},{4,20},{8,24},{12,28},{16,0},{20,4},{24,8},{28,12},{1,17},{... | collective-permute-start | bytes 1572872 | tf_op jit(solution)/shard_map/ppermute | solution.py:251
  354.7 29.5 %collective-permute-start.44 = (bf16[128,2048]{0,1:T(8,128)(2,1)}, bf16[128,2048]{0,1:T(8,128)(2,1)}, u32[]{:S(2)}, u32[]{:S(2)}) collective-permute-start(bf16[128,2048]{0,1:T(8,128)(2,1)} %get-tuple-element.131), channel_id=1, source_target_pairs={{0,8},{4,12},{8,0},{12,4},{16,24},{20,28},{24,16},{28,20},{1,9},{5... | collective-permute-start | bytes 1572872 | tf_op jit(solution)/shard_map/ppermute | solution.py:251
  360.0 33.5 %collective-permute-start.34 = (bf16[768,1024]{1,0:T(8,128)(2,1)S(1)}, bf16[768,1024]{1,0:T(8,128)(2,1)S(1)}, u32[]{:S(2)}, u32[]{:S(2)}) collective-permute-start(bf16[768,1024]{1,0:T(8,128)(2,1)S(1)} %fusion.17), channel_id=1, source_target_pairs={{0,4},{4,0},{8,12},{12,8},{16,20},{20,16},{24,28},{28,24},{1,5},{5... | collective-permute-start | bytes 4718600 | tf_op jit(solution)/shard_map/ppermute | solution.py:251
  361.7 29.8 %collective-permute-start.63 = (bf16[256,1536]{1,0:T(8,128)(2,1)S(1)}, bf16[256,1536]{1,0:T(8,128)(2,1)S(1)}, u32[]{:S(2)}, u32[]{:S(2)}) collective-permute-start(bf16[256,1536]{1,0:T(8,128)(2,1)S(1)} %add_convert_fusion), channel_id=1, source_target_pairs={{0,1},{1,0},{2,3},{3,2},{4,5},{5,4},{6,7},{7,6},{8,9},{9,8},{10,11... | collective-permute-start | bytes 2359304 | tf_op jit(solution)/shard_map/ppermute | solution.py:251
  364.8 15.4 %collective-permute-start.51 = (bf16[256,1024]{1,0:T(8,128)(2,1)S(1)}, bf16[256,1024]{1,0:T(8,128)(2,1)S(1)}, u32[]{:S(2)}, u32[]{:S(2)}) collective-permute-start(bf16[256,1024]{1,0:T(8,128)(2,1)S(1)} %pad_maximum_fusion.13), channel_id=1, source_target_pairs={{0,8},{4,12},{8,0},{12,4},{16,24},{20,28},{24,16},{28,20},{1,9},{5... | collective-permute-start | bytes 1572872 | tf_op jit(solution)/shard_map/ppermute | solution.py:251
  380.2 24.3 %collective-permute-start.43 = (bf16[256,2048]{0,1:T(8,128)(2,1)S(1)}, bf16[256,2048]{0,1:T(8,128)(2,1)S(1)}, u32[]{:S(2)}, u32[]{:S(2)}) collective-permute-start(bf16[256,2048]{0,1:T(8,128)(2,1)S(1)} %pad_maximum_fusion.6), channel_id=1, source_target_pairs={{0,8},{4,12},{8,0},{12,4},{16,24},{20,28},{24,16},{28,20},{1,9},{5... | collective-permute-start | bytes 3145736 | tf_op jit(solution)/shard_map/ppermute | solution.py:251
  385.5 23.4 %collective-permute-start.45 = (bf16[256,2048]{0,1:T(8,128)(2,1)S(1)}, bf16[256,2048]{0,1:T(8,128)(2,1)S(1)}, u32[]{:S(2)}, u32[]{:S(2)}) collective-permute-start(bf16[256,2048]{0,1:T(8,128)(2,1)S(1)} %pad_maximum_fusion.7), channel_id=1, source_target_pairs={{0,16},{4,20},{8,24},{12,28},{16,0},{20,4},{24,8},{28,12},{1,17},{... | collective-permute-start | bytes 3145736 | tf_op jit(solution)/shard_map/ppermute | solution.py:251
  389.3 25.6 %collective-permute-start.55 = (bf16[128,1024]{1,0:T(8,128)(2,1)S(1)}, bf16[128,1024]{1,0:T(8,128)(2,1)S(1)}, u32[]{:S(2)}, u32[]{:S(2)}) collective-permute-start(bf16[128,1024]{1,0:T(8,128)(2,1)S(1)} %add_convert_fusion.9), channel_id=1, source_target_pairs={{0,2},{1,3},{2,0},{3,1},{4,6},{5,7},{6,4},{7,5},{8,10},{9,11},{10,... | collective-permute-start | bytes 786440 | tf_op jit(solution)/shard_map/ppermute | solution.py:251
  394.2 15.2 %collective-permute-start.37 = (f32[18,128]{1,0:T(8,128)S(1)}, f32[18,128]{1,0:T(8,128)S(1)}, u32[]{:S(2)}, u32[]{:S(2)}) collective-permute-start(f32[18,128]{1,0:T(8,128)S(1)} %maximum_bitcast_fusion), channel_id=1, source_target_pairs={{0,4},{4,0},{8,12},{12,8},{16,20},{20,16},{24,28},{28,24},{1,5},{5... | collective-permute-start | bytes 27656 | tf_op jit(solution)/shard_map/ppermute | solution.py:251
  415.7 22.0 %collective-permute-start.56 = (bf16[128,1024]{1,0:T(8,128)(2,1)}, bf16[128,1024]{1,0:T(8,128)(2,1)}, u32[]{:S(2)}, u32[]{:S(2)}) collective-permute-start(bf16[128,1024]{1,0:T(8,128)(2,1)} %add_convert_fusion.8), channel_id=1, source_target_pairs={{0,1},{1,0},{2,3},{3,2},{4,5},{5,4},{6,7},{7,6},{8,9},{9,8},{10,11... | collective-permute-start | bytes 786440 | tf_op jit(solution)/shard_map/ppermute | solution.py:251
  416.8 25.2 %collective-permute-start.35 = (bf16[256,1024]{1,0:T(8,128)(2,1)}, bf16[256,1024]{1,0:T(8,128)(2,1)}, u32[]{:S(2)}, u32[]{:S(2)}) collective-permute-start(bf16[256,1024]{1,0:T(8,128)(2,1)} %slice.1043), channel_id=1, source_target_pairs={{1,0},{2,1},{3,2},{5,4},{6,5},{7,6},{9,8},{10,9},{11,10},{13,12},{... | collective-permute-start | bytes 1572872 | tf_op jit(solution)/shard_map/ppermute | solution.py:254
  418.2 18.5 %collective-permute-start.40 = (f32[18,128]{1,0:T(8,128)S(1)}, f32[18,128]{1,0:T(8,128)}, u32[]{:S(2)}, u32[]{:S(2)}) collective-permute-start(f32[18,128]{1,0:T(8,128)S(1)} %add.290), channel_id=1, source_target_pairs={{0,1},{1,0},{2,3},{3,2},{4,5},{5,4},{6,7},{7,6},{8,9},{9,8},{10,11... | collective-permute-start | bytes 27656 | tf_op jit(solution)/shard_map/ppermute | solution.py:251
  421.8 24.5 %collective-permute-start.47 = (bf16[128,2048]{0,1:T(8,128)(2,1)}, bf16[128,2048]{0,1:T(8,128)(2,1)}, u32[]{:S(2)}, u32[]{:S(2)}) collective-permute-start(bf16[128,2048]{0,1:T(8,128)(2,1)} %fusion.21), channel_id=1, source_target_pairs={{0,1},{1,0},{2,3},{3,2},{4,5},{5,4},{6,7},{7,6},{8,9},{9,8},{10,11... | collective-permute-start | bytes 1572872 | tf_op jit(solution)/shard_map/ppermute | solution.py:251
  443.3 17.2 %collective-permute-start.36 = (bf16[256,1024]{1,0:T(8,128)(2,1)S(1)}, bf16[256,1024]{1,0:T(8,128)(2,1)S(1)}, u32[]{:S(2)}, u32[]{:S(2)}) collective-permute-start(bf16[256,1024]{1,0:T(8,128)(2,1)S(1)} %fusion.26), channel_id=1, source_target_pairs={{1,0},{2,1},{3,2},{5,4},{6,5},{7,6},{9,8},{10,9},{11,10},{13,12},{... | collective-permute-start | bytes 1572872 | tf_op jit(solution)/shard_map/ppermute | solution.py:254
  447.5 36.7 %collective-permute-start.48 = (bf16[128,2048]{0,1:T(8,128)(2,1)S(1)}, bf16[128,2048]{0,1:T(8,128)(2,1)S(1)}, u32[]{:S(2)}, u32[]{:S(2)}) collective-permute-start(bf16[128,2048]{0,1:T(8,128)(2,1)S(1)} %fusion.20), channel_id=1, source_target_pairs={{0,2},{1,3},{2,0},{3,1},{4,6},{5,7},{6,4},{7,5},{8,10},{9,11},{10,... | collective-permute-start | bytes 1572872 | tf_op jit(solution)/shard_map/ppermute | solution.py:251
  (82 other events, 552.3 us)

commit v2 on v1

v2 whole, which is shorter than its diff:
```python
import functools
import math

import jax
import jax.numpy as jnp
from jax import lax
from jax.experimental import pallas as pl
from jax.experimental.pallas import tpu as pltpu
from jax.sharding import PartitionSpec as P

EPS = 1e-06
ROPE_BASE = 1000000.0
NEG = -1e30
DOC_MAX = 512
QB = 128

f32 = jnp.float32
bf16 = jnp.bfloat16


def mm(a, b, ca, cb):
    return lax.dot_general(a, b, (((ca,), (cb,)), ((), ())), preferred_element_type=f32)


def head_norm(x, gain):
    scale = lax.rsqrt(jnp.mean(x * x, axis=-1, keepdims=True) + EPS)
    return x * scale * gain, scale


def rotate(u, cosine, sine):
    return u * cosine + pltpu.roll(u, u.shape[-1] // 2, axis=1) * sine


def rotate_back(r, cosine, sine):
    return r * cosine - pltpu.roll(r, r.shape[-1] // 2, axis=1) * sine


def mask_bias(segc, segr, lo, halo, width):
    row = lax.broadcasted_iota(jnp.int32, (QB, width), 0)
    col = lax.broadcasted_iota(jnp.int32, (QB, width), 1)
    same = segc[lo : lo + QB, :] == segr[:, lo : lo + width]
    return jnp.where(same & (col <= row + halo), 0.0, NEG)


def attend_kernel(group, halo, q_ref, kv_ref, cos_ref, sin_ref, segc_ref, segr_ref, qg_ref, kg_ref, ctx_ref):
    hd = cos_ref.shape[1]
    rows = q_ref.shape[0]
    width = halo + QB
    scale = 1.0 / math.sqrt(hd)
    cosine, sine = cos_ref[...], sin_ref[...]
    kn, _ = head_norm(kv_ref[:, :hd], kg_ref[...])
    k_low = rotate(kn, cosine, sine).astype(bf16)
    v_low = kv_ref[:, hd:].astype(bf16)
    for i in range(rows // QB):
        lo = i * QB
        bias = mask_bias(segc_ref[0], segr_ref[0], lo, halo, width)
        qs = []
        for h in range(group):
            qn, _ = head_norm(q_ref[lo : lo + QB, h * hd : (h + 1) * hd], qg_ref[...])
            at = halo + lo
            qs.append(rotate(qn, cosine[at : at + QB], sine[at : at + QB]).astype(bf16))
        q_low = jnp.concatenate(qs, axis=0)
        s = mm(q_low, k_low[lo : lo + width], 1, 1)
        e = jnp.exp(s * scale + jnp.concatenate([bias] * group, axis=0))
        p = (e * (1.0 / jnp.sum(e, axis=-1, keepdims=True))).astype(bf16)
        c = mm(p, v_low[lo : lo + width], 1, 0).astype(bf16)
        for h in range(group):
            ctx_ref[lo : lo + QB, h * hd : (h + 1) * hd] = c[h * QB : (h + 1) * QB]


def attend_back_kernel(
    group, halo, q_ref, kv_ref, dc_ref, cos_ref, sin_ref, segc_ref, segr_ref, qg_ref, kg_ref,
    dq_ref, dkv_ref, qgg_ref, kgg_ref, dk_ref, dv_ref,
):
    hd = cos_ref.shape[1]
    rows = q_ref.shape[0]
    width = halo + QB
    scale = 1.0 / math.sqrt(hd)
    cosine, sine = cos_ref[...], sin_ref[...]
    q_gain, k_gain = qg_ref[...], kg_ref[...]

    @pl.when((pl.program_id(0) == 0) & (pl.program_id(1) == 0))
    def _():
        qgg_ref[...] = jnp.zeros_like(qgg_ref)
        kgg_ref[...] = jnp.zeros_like(kgg_ref)

    k_raw = kv_ref[:, :hd]
    kn, k_scale = head_norm(k_raw, k_gain)
    k_low = rotate(kn, cosine, sine).astype(bf16)
    v_low = kv_ref[:, hd:].astype(bf16)
    dk_ref[...] = jnp.zeros_like(dk_ref)
    dv_ref[...] = jnp.zeros_like(dv_ref)
    q_gain_grad = jnp.zeros((1, hd), f32)
    for i in range(rows // QB):
        lo = i * QB
        at = halo + lo
        cq, sq = cosine[at : at + QB], sine[at : at + QB]
        bias = mask_bias(segc_ref[0], segr_ref[0], lo, halo, width)
        raws, scales, lows, dcs = [], [], [], []
        for h in range(group):
            raw = q_ref[lo : lo + QB, h * hd : (h + 1) * hd]
            qn, q_scale = head_norm(raw, q_gain)
            raws.append(raw)
            scales.append(q_scale)
            lows.append(rotate(qn, cq, sq).astype(bf16))
            dcs.append(dc_ref[lo : lo + QB, h * hd : (h + 1) * hd])
        q_low = jnp.concatenate(lows, axis=0)
        dc = jnp.concatenate(dcs, axis=0)
        kw, vw = k_low[lo : lo + width], v_low[lo : lo + width]
        s = mm(q_low, kw, 1, 1)
        e = jnp.exp(s * scale + jnp.concatenate([bias] * group, axis=0))
        p = e * (1.0 / jnp.sum(e, axis=-1, keepdims=True))
        dp = mm(dc, vw, 1, 1)
        inner = jnp.sum(p * dp, axis=-1, keepdims=True)
        ds = (p * (dp - inner)).astype(bf16)
        dq = mm(ds, kw, 1, 0) * scale
        dk_ref[lo : lo + width, :] += mm(ds, q_low, 0, 0)
        dv_ref[lo : lo + width, :] += mm(p.astype(bf16), dc, 0, 0)
        for h in range(group):
            rot = rotate_back(dq[h * QB : (h + 1) * QB], cq, sq)
            raw, sc = raws[h], scales[h]
            b = rot * q_gain
            q_gain_grad += jnp.sum(rot * raw * sc, axis=0, keepdims=True)
            grad = sc * b - raw * (sc * sc * sc * jnp.mean(b * raw, axis=-1, keepdims=True))
            dq_ref[lo : lo + QB, h * hd : (h + 1) * hd] = grad.astype(bf16)
    qgg_ref[...] += q_gain_grad
    rot = rotate_back(dk_ref[...] * scale, cosine, sine)
    b = rot * k_gain
    kgg_ref[...] += jnp.sum(rot * k_raw * k_scale, axis=0, keepdims=True)
    grad = k_scale * b - k_raw * (k_scale * k_scale * k_scale * jnp.mean(b * k_raw, axis=-1, keepdims=True))
    dkv_ref[:, :hd] = grad.astype(bf16)
    dkv_ref[:, hd:] = dv_ref[...].astype(bf16)


def attention_specs(seqs, rows, keys, group, hd):
    return [
        pl.BlockSpec((rows, group * hd), lambda j, g: (j, g)),
        pl.BlockSpec((keys, 2 * hd), lambda j, g: (j, g)),
    ], [
        pl.BlockSpec((keys, hd), lambda j, g: (0, 0)),
        pl.BlockSpec((keys, hd), lambda j, g: (0, 0)),
        pl.BlockSpec((1, rows, 1), lambda j, g: (j, 0, 0)),
        pl.BlockSpec((1, 1, keys), lambda j, g: (j, 0, 0)),
        pl.BlockSpec((1, hd), lambda j, g: (0, 0)),
        pl.BlockSpec((1, hd), lambda j, g: (0, 0)),
    ]


def attend(q_raw, kv_raw, tables, seqs, rows, keys, group, hd):
    heads = kv_raw.shape[1] // (2 * hd)
    first, rest = attention_specs(seqs, rows, keys, group, hd)
    pairs = seqs * heads * group * rows * (keys - rows + QB)
    return pl.pallas_call(
        functools.partial(attend_kernel, group, keys - rows),
        grid=(seqs, heads),
        in_specs=first + rest,
        out_specs=pl.BlockSpec((rows, group * hd), lambda j, g: (j, g)),
        out_shape=jax.ShapeDtypeStruct(q_raw.shape, bf16),
        cost_estimate=pl.CostEstimate(
            flops=4 * pairs * hd, bytes_accessed=q_raw.size * 6 + kv_raw.size * 4, transcendentals=pairs
        ),
        compiler_params=pltpu.CompilerParams(vmem_limit_bytes=20 << 20),
        name="attend",
    )(q_raw, kv_raw, *tables)


def attend_back(q_raw, kv_raw, context_grad, tables, seqs, rows, keys, group, hd):
    heads = kv_raw.shape[1] // (2 * hd)
    first, rest = attention_specs(seqs, rows, keys, group, hd)
    pairs = seqs * heads * group * rows * (keys - rows + QB)
    gain_spec = pl.BlockSpec((1, hd), lambda j, g: (0, 0))
    return pl.pallas_call(
        functools.partial(attend_back_kernel, group, keys - rows),
        grid=(seqs, heads),
        in_specs=first + [first[0]] + rest,
        out_specs=[first[0], first[1], gain_spec, gain_spec],
        out_shape=[
            jax.ShapeDtypeStruct(q_raw.shape, bf16),
            jax.ShapeDtypeStruct(kv_raw.shape, bf16),
            jax.ShapeDtypeStruct((1, hd), f32),
            jax.ShapeDtypeStruct((1, hd), f32),
        ],
        scratch_shapes=[pltpu.VMEM((keys, hd), f32), pltpu.VMEM((keys, hd), f32)],
        cost_estimate=pl.CostEstimate(
            flops=10 * pairs * hd,
            bytes_accessed=seqs * heads * (8 * rows * group * hd + 12 * keys * hd),
            transcendentals=pairs,
        ),
        compiler_params=pltpu.CompilerParams(vmem_limit_bytes=28 << 20),
        name="attend_back",
    )(q_raw, kv_raw, context_grad, *tables)


def diagonal(gain_ref):
    n = gain_ref.shape[1]
    row = lax.broadcasted_iota(jnp.int32, (n, n), 0)
    col = lax.broadcasted_iota(jnp.int32, (n, n), 1)
    return jnp.where(row == col, gain_ref[...].astype(f32), 0.0).astype(bf16)


def select_kernel(chips, qc, hd, split, core_ref, gain_ref, wq_ref, wk_ref, wv_ref, mine_ref, theirs_ref):
    gain = diagonal(gain_ref)
    for out_ref, k in ((mine_ref, core_ref[0]), (theirs_ref, 1 - core_ref[0])):
        for i in range(chips):
            at = pl.ds(pl.multiple_of((2 * i + k) * qc, qc), qc)
            out_ref[:, i * qc : (i + 1) * qc] = mm(gain, wq_ref[:, at], 1, 0).astype(bf16)
            at = pl.ds(pl.multiple_of((2 * i + k if split else i) * hd, hd), hd)
            base = chips * qc + 2 * i * hd
            out_ref[:, base : base + hd] = mm(gain, wk_ref[:, at], 1, 0).astype(bf16)
            out_ref[:, base + hd : base + 2 * hd] = mm(gain, wv_ref[:, at], 1, 0).astype(bf16)


def small_call(kernel, scalars, args, outs, name):
    spec = lambda a: pl.BlockSpec(a.shape, lambda i, *_: (0,) * len(a.shape), pipeline_mode=pl.Buffered(1))
    size = lambda a: math.prod(a.shape) * a.dtype.itemsize
    return pl.pallas_call(
        kernel,
        grid_spec=pltpu.PrefetchScalarGridSpec(
            num_scalar_prefetch=1,
            grid=(1,),
            in_specs=[spec(a) for a in args],
            out_specs=[spec(o) for o in outs],
        ),
        out_shape=outs,
        cost_estimate=pl.CostEstimate(
            flops=0, bytes_accessed=sum(size(a) for a in (*args, *outs)), transcendentals=0
        ),
        compiler_params=pltpu.CompilerParams(vmem_limit_bytes=16 << 20),
        name=name,
    )(scalars, *args)


def select_qkv(core, gain, wq, wk, wv, chips, qc, hd, split):
    out = jax.ShapeDtypeStruct((wq.shape[0], chips * (qc + 2 * hd)), bf16)
    kernel = functools.partial(select_kernel, chips, qc, hd, split)
    return small_call(kernel, core[None], (gain, wq, wk, wv), (out, out), "select_qkv")


def select_units_kernel(chips, where_ref, gain_ref, wg_ref, wu_ref, mine_ref, theirs_ref):
    n = wg_ref.shape[1] // (4 * chips)
    gain = diagonal(gain_ref)
    for k in range(2):
        for z in range(2):

            @pl.when((where_ref[0] == k) & (where_ref[1] == z))
            def _():
                for out_ref, kk in ((mine_ref, k), (theirs_ref, 1 - k)):
                    for m, w_ref in enumerate((wg_ref, wu_ref)):
                        cols = [w_ref[:, (4 * i + 2 * kk + z) * n : (4 * i + 2 * kk + z + 1) * n] for i in range(chips)]
                        out = mm(gain, jnp.concatenate(cols, axis=1), 1, 0)
                        out_ref[:, m * chips * n : (m + 1) * chips * n] = out.astype(bf16)


def select_units(where, gain, wg, wu, chips):
    out = jax.ShapeDtypeStruct((wg.shape[0], wg.shape[1] // 2), bf16)
    kernel = functools.partial(select_units_kernel, chips)
    return small_call(kernel, where, (gain, wg, wu), (out, out), "select_units")


def place_units_kernel(chips, where_ref, gain_ref, a_ref, b_ref, dg_ref, du_ref):
    dr = dg_ref.shape[0]
    n = dg_ref.shape[1] // (4 * chips)
    gain = diagonal(gain_ref)
    for k in range(2):
        for z in range(2):

            @pl.when((where_ref[0] == k) & (where_ref[1] == z))
            def _():
                for m, out_ref in enumerate((dg_ref, du_ref)):
                    for i in range(chips):
                        cols = []
                        for kk in range(2):
                            for zz in range(2):
                                ref = a_ref if zz == z else b_ref
                                top = 0 if kk == k else dr
                                at = (m * chips + i) * n
                                cols.append(ref[top : top + dr, at : at + n])
                        out_ref[:, 4 * i * n : 4 * (i + 1) * n] = mm(gain, jnp.concatenate(cols, axis=1), 1, 0)


def place_units(where, gain, a, b, chips):
    out = jax.ShapeDtypeStruct((a.shape[0] // 2, 2 * a.shape[1]), f32)
    kernel = functools.partial(place_units_kernel, chips)
    return small_call(kernel, where, (gain, a, b), (out, out), "place_units")


def feed_kernel(chip_ref, xa_ref, xb_ref, ua_ref, ub_ref, wgu_ref, parts, hid_ref, gug_ref, ng_ref, out_ref, wd_ref):
    n = wd_ref.shape[0]
    first = pl.program_id(0) == 0

    @pl.when(first)
    def _():
        rows = n // len(parts)
        for rel, part in enumerate(parts):
            wd_ref[pl.ds(pl.multiple_of((chip_ref[0] ^ rel) * rows, rows), rows), :] = part[...]

    wgu, wd = wgu_ref[...], wd_ref[...]
    gu = mm(jnp.where(first, xa_ref[...], xb_ref[...]), wgu, 1, 0)
    hg = mm(jnp.where(first, ua_ref[...], ub_ref[...]), wd, 1, 1)
    gate, upper = gu[:, :n], gu[:, n:]
    sig = 1.0 / (1.0 + jnp.exp(-gate))
    act = gate * sig
    hidden = (act * upper).astype(bf16)
    hid_ref[...] = hidden
    gg = (hg * upper * sig * (1.0 + gate * (1.0 - sig))).astype(bf16)
    ug = (hg * act).astype(bf16)
    gug_ref[:, :n] = gg
    gug_ref[:, n:] = ug
    ng_ref[...] = (mm(gg, wgu[:, :n], 1, 1) + mm(ug, wgu[:, n:], 1, 1)).astype(bf16)
    out_ref[...] = mm(hidden, wd, 1, 0).astype(bf16)


def feed(xs, us, wgu, wd_parts, chip, first, blocks, into=()):
    r, d = xs[0].shape
    n = wgu.shape[1] // 2
    row = pl.BlockSpec((r, d), lambda i, _: (i, 0))
    block = lambda cols: pl.BlockSpec((r, cols), lambda i, _: (i + first, 0))
    whole = lambda a: pl.BlockSpec(a.shape, lambda i, _: (0, 0), pipeline_mode=pl.Buffered(1))
    shape = lambda rows, cols: jax.ShapeDtypeStruct((rows, cols), bf16)
    args = (*xs, *us, wgu, *wd_parts)
    k = 1 + len(args)
    body = lambda *refs: feed_kernel(*refs[:6], refs[6:k], *refs[k + len(into) :])
    return pl.pallas_call(
        body,
        grid_spec=pltpu.PrefetchScalarGridSpec(
            num_scalar_prefetch=1,
            grid=(2,),
            in_specs=[whole(a) for a in args] + [pl.BlockSpec(memory_space=pl.ANY)] * len(into),
            out_specs=[block(n), block(2 * n), row, row],
            scratch_shapes=[pltpu.VMEM((n, d), bf16)],
        ),
        out_shape=[shape(blocks * r, n), shape(blocks * r, 2 * n)] + [shape(2 * r, d)] * 2,
        input_output_aliases={k + i: i for i in range(len(into))},
        cost_estimate=pl.CostEstimate(
            flops=28 * r * d * n, bytes_accessed=2 * (8 * r * d + 6 * r * n + 3 * d * n), transcendentals=2 * r * n
        ),
        name="feed",
    )(chip[None], *args, *into)


def after(x, *deps):
    return lax.optimization_barrier((x, *deps))[0]


def row_norm(values):
    scale = lax.rsqrt(jnp.mean(values * values, axis=-1, keepdims=True) + EPS)
    return (values * scale).astype(bf16), scale


def row_norm_back(values, scale, weighted):
    inner = jnp.mean(weighted * values, axis=-1, keepdims=True)
    return scale * weighted - values * (scale * scale * scale * inner)


def build(mesh):
    F, Z = mesh.shape["fsdp"], mesh.shape["ctx"]
    C = F // 2
    assert F == 2 * C and F & (F - 1) == 0 and Z & (Z - 1) == 0 and Z > 1
    chip_bits = [2 << i for i in range(C.bit_length() - 1)]
    z_bits = [1 << i for i in range(Z.bit_length() - 1)]
    sizes = {"fsdp": F, "ctx": Z}

    def hop(x, axis, bit):
        return lax.ppermute(x, axis, [(i, i ^ bit) for i in range(sizes[axis])])

    def shift(x, by):
        return lax.ppermute(x, "ctx", [(i, i + by) for i in range(Z) if 0 <= i + by < Z])

    def place(buf, part, c, rel):
        return lax.dynamic_update_slice(buf, part, ((c ^ rel) * (buf.shape[0] // C), 0))

    def by_chip(parts, c, *deps):
        r, n = parts[0].shape
        out = after(jnp.zeros((C * r, n), parts[0].dtype), *deps)
        for rel, part in enumerate(parts):
            out = place(out, part, c, rel)
        return out

    def spread(piece):
        return [piece] + [hop(piece, "fsdp", 2 * rel) for rel in range(1, C)]

    def by_chip_copies(piece):
        return jnp.broadcast_to(piece, (C, *piece.shape))

    def exchange(copies):
        out = lax.all_to_all(copies, "fsdp", 0, 0, axis_index_groups=groups)
        return out.reshape(-1, out.shape[-1])

    groups = [[2 * i + k for i in range(C)] for k in range(2)]

    def scatter(full):
        full = full.reshape(C, -1, full.shape[-1])
        return lax.all_to_all(full, "fsdp", 0, 0, axis_index_groups=groups)

    def scatter_hops(full, c):
        r = full.shape[0] // C
        parts = [lax.dynamic_slice_in_dim(full, (c ^ rel) * r, r) for rel in range(C)]
        return [parts[0]] + [hop(parts[rel], "fsdp", 2 * rel) for rel in range(1, C)]

    def total(parts, *deps):
        if not isinstance(parts, list):
            return jnp.sum(after(parts, *deps).astype(f32), axis=0)
        return functools.reduce(lambda a, b: a + b, [after(p, *deps).astype(f32) for p in parts])

    def z_sum(b, bits):
        for bit in bits:
            b = (b.astype(f32) + hop(b, "ctx", bit).astype(f32)).astype(bf16)
        return b

    def z_sum_split(own, zb):
        h = own.shape[0] // 2
        top, bottom = own[:h], own[h:]
        mine, theirs = jnp.where(zb == 0, top, bottom), jnp.where(zb == 0, bottom, top)
        mine = mine.astype(f32) + hop(theirs.astype(bf16), "ctx", 1).astype(f32)
        b = z_sum(mine.astype(bf16), z_bits[1:])
        o = hop(b, "ctx", 1)
        return jnp.where(zb == 0, jnp.concatenate([b, o]), jnp.concatenate([o, b]))

    def body(
        tokens, segments, cotangent, attn_gain, w_query, key_matrix, value_matrix, w_out,
        query_gain, key_gain, ffn_gain, w_gate, w_up, w_down,
    ):
        me = lax.axis_index("fsdp")
        core, c = me % 2, me // 2
        zb = lax.axis_index("ctx") % 2
        R, D = tokens.shape[1:]
        hd = query_gain.shape[0]
        heads, kv_heads = w_query.shape[1] // hd, key_matrix.shape[1] // hd
        group = heads // F
        kv_split = kv_heads == F
        assert heads % F == 0 and (kv_split or (kv_heads == C and heads == F))
        halos = -(-(DOC_MAX - 1) // R)
        K = (halos + 1) * R
        qc = group * hd
        dr = w_query.shape[0]
        FS = w_down.shape[0] // 2
        swap = lambda x: hop(x, "fsdp", 1)
        by_core = lambda a, b: jnp.where(core == 0, a, b)

        where = jnp.stack([core, zb])

        def chip_rows(mine, theirs):
            got = swap(theirs)
            return by_core(jnp.concatenate([mine, got]), jnp.concatenate([got, mine]))

        mine, theirs = select_qkv(core, attn_gain[None], w_query, key_matrix, value_matrix, C, qc, hd, kv_split)
        qkv_piece = by_chip_copies(chip_rows(mine, theirs))
        qkv = exchange(qkv_piece)
        pad = 16
        seg_rows = jnp.zeros((pad, D), bf16).at[0, :R].set((segments[0] + 1).astype(bf16))
        cur = jnp.concatenate([tokens[0], seg_rows])

        gu_piece = chip_rows(*select_units(where, ffn_gain[None], after(w_gate, qkv_piece), w_up, C))
        gu_copies = by_chip_copies(gu_piece)
        d_w = after(w_down, gu_piece)
        d_piece = jnp.where(zb == 0, d_w[:FS], d_w[FS:])
        cur = after(cur, qkv_piece)
        window = [shift(cur, i) for i in range(halos, 0, -1)] + [cur]
        half = hd // 2
        freq = 1.0 / ROPE_BASE ** (jnp.arange(half, dtype=f32) * 2.0 / hd)
        angle = after(jnp.arange(K, dtype=f32), qkv_piece)[:, None] * freq[None, :]
        cosine, sine = jnp.cos(angle), jnp.sin(angle)
        window = jnp.stack(window)
        window = jnp.stack([window, swap(window)])
        seg = window[:, :, R, :R].reshape(2, K).astype(jnp.int32)
        toks = window[:, :, :R].reshape(2, K, D)
        tables = (
            jnp.concatenate([cosine, cosine], axis=1),
            jnp.concatenate([-sine, sine], axis=1),
            seg[:, K - R :, None],
            seg[:, None, :],
            query_gain.astype(f32)[None],
            key_gain.astype(f32)[None],
        )
        normed, scale_attn = row_norm(after(toks, gu_copies, tables[0], tables[1], d_piece).astype(f32))

        qkv, normed = lax.optimization_barrier((qkv, normed))
        o_parts = spread(after(w_out, qkv))

        wq, wkv = qkv[:, : C * qc], qkv[:, C * qc :]
        normed_own = normed[:, K - R :].reshape(2 * R, D)
        normed_all = normed.reshape(2 * K, D)
        kv_raw = mm(normed_all, wkv, 1, 0)
        q_raw = mm(normed_own, wq, 1, 0)
        w_gu = exchange(after(gu_copies, q_raw))
        d_parts = spread(after(d_piece, q_raw))
        context = attend(q_raw, after(kv_raw, q_raw), tables, 2, R, K, group, hd)
        context = after(context, w_gu)
        cot = after(cotangent[0], context)
        cot_z = hop(cot, "ctx", 1)
        us = [cot, swap(cot), cot_z, swap(cot_z)]
        w_o = by_chip([after(p, context) for p in o_parts], c)
        part = mm(context, w_o, 1, 0)
        middle = toks[0, K - R :].astype(f32) + part[:R] + swap(part[R:].astype(bf16)).astype(f32)

        nf, scale_ffn = row_norm(middle)
        nf_z = hop(nf, "ctx", 1)
        xs = [nf, swap(nf)]
        hidden, gug, ng_own, out_own = feed(xs, us[:2], w_gu, d_parts, c, 0, 4)
        xs += [nf_z, swap(after(nf_z, ng_own))]
        hidden, gug, ng_z, out_z = feed(xs[2:], us[2:], w_gu, d_parts, c, 2, 4, (hidden, gug))
        x4, u4 = jnp.concatenate(xs), jnp.concatenate(us)

        ng_send = (ng_z[:R].astype(f32) + swap(ng_z[R:]).astype(f32)).astype(bf16)
        ng_got = hop(ng_send, "ctx", 1)
        ng_here = ng_own[:R].astype(f32) + swap(ng_own[R:]).astype(f32)

        gu_grads = scatter(mm(after(x4, ng_send), gug, 0, 0).astype(bf16))
        down_full = mm(after(hidden, ng_send), u4, 0, 0).astype(bf16)

        normed_grad = ng_here + after(ng_got, down_full).astype(f32)
        ffn_gain_term = jnp.sum(normed_grad * middle * scale_ffn, axis=0)
        middle_grad = cotangent[0].astype(f32) + row_norm_back(middle, scale_ffn, normed_grad)

        ml = middle_grad.astype(bf16)
        ml2 = jnp.concatenate([ml, swap(ml)])
        out_send = (out_z[:R].astype(f32) + swap(after(out_z[R:], ml)).astype(f32)).astype(bf16)
        out_here = out_own[:R].astype(f32) + swap(out_own[R:]).astype(f32)
        out_got = hop(out_send, "ctx", 1)
        context_grad = mm(ml2, w_o, 1, 1).astype(bf16)
        out_full = mm(context, after(ml2, context_grad), 0, 0).astype(bf16)
        down_out = jnp.concatenate([down_full.reshape(C, -1, D), out_full.reshape(C, -1, D)], axis=1).reshape(-1, D)
        do_grads = scatter_hops(down_out, c)

        def core_rows(rows):
            top, bottom = rows[:dr], rows[dr:]
            mine, theirs = by_core(top, bottom), by_core(bottom, top)
            return mine, swap(theirs.astype(bf16)).astype(f32)

        def by_parity(mine, other):
            return by_core(mine, other), by_core(other, mine)

        cg = after(context_grad, out_send, down_out)
        dq, dkv, qgg, kgg = attend_back(q_raw, kv_raw, cg, tables, 2, R, K, group, hd)
        gu_grads = after(gu_grads, dq)
        mine, got = core_rows(total(gu_grads))
        gu_s = jnp.concatenate([mine, got]).astype(bf16)
        gu_z = z_sum(gu_s, z_bits[1:])

        q_full = mm(normed_own, after(dq, gu_s), 0, 0).astype(bf16)
        kv_full = mm(normed_all, after(dkv, gu_s), 0, 0).astype(bf16)
        qkv_grads = scatter(jnp.concatenate([q_full, kv_full], axis=1))

        do_sum = total(do_grads, q_full, kv_full, gu_z)
        zpick = lambda x: (jnp.where(zb == 0, x[0], x[1]), jnp.where(zb == 0, x[1], x[0]))
        mine, theirs = zpick(do_sum[FS:].reshape(2, -1, D))
        mine = mine + hop(theirs.astype(bf16), "ctx", 1).astype(f32)
        do_s = jnp.concatenate([do_sum[:FS], mine]).astype(bf16)
        do_z = z_sum(do_s, z_bits[1:])
        do_o = hop(do_z, "ctx", 1)
        o = hop(gu_z, "ctx", 1)

        sent = (qkv_grads, do_s)
        own_rows = mm(after(dq, *sent), wq, 1, 1)
        attn_grad = mm(after(dkv, *sent), wkv, 1, 1).reshape(2, K, D)
        attn_grad = attn_grad + jnp.pad(own_rows.reshape(2, R, D), ((0, 0), (K - R, 0), (0, 0)))
        attn_grad = attn_grad[0] + swap(attn_grad[1].astype(bf16)).astype(f32)
        attn_gain_term = jnp.sum(attn_grad * toks[0].astype(f32) * scale_attn[0], axis=0)
        carry = attn_grad[:R]
        for i in range(1, halos + 1):
            carry = after(carry, o)
            carry = attn_grad[i * R : (i + 1) * R] + shift(carry.astype(bf16), -1).astype(f32)
        input_grad = middle_grad + row_norm_back(
            toks[0, K - R :].astype(f32), scale_attn[0, K - R :], carry
        )

        small = jnp.concatenate([qgg[0], kgg[0], ffn_gain_term, attn_gain_term])
        small = small.reshape(-1, 128)
        small = small + swap(small)
        small = functools.reduce(lambda a, b: a + b, [small] + [hop(small, "fsdp", 2 * rel) for rel in range(1, C)])
        small = small.reshape(-1)
        own = lambda base: lax.dynamic_slice_in_dim(small, base + me * dr, dr)
        gains = jnp.concatenate([own(2 * hd), own(2 * hd + D), small[: 2 * hd]]).reshape(-1, 128)
        for bit in z_bits:
            gains = gains + hop(gains, "ctx", bit)
        gains = gains.reshape(-1)

        attn_rows = attn_gain.astype(f32)[:, None]
        d_gate, d_up = place_units(where, ffn_gain[None], gu_z, o, C)
        output = (middle + out_here + after(out_got, dq).astype(f32)).astype(bf16)

        mine, got = core_rows(total(qkv_grads))
        nq = C * qc
        rows = [mine[:, :nq], got[:, :nq]]
        if kv_split:
            rows += [mine[:, nq:], got[:, nq:]]
        full = z_sum_split(jnp.concatenate(rows), zb).astype(f32)
        rows = [full[i * dr : (i + 1) * dr] * attn_rows for i in range(len(rows))]
        pair = by_parity(*rows[:2])
        d_query = jnp.concatenate([p[:, i * qc : (i + 1) * qc] for i in range(C) for p in pair], axis=1)
        if kv_split:
            kv = by_parity(*rows[2:])
        else:
            kv = (z_sum_split(mine[:, nq:] + got[:, nq:], zb).astype(f32) * attn_rows,)
        pick = lambda off: jnp.concatenate(
            [p[:, 2 * i * hd + off : 2 * i * hd + off + hd] for i in range(C) for p in kv], axis=1
        )
        d_key, d_value = pick(0), pick(hd)

        both = [jnp.where(zb == 0, do_z, do_o), jnp.where(zb == 0, do_o, do_z)]
        d_down = jnp.concatenate([b[:FS] for b in both]).astype(f32)
        d_out = jnp.concatenate([b[FS:] for b in both]).astype(f32)
        d_ffn_gain = gains[:dr] / ffn_gain.astype(f32)
        d_attn_gain = gains[dr : 2 * dr] / attn_gain.astype(f32)
        head_gains = gains[2 * dr : 2 * dr + 2 * hd]
        return (
            output[None],
            input_grad[None],
            d_attn_gain,
            d_query,
            d_key,
            d_value,
            d_out,
            head_gains[:hd],
            head_gains[hd:],
            d_ffn_gain,
            d_gate,
            d_up,
            d_down,
        )

    return body


def solution(mesh):
    row = P("fsdp", None)
    token = P("fsdp", "ctx", None)
    in_specs = (token, P("fsdp", "ctx"), token, P("fsdp"), row, row, row, row, P(), P(), P("fsdp"), row, row, row)
    out_specs = (token, token, P("fsdp"), row, row, row, row, P(), P(), P("fsdp"), row, row, row)
    return jax.shard_map(build(mesh), mesh=mesh, in_specs=in_specs, out_specs=out_specs, check_vma=False)
```

time: 516 us -> 480 us (0.930)
  waiting for transfers between devices: 193 us -> 213 us
  local copies, waits for them, and re-layouts: 62.2 us -> 43.1 us
  other arithmetic: 70.3 us -> 53.6 us
  starting transfers between devices: 73.4 us -> 60.6 us
  matrix products: 47.5 us -> 36 us
  Pallas kernels: 58.2 us -> 64 us
    ppermute x66 -> x43, starting transfers between devices: 63 us -> 29 us  [hop(): return lax.ppermute(x, axis, [(i, i ^ bit) for i in range(sizes[axis])])]
    all_to_all x0 -> x4, waiting for transfers between devices: none -> 27.8 us  [the longest x2 27.8 us: exchange(): out = lax.all_to_all(copies, 'fsdp', 0, 0, axis_index_groups=groups)]
    ppermute x66 -> x43, waiting for transfers between devices: 187 us -> 162 us  [hop(): return lax.ppermute(x, axis, [(i, i ^ bit) for i in range(sizes[axis])])]
    all_to_all x0 -> x4, starting transfers between devices: none -> 19.8 us  [the longest x2 10.1 us: exchange(): out = lax.all_to_all(copies, 'fsdp', 0, 0, axis_index_groups=groups)]
    ppermute x4, waiting for transfers between devices: 6.58 us -> 23.2 us  [shift(): lax.ppermute(x, 'ctx', [(i, i + by) for i in range(Z) if 0 <= i + by < Z])]
    convert_element_type x17 -> x9, other arithmetic: 21.9 us -> 9.03 us  [the longest x2 3.27 us: row_norm(): return ((values * scale).astype(bf16), scale)]
    dot_general x11, matrix products: 47.5 us -> 36 us  [mm(): lax.dot_general(a, b, (((ca,), (cb,)), ((), ())), preferred_element_type=...]
    dynamic_update_slice x17 -> x4, local copies, waits for them, and re-layouts: 14.2 us -> 3.37 us  [place(): lax.dynamic_update_slice(buf, part, ((c ^ rel) * (buf.shape[0] // C), 0))]
  transfers between devices with their start and end apart: 70 -> 51, of which waited for: 24 -> 27; matrix products, arithmetic and copies ran while one was open for 31% -> 19% of each run, Pallas kernels for 8% -> 11%
where the time goes in v2:
time: 480 us; the launch traced here: 473 us
  waiting for transfers between devices  213 us (44%)
  Pallas kernels  64 us (13%)
  starting transfers between devices  60.6 us (13%)
  other arithmetic  53.6 us (11%)
  local copies, waits for them, and re-layouts  43.1 us (9%)
  matrix products  36 us (8%)
    ppermute x43, waiting for transfers between devices, hop(): return lax.ppermute(x, axis, [(i, i ^ bit) for i in range(sizes[axis])])  162 us
    dot_general x11, matrix products, mm(): lax.dot_general(a, b, (((ca,), (cb,)), ((), ())), preferred_element_type=...  36 us
    ppermute x43, starting transfers between devices, hop(): return lax.ppermute(x, axis, [(i, i ^ bit) for i in range(sizes[axis])])  29 us
    all_to_all x2, waiting for transfers between devices, exchange(): out = lax.all_to_all(copies, 'fsdp', 0, 0, axis_index_groups=groups)  27.8 us
    pallas_call x1, Pallas kernels, attend_back(): pl.pallas_call(functools.partial(attend_back_kernel, group, keys - rows),...  24.8 us
    ppermute x4, waiting for transfers between devices, shift(): lax.ppermute(x, 'ctx', [(i, i + by) for i in range(Z) if 0 <= i + by < Z])  23.2 us
    pallas_call x2, Pallas kernels, feed(): pl.pallas_call(body, grid_spec=pltpu.PrefetchScalarGridSpec(num_scalar_pr...  19.7 us
    unnamed x128, local copies, waits for them, and re-layouts  16.5 us
  transfers between devices with their start and end apart: 51, of which 27 were waited for; matrix products, arithmetic and copies ran while one was open for 19% of the time, Pallas kernels for 11%

profile of v2, /device:TPU:0, one launch (start us, length us, event | category | flops | bytes accessed | tf_op | source)
XLA Modules:
  0.0 472.7 jit_solution(18246368361553406772)
XLA Ops:
  7.3 2.5 broadcast_in_dim.55
  9.8 4.6 collective-permute-start.2
  14.4 4.5 collective-permute-start.1
  18.9 4.9 %all-to-all-start = ((bf16[4,256,2048]{2,1,0:T(8,128)(2,1)}), bf16[4,256,2048]{2,1,0:T(8,128)(2,1)}, u32[]{:S(2)}, u32[]{:S(2)}) async-start(bf16[4,256,2048]{2,1,0:T(8,128)(2,1)} %broadcast_in_dim.55), calls=%async_computation | async-start | bytes 8388608 | tf_op jit(solution)/shard_map/all_to_all | solution.py:386
  23.8 3.6 collective-permute-done.2
  27.4 11.4 %collective-permute-done.1 = bf16[272,1024]{1,0:T(8,128)(2,1)S(1)} collective-permute-done((bf16[272,1024]{1,0:T(8,128)(2,1)S(1)}, bf16[272,1024]{1,0:T(8,128)(2,1)S(1)}, u32[]{:S(2)}, u32[]{:S(2)}) %collective-permute-start.1) | collective-permute-done | bytes 557088 | tf_op jit(solution)/shard_map/ppermute | solution.py:367
  50.5 2.4 fusion.1
  52.8 18.7 %all-to-all-done = bf16[4,256,2048]{2,1,0:T(8,128)(2,1)} async-done(((bf16[4,256,2048]{2,1,0:T(8,128)(2,1)}), bf16[4,256,2048]{2,1,0:T(8,128)(2,1)}, u32[]{:S(2)}, u32[]{:S(2)}) %all-to-all-start) | async-done | bytes 4194336 | tf_op jit(solution)/shard_map/all_to_all | solution.py:386
  73.8 2.9 fusion.20.q_ref
  76.7 5.2 %all-to-all-start.1 = ((bf16[4,256,1536]{2,1,0:T(8,128)(2,1)}), bf16[4,256,1536]{2,1,0:T(8,128)(2,1)}, u32[]{:S(2)}, u32[]{:S(2)}) async-start(bf16[4,256,1536]{2,1,0:T(8,128)(2,1)} %broadcast_in_dim.57), calls=%async_computation.1 | async-start | bytes 6291456 | tf_op jit(solution)/shard_map/all_to_all | solution.py:386
  86.5 6.0 %fusion.16.kv_ref = f32[1536,1024]{1,0:T(8,128)S(1)} fusion(bf16[1536,1024]{1,0:T(8,128)(2,1)} %bitcast.133, bf16[1024,2048]{1,0:T(8,128)(2,1)} %bitcast.10), kind=kOutput, calls=%fused_computation.34 | convolution fusion | flops 3221225472 | bytes 11534336 | tf_op jit(solution)/shard_map/dot_general | solution.py:22
  92.6 14.1 %attend.1 = bf16[512,1024]{1,0:T(8,128)(2,1)S(1)} custom-call(f32[512,1024]{1,0:T(8,128)S(1)} %fusion.20.q_ref, f32[1536,1024]{1,0:T(8,128)S(1)} %fusion.16.kv_ref, f32[768,128]{1,0:T(8,128)S(1)} %get-tuple-element.201.cos_ref, f32[768,128]{1,0:T(8,128)S(1)} %get-tuple-element.202.sin_ref, s32[2,256,1]{2,1,0:T(8,128)S(1)} %copy.31.segc_ref, ...), custom_call_target="tpu_custom_call" | custom-call | flops 1342177280 | bytes 9437184 | tf_op jit(solution)/shard_map/attend/pallas_call | solution.py:153
  106.7 2.6 copy-done
  110.3 9.1 %all-to-all-done.1 = bf16[4,256,1536]{2,1,0:T(8,128)(2,1)} async-done(((bf16[4,256,1536]{2,1,0:T(8,128)(2,1)}), bf16[4,256,1536]{2,1,0:T(8,128)(2,1)}, u32[]{:S(2)}, u32[]{:S(2)}) %all-to-all-start.1) | async-done | bytes 3145760 | tf_op jit(solution)/shard_map/all_to_all | solution.py:386
  119.4 11.2 %collective-permute-done.5 = bf16[256,1024]{1,0:T(8,128)(2,1)} collective-permute-done((bf16[256,1024]{1,0:T(8,128)(2,1)}, bf16[256,1024]{1,0:T(8,128)(2,1)}, u32[]{:S(2)}, u32[]{:S(2)}) %collective-permute-start.5) | collective-permute-done | bytes 524320 | tf_op jit(solution)/shard_map/ppermute | solution.py:364
  130.7 10.3 %collective-permute-done.7 = bf16[256,1024]{1,0:T(8,128)(2,1)} collective-permute-done((bf16[256,1024]{1,0:T(8,128)(2,1)}, bf16[256,1024]{1,0:T(8,128)(2,1)}, u32[]{:S(2)}, u32[]{:S(2)}) %collective-permute-start.7) | collective-permute-done | bytes 524320 | tf_op jit(solution)/shard_map/ppermute | solution.py:364
  152.0 5.7 %collective-permute-done.11.refs_7_ = bf16[192,1024]{1,0:T(8,128)(2,1)S(1)} collective-permute-done((bf16[192,1024]{1,0:T(8,128)(2,1)S(1)}, bf16[192,1024]{1,0:T(8,128)(2,1)S(1)}, u32[]{:S(2)}, u32[]{:S(2)}) %collective-permute-start.11) | collective-permute-done | bytes 393248 | tf_op jit(solution)/shard_map/ppermute | solution.py:364
  158.2 13.0 %collective-permute-done.12.refs_8_ = bf16[192,1024]{1,0:T(8,128)(2,1)S(1)} collective-permute-done((bf16[192,1024]{1,0:T(8,128)(2,1)S(1)}, bf16[192,1024]{1,0:T(8,128)(2,1)S(1)}, u32[]{:S(2)}, u32[]{:S(2)}) %collective-permute-start.12) | collective-permute-done | bytes 393248 | tf_op jit(solution)/shard_map/ppermute | solution.py:364
  173.2 9.9 %feed.2 = (bf16[1024,768]{1,0:T(8,128)(2,1)}, bf16[1024,1536]{1,0:T(8,128)(2,1)}, bf16[512,1024]{1,0:T(8,128)(2,1)}, bf16[512,1024]{1,0:T(8,128)(2,1)}) custom-call(s32[1]{0:T(128)} %bitcast.20.refs_0_, bf16[256,1024]{1,0:T(8,128)(2,1)} %multiply_convert_fusion.refs_1_, bf16[256,1024]{1,0:T(8,128)(2,1)} %collective-permute-done.9.refs_2_, ...), custom_call_target="tpu_custom_call" | custom-call | flops 5637144576 | bytes 11272192 | tf_op jit(solution)/shard_map/feed/pallas_call | solution.py:323
  187.2 9.9 %feed.3 = (bf16[1024,768]{1,0:T(8,128)(2,1)}, bf16[1024,1536]{1,0:T(8,128)(2,1)}, bf16[512,1024]{1,0:T(8,128)(2,1)}, bf16[512,1024]{1,0:T(8,128)(2,1)}) custom-call(s32[1]{0:T(128)} %bitcast.20.refs_0_, bf16[256,1024]{1,0:T(8,128)(2,1)} %collective-permute-done.15.refs_1_, ...), custom_call_target="tpu_custom_call", output_to_operand_aliasing={{0}: (10, {}), {1}: (11, {})} | custom-call | flops 5637144576 | bytes 11272192 | tf_op jit(solution)/shard_map/feed/pallas_call | solution.py:323
  204.5 5.0 %convolution_convert_fusion = bf16[1024,1536]{1,0:T(8,128)(2,1)} fusion(bf16[1024,1024]{1,0:T(8,128)(2,1)S(1)} %pad_maximum_fusion.2, bf16[1024,1536]{1,0:T(8,128)(2,1)S(1)} %copy-done.52), kind=kOutput, calls=%fused_computation.9 | convolution fusion | flops 3222798336 | bytes 8388608 | tf_op jit(solution)/shard_map/dot_general | solution.py:22
  209.4 4.9 %all-to-all-start.2 = ((bf16[4,256,1536]{2,1,0:T(8,128)(2,1)}), bf16[4,256,1536]{2,1,0:T(8,128)(2,1)}, u32[]{:S(2)}, u32[]{:S(2)}) async-start(bf16[4,256,1536]{2,1,0:T(8,128)(2,1)} %bitcast.135), calls=%async_computation.2 | async-start | bytes 6291456 | tf_op jit(solution)/shard_map/all_to_all | solution.py:393
  214.4 4.0 fusion.22
  220.6 2.7 fusion.51
  231.1 24.8 %attend_back.1 = (bf16[512,1024]{1,0:T(8,128)(2,1)S(1)}, bf16[1536,1024]{1,0:T(8,128)(2,1)S(1)}, f32[1,128]{1,0:T(1,128)S(1)}, f32[1,128]{1,0:T(1,128)S(1)}) custom-call(f32[512,1024]{1,0:T(8,128)S(1)} %fusion.20.q_ref, f32[1536,1024]{1,0:T(8,128)S(1)} %bitcast.114, bf16[512,1024]{1,0:T(8,128)(2,1)S(1)} %convolution_convert_fusion.4.dc_ref, ...), custom_call_target="tpu_custom_call" | custom-call | flops 3355443200 | bytes 13631488 | tf_op jit(solution)/shard_map/attend_back/pallas_call | solution.py:172
  261.2 3.7 constant_dynamic-slice_fusion.3
  264.9 2.9 collective-permute-start.29
  269.4 4.0 convolution_convert_fusion.1
  277.5 4.8 %all-to-all-start.3 = ((bf16[4,256,2048]{1,2,0:T(8,128)(2,1)}), bf16[4,256,2048]{1,2,0:T(8,128)(2,1)}, u32[]{:S(2)}, u32[]{:S(2)}) async-start(bf16[4,256,2048]{1,2,0:T(8,128)(2,1)} %bitcast.129), calls=%async_computation.3 | async-start | bytes 8388608 | tf_op jit(solution)/shard_map/all_to_all | solution.py:393
  282.3 24.3 %collective-permute-done.26 = bf16[256,1536]{1,0:T(8,128)(2,1)} collective-permute-done((bf16[256,1536]{1,0:T(8,128)(2,1)}, bf16[256,1536]{1,0:T(8,128)(2,1)}, u32[]{:S(2)}, u32[]{:S(2)}) %collective-permute-start.26) | collective-permute-done | bytes 786464 | tf_op jit(solution)/shard_map/ppermute | solution.py:364
  309.6 2.4 convert_add_fusion
  313.3 6.4 %collective-permute-done.30 = bf16[128,1024]{1,0:T(8,128)(2,1)S(1)} collective-permute-done((bf16[128,1024]{1,0:T(8,128)(2,1)S(1)}, bf16[128,1024]{1,0:T(8,128)(2,1)S(1)}, u32[]{:S(2)}, u32[]{:S(2)}) %collective-permute-start.30) | collective-permute-done | bytes 262176 | tf_op jit(solution)/shard_map/ppermute | solution.py:364
  322.8 27.4 %collective-permute-done.45 = bf16[320,1024]{1,0:T(8,128)(2,1)S(1)} collective-permute-done((bf16[320,1024]{1,0:T(8,128)(2,1)S(1)}, bf16[320,1024]{1,0:T(8,128)(2,1)S(1)}, u32[]{:S(2)}, u32[]{:S(2)}) %collective-permute-start.45) | collective-permute-done | bytes 655392 | tf_op jit(solution)/shard_map/ppermute | solution.py:364
  351.2 2.7 slice.377
  354.4 2.8 fusion.35
  357.2 8.8 %collective-permute-done.32.b_ref = bf16[256,1536]{1,0:T(8,128)(2,1)S(1)} collective-permute-done((bf16[256,1536]{1,0:T(8,128)(2,1)S(1)}, bf16[256,1536]{1,0:T(8,128)(2,1)S(1)}, u32[]{:S(2)}, u32[]{:S(2)}) %collective-permute-start.32) | collective-permute-done | bytes 786464 | tf_op jit(solution)/shard_map/ppermute | solution.py:364
  365.9 3.1 place_units.1
  369.1 10.6 %collective-permute-done.46 = bf16[320,1024]{1,0:T(8,128)(2,1)} collective-permute-done((bf16[320,1024]{1,0:T(8,128)(2,1)S(1)}, bf16[320,1024]{1,0:T(8,128)(2,1)}, u32[]{:S(2)}, u32[]{:S(2)}) %collective-permute-start.46) | collective-permute-done | bytes 655392 | tf_op jit(solution)/shard_map/ppermute | solution.py:364
  382.7 6.1 %fusion.14 = f32[1536,1024]{1,0:T(8,128)S(1)} fusion(bf16[1536,1024]{1,0:T(8,128)(2,1)} %copy-done.12, bf16[1024,2048]{1,0:T(8,128)(2,1)} %bitcast.10), kind=kOutput, calls=%fused_computation.32 | convolution fusion | flops 3221225472 | bytes 11534336 | tf_op jit(solution)/shard_map/dot_general | solution.py:22
  388.8 2.9 fusion.18
  393.6 3.0 convert_reduce_fusion
  406.7 6.6 %collective-permute-done.42 = bf16[256,1024]{0,1:T(8,128)(2,1)S(1)} collective-permute-done((bf16[256,1024]{0,1:T(8,128)(2,1)S(1)}, bf16[256,1024]{0,1:T(8,128)(2,1)S(1)}, u32[]{:S(2)}, u32[]{:S(2)}) %collective-permute-start.42) | collective-permute-done | bytes 524320 | tf_op jit(solution)/shard_map/ppermute | solution.py:364
  420.2 6.9 %collective-permute-done.39 = f32[4,128]{1,0:T(4,128)S(1)} collective-permute-done((f32[4,128]{1,0:T(4,128)S(1)}, f32[4,128]{1,0:T(4,128)S(1)}, u32[]{:S(2)}, u32[]{:S(2)}) %collective-permute-start.39) | collective-permute-done | bytes 2080 | tf_op jit(solution)/shard_map/ppermute | solution.py:364
  427.1 3.4 collective-permute-start.40
  430.5 9.6 %collective-permute-done.43 = bf16[256,1024]{0,1:T(8,128)(2,1)S(1)} collective-permute-done((bf16[256,1024]{0,1:T(8,128)(2,1)S(1)}, bf16[256,1024]{0,1:T(8,128)(2,1)S(1)}, u32[]{:S(2)}, u32[]{:S(2)}) %collective-permute-start.43) | collective-permute-done | bytes 524320 | tf_op jit(solution)/shard_map/ppermute | solution.py:364
  440.3 10.3 %collective-permute-done.40 = f32[4,128]{1,0:T(4,128)S(1)} collective-permute-done((f32[4,128]{1,0:T(4,128)S(1)}, f32[4,128]{1,0:T(4,128)S(1)}, u32[]{:S(2)}, u32[]{:S(2)}) %collective-permute-start.40) | collective-permute-done | bytes 2080 | tf_op jit(solution)/shard_map/ppermute | solution.py:364
  459.5 8.2 %collective-permute-done.34 = bf16[256,1024]{1,0:T(8,128)(2,1)} collective-permute-done((bf16[256,1024]{1,0:T(8,128)(2,1)}, bf16[256,1024]{1,0:T(8,128)(2,1)}, u32[]{:S(2)}, u32[]{:S(2)}) %collective-permute-start.34) | collective-permute-done | bytes 524320 | tf_op jit(solution)/shard_map/ppermute | solution.py:367
  469.5 2.8 fusion.31
  (300 shorter events, 112.9 us)
Async XLA Ops:
  4.7 2.3 collective-permute-start
  9.8 17.6 %collective-permute-start.2 = (bf16[272,1024]{1,0:T(8,128)(2,1)S(1)}, bf16[272,1024]{1,0:T(8,128)(2,1)S(1)}, u32[]{:S(2)}, u32[]{:S(2)}) collective-permute-start(bf16[272,1024]{1,0:T(8,128)(2,1)S(1)} %fusion.34), channel_id=1, source_target_pairs={{0,1},{1,2},{2,3},{4,5},{5,6},{6,7},{8,9},{9,10},{10,11},{12,13},{... | collective-permute-start | bytes 1671176 | tf_op jit(solution)/shard_map/ppermute | solution.py:367
  14.4 24.4 %collective-permute-start.1 = (bf16[272,1024]{1,0:T(8,128)(2,1)S(1)}, bf16[272,1024]{1,0:T(8,128)(2,1)S(1)}, u32[]{:S(2)}, u32[]{:S(2)}) collective-permute-start(bf16[272,1024]{1,0:T(8,128)(2,1)S(1)} %fusion.34), channel_id=1, source_target_pairs={{0,2},{1,3},{4,6},{5,7},{8,10},{9,11},{12,14},{13,15},{16,18},{17,... | collective-permute-start | bytes 1671176 | tf_op jit(solution)/shard_map/ppermute | solution.py:367
  18.9 52.6 %all-to-all-start = ((bf16[4,256,2048]{2,1,0:T(8,128)(2,1)}), bf16[4,256,2048]{2,1,0:T(8,128)(2,1)}, u32[]{:S(2)}, u32[]{:S(2)}) async-start(bf16[4,256,2048]{2,1,0:T(8,128)(2,1)} %broadcast_in_dim.55), calls=%async_computation | async-start | bytes 8388608 | tf_op jit(solution)/shard_map/all_to_all | solution.py:386
  40.8 5.3 %collective-permute-start.3 = (bf16[3,272,1024]{2,1,0:T(8,128)(2,1)}, bf16[3,272,1024]{2,1,0:T(8,128)(2,1)}, u32[]{:S(2)}, u32[]{:S(2)}) collective-permute-start(bf16[3,272,1024]{2,1,0:T(8,128)(2,1)} %get-tuple-element.164), channel_id=1, source_target_pairs={{0,4},{4,0},{8,12},{12,8},{16,20},{20,16},{24,28},{28,24},{1,5},{5... | collective-permute-start | bytes 5013512 | tf_op jit(solution)/shard_map/ppermute | solution.py:364
  42.6 2.5 collective-permute-start.4
  76.7 42.7 %all-to-all-start.1 = ((bf16[4,256,1536]{2,1,0:T(8,128)(2,1)}), bf16[4,256,1536]{2,1,0:T(8,128)(2,1)}, u32[]{:S(2)}, u32[]{:S(2)}) async-start(bf16[4,256,1536]{2,1,0:T(8,128)(2,1)} %broadcast_in_dim.57), calls=%async_computation.1 | async-start | bytes 6291456 | tf_op jit(solution)/shard_map/all_to_all | solution.py:386
  82.9 47.7 %collective-permute-start.5 = (bf16[256,1024]{1,0:T(8,128)(2,1)}, bf16[256,1024]{1,0:T(8,128)(2,1)}, u32[]{:S(2)}, u32[]{:S(2)}) collective-permute-start(bf16[256,1024]{1,0:T(8,128)(2,1)} %param.23), channel_id=1, source_target_pairs={{0,8},{4,12},{8,0},{12,4},{16,24},{20,28},{24,16},{28,20},{1,9},{5... | collective-permute-start | bytes 1572872 | tf_op jit(solution)/shard_map/ppermute | solution.py:364
  85.0 45.7 %collective-permute-start.6 = (bf16[256,1024]{1,0:T(8,128)(2,1)}, bf16[256,1024]{1,0:T(8,128)(2,1)}, u32[]{:S(2)}, u32[]{:S(2)}) collective-permute-start(bf16[256,1024]{1,0:T(8,128)(2,1)} %param.23), channel_id=1, source_target_pairs={{0,16},{4,20},{8,24},{12,28},{16,0},{20,4},{24,8},{28,12},{1,17},{... | collective-permute-start | bytes 1572872 | tf_op jit(solution)/shard_map/ppermute | solution.py:364
  86.4 54.5 %collective-permute-start.7 = (bf16[256,1024]{1,0:T(8,128)(2,1)}, bf16[256,1024]{1,0:T(8,128)(2,1)}, u32[]{:S(2)}, u32[]{:S(2)}) collective-permute-start(bf16[256,1024]{1,0:T(8,128)(2,1)} %param.23), channel_id=1, source_target_pairs={{0,24},{4,28},{8,16},{12,20},{16,8},{20,12},{24,0},{28,4},{1,25},{... | collective-permute-start | bytes 1572872 | tf_op jit(solution)/shard_map/ppermute | solution.py:364
  146.2 11.5 %collective-permute-start.11 = (bf16[192,1024]{1,0:T(8,128)(2,1)S(1)}, bf16[192,1024]{1,0:T(8,128)(2,1)S(1)}, u32[]{:S(2)}, u32[]{:S(2)}) collective-permute-start(bf16[192,1024]{1,0:T(8,128)(2,1)S(1)} %copy-done.42), channel_id=1, source_target_pairs={{0,8},{4,12},{8,0},{12,4},{16,24},{20,28},{24,16},{28,20},{1,9},{5... | collective-permute-start | bytes 1179656 | tf_op jit(solution)/shard_map/ppermute | solution.py:364
  146.8 25.4 %collective-permute-start.10 = (bf16[256,1024]{1,0:T(8,128)(2,1)S(1)}, bf16[256,1024]{1,0:T(8,128)(2,1)S(1)}, u32[]{:S(2)}, u32[]{:S(2)}) collective-permute-start(bf16[256,1024]{1,0:T(8,128)(2,1)S(1)} %bitcast.146), channel_id=1, source_target_pairs={{0,4},{4,0},{8,12},{12,8},{16,20},{20,16},{24,28},{28,24},{1,5},{5... | collective-permute-start | bytes 1572872 | tf_op jit(solution)/shard_map/ppermute | solution.py:364
  147.0 25.2 %collective-permute-start.17 = (bf16[256,1024]{1,0:T(8,128)(2,1)S(1)}, bf16[256,1024]{1,0:T(8,128)(2,1)}, u32[]{:S(2)}, u32[]{:S(2)}) collective-permute-start(bf16[256,1024]{1,0:T(8,128)(2,1)S(1)} %bitcast.147), channel_id=1, source_target_pairs={{0,1},{1,0},{2,3},{3,2},{4,5},{5,4},{6,7},{7,6},{8,9},{9,8},{10,11... | collective-permute-start | bytes 1572872 | tf_op jit(solution)/shard_map/ppermute | solution.py:364
  151.3 21.8 %collective-permute-start.9 = (bf16[256,1024]{1,0:T(8,128)(2,1)}, bf16[256,1024]{1,0:T(8,128)(2,1)}, u32[]{:S(2)}, u32[]{:S(2)}) collective-permute-start(bf16[256,1024]{1,0:T(8,128)(2,1)} %multiply_convert_fusion.refs_1_), channel_id=1, source_target_pairs={{0,4},{4,0},{8,12},{12,8},{16,20},{20,16},{24,28},{28,24},{1,5},{5... | collective-permute-start | bytes 1572872 | tf_op jit(solution)/shard_map/ppermute | solution.py:364
  151.4 19.8 %collective-permute-start.12 = (bf16[192,1024]{1,0:T(8,128)(2,1)S(1)}, bf16[192,1024]{1,0:T(8,128)(2,1)S(1)}, u32[]{:S(2)}, u32[]{:S(2)}) collective-permute-start(bf16[192,1024]{1,0:T(8,128)(2,1)S(1)} %copy-done.42), channel_id=1, source_target_pairs={{0,16},{4,20},{8,24},{12,28},{16,0},{20,4},{24,8},{28,12},{1,17},{... | collective-permute-start | bytes 1179656 | tf_op jit(solution)/shard_map/ppermute | solution.py:364
  157.7 14.5 %collective-permute-start.13 = (bf16[192,1024]{1,0:T(8,128)(2,1)S(1)}, bf16[192,1024]{1,0:T(8,128)(2,1)S(1)}, u32[]{:S(2)}, u32[]{:S(2)}) collective-permute-start(bf16[192,1024]{1,0:T(8,128)(2,1)S(1)} %copy-done.42), channel_id=1, source_target_pairs={{0,24},{4,28},{8,16},{12,20},{16,8},{20,12},{24,0},{28,4},{1,25},{... | collective-permute-start | bytes 1179656 | tf_op jit(solution)/shard_map/ppermute | solution.py:364
  171.3 13.7 %collective-permute-start.15 = (bf16[256,1024]{1,0:T(8,128)(2,1)}, bf16[256,1024]{1,0:T(8,128)(2,1)}, u32[]{:S(2)}, u32[]{:S(2)}) collective-permute-start(bf16[256,1024]{1,0:T(8,128)(2,1)} %multiply_convert_fusion.refs_1_), channel_id=1, source_target_pairs={{0,1},{1,0},{2,3},{3,2},{4,5},{5,4},{6,7},{7,6},{8,9},{9,8},{10,11... | collective-permute-start | bytes 1572872 | tf_op jit(solution)/shard_map/ppermute | solution.py:364
  172.2 12.7 %collective-permute-start.18 = (bf16[256,1024]{1,0:T(8,128)(2,1)}, bf16[256,1024]{1,0:T(8,128)(2,1)}, u32[]{:S(2)}, u32[]{:S(2)}) collective-permute-start(bf16[256,1024]{1,0:T(8,128)(2,1)} %collective-permute-done.17.refs_3_), channel_id=1, source_target_pairs={{0,4},{4,0},{8,12},{12,8},{16,20},{20,16},{24,28},{28,24},{1,5},{5... | collective-permute-start | bytes 1572872 | tf_op jit(solution)/shard_map/ppermute | solution.py:364
  184.9 2.3 collective-permute-start.16
  198.1 4.3 collective-permute-start.20
  200.2 18.2 %collective-permute-start.19 = (bf16[256,1024]{1,0:T(8,128)(2,1)}, bf16[256,1024]{1,0:T(8,128)(2,1)}, u32[]{:S(2)}, u32[]{:S(2)}) collective-permute-start(bf16[256,1024]{1,0:T(8,128)(2,1)} %slice.296), channel_id=1, source_target_pairs={{0,4},{4,0},{8,12},{12,8},{16,20},{20,16},{24,28},{28,24},{1,5},{5... | collective-permute-start | bytes 1572872 | tf_op jit(solution)/shard_map/ppermute | solution.py:364
  203.5 14.9 %collective-permute-start.21 = (bf16[256,1024]{1,0:T(8,128)(2,1)}, bf16[256,1024]{1,0:T(8,128)(2,1)}, u32[]{:S(2)}, u32[]{:S(2)}) collective-permute-start(bf16[256,1024]{1,0:T(8,128)(2,1)} %add_convert_fusion.6), channel_id=1, source_target_pairs={{0,1},{1,0},{2,3},{3,2},{4,5},{5,4},{6,7},{7,6},{8,9},{9,8},{10,11... | collective-permute-start | bytes 1572872 | tf_op jit(solution)/shard_map/ppermute | solution.py:364
  209.4 49.1 %all-to-all-start.2 = ((bf16[4,256,1536]{2,1,0:T(8,128)(2,1)}), bf16[4,256,1536]{2,1,0:T(8,128)(2,1)}, u32[]{:S(2)}, u32[]{:S(2)}) async-start(bf16[4,256,1536]{2,1,0:T(8,128)(2,1)} %bitcast.135), calls=%async_computation.2 | async-start | bytes 6291456 | tf_op jit(solution)/shard_map/all_to_all | solution.py:393
  223.3 6.8 %collective-permute-start.22 = (bf16[256,1024]{1,0:T(8,128)(2,1)S(1)}, bf16[256,1024]{1,0:T(8,128)(2,1)S(1)}, u32[]{:S(2)}, u32[]{:S(2)}) collective-permute-start(bf16[256,1024]{1,0:T(8,128)(2,1)S(1)} %slice.294), channel_id=1, source_target_pairs={{0,4},{4,0},{8,12},{12,8},{16,20},{20,16},{24,28},{28,24},{1,5},{5... | collective-permute-start | bytes 1572872 | tf_op jit(solution)/shard_map/ppermute | solution.py:364
  260.9 7.4 %collective-permute-start.25 = (bf16[128,1536]{1,0:T(8,128)(2,1)S(1)}, bf16[128,1536]{1,0:T(8,128)(2,1)S(1)}, u32[]{:S(2)}, u32[]{:S(2)}) collective-permute-start(bf16[128,1536]{1,0:T(8,128)(2,1)S(1)} %get-tuple-element.171), channel_id=1, source_target_pairs={{0,4},{4,0},{8,12},{12,8},{16,20},{20,16},{24,28},{28,24},{1,5},{5... | collective-permute-start | bytes 1179656 | tf_op jit(solution)/shard_map/ppermute | solution.py:364
  264.9 43.1 %collective-permute-start.29 = (bf16[448,1024]{1,0:T(8,128)(2,1)}, bf16[448,1024]{1,0:T(8,128)(2,1)}, u32[]{:S(2)}, u32[]{:S(2)}) collective-permute-start(bf16[448,1024]{1,0:T(8,128)(2,1)} %get-tuple-element.157), channel_id=1, source_target_pairs={{0,24},{4,28},{8,16},{12,20},{16,8},{20,12},{24,0},{28,4},{1,25},{... | collective-permute-start | bytes 2752520 | tf_op jit(solution)/shard_map/ppermute | solution.py:364
  267.8 41.3 %collective-permute-start.28 = (bf16[448,1024]{1,0:T(8,128)(2,1)}, bf16[448,1024]{1,0:T(8,128)(2,1)}, u32[]{:S(2)}, u32[]{:S(2)}) collective-permute-start(bf16[448,1024]{1,0:T(8,128)(2,1)} %get-tuple-element.158), channel_id=1, source_target_pairs={{0,16},{4,20},{8,24},{12,28},{16,0},{20,4},{24,8},{28,12},{1,17},{... | collective-permute-start | bytes 2752520 | tf_op jit(solution)/shard_map/ppermute | solution.py:364
  268.4 41.2 %collective-permute-start.27 = (bf16[448,1024]{1,0:T(8,128)(2,1)}, bf16[448,1024]{1,0:T(8,128)(2,1)}, u32[]{:S(2)}, u32[]{:S(2)}) collective-permute-start(bf16[448,1024]{1,0:T(8,128)(2,1)} %get-tuple-element.159), channel_id=1, source_target_pairs={{0,8},{4,12},{8,0},{12,4},{16,24},{20,28},{24,16},{28,20},{1,9},{5... | collective-permute-start | bytes 2752520 | tf_op jit(solution)/shard_map/ppermute | solution.py:364
  269.3 37.3 %collective-permute-start.26 = (bf16[256,1536]{1,0:T(8,128)(2,1)}, bf16[256,1536]{1,0:T(8,128)(2,1)}, u32[]{:S(2)}, u32[]{:S(2)}) collective-permute-start(bf16[256,1536]{1,0:T(8,128)(2,1)} %pad_maximum_fusion.7), channel_id=1, source_target_pairs={{0,2},{1,3},{2,0},{3,1},{4,6},{5,7},{6,4},{7,5},{8,10},{9,11},{10,... | collective-permute-start | bytes 2359304 | tf_op jit(solution)/shard_map/ppermute | solution.py:364
  277.5 105.2 %all-to-all-start.3 = ((bf16[4,256,2048]{1,2,0:T(8,128)(2,1)}), bf16[4,256,2048]{1,2,0:T(8,128)(2,1)}, u32[]{:S(2)}, u32[]{:S(2)}) async-start(bf16[4,256,2048]{1,2,0:T(8,128)(2,1)} %bitcast.129), calls=%async_computation.3 | async-start | bytes 8388608 | tf_op jit(solution)/shard_map/all_to_all | solution.py:393
  312.1 7.6 %collective-permute-start.30 = (bf16[128,1024]{1,0:T(8,128)(2,1)S(1)}, bf16[128,1024]{1,0:T(8,128)(2,1)S(1)}, u32[]{:S(2)}, u32[]{:S(2)}) collective-permute-start(bf16[128,1024]{1,0:T(8,128)(2,1)S(1)} %select_convert_fusion.4), channel_id=1, source_target_pairs={{0,1},{1,0},{2,3},{3,2},{4,5},{5,4},{6,7},{7,6},{8,9},{9,8},{10,11... | collective-permute-start | bytes 786440 | tf_op jit(solution)/shard_map/ppermute | solution.py:364
  319.9 30.3 %collective-permute-start.45 = (bf16[320,1024]{1,0:T(8,128)(2,1)S(1)}, bf16[320,1024]{1,0:T(8,128)(2,1)S(1)}, u32[]{:S(2)}, u32[]{:S(2)}) collective-permute-start(bf16[320,1024]{1,0:T(8,128)(2,1)S(1)} %pad_maximum_fusion.8), channel_id=1, source_target_pairs={{0,2},{1,3},{2,0},{3,1},{4,6},{5,7},{6,4},{7,5},{8,10},{9,11},{10,... | collective-permute-start | bytes 1966088 | tf_op jit(solution)/shard_map/ppermute | solution.py:364
  320.8 33.6 %collective-permute-start.14 = (bf16[256,1024]{1,0:T(8,128)(2,1)}, bf16[256,1024]{1,0:T(8,128)(2,1)}, u32[]{:S(2)}, u32[]{:S(2)}) collective-permute-start(bf16[256,1024]{1,0:T(8,128)(2,1)} %slice.292), channel_id=1, source_target_pairs={{0,4},{4,0},{8,12},{12,8},{16,20},{20,16},{24,28},{28,24},{1,5},{5... | collective-permute-start | bytes 1572872 | tf_op jit(solution)/shard_map/ppermute | solution.py:364
  320.8 33.6 %collective-permute-start.23 = (bf16[256,1024]{1,0:T(8,128)(2,1)S(1)}, bf16[256,1024]{1,0:T(8,128)(2,1)}, u32[]{:S(2)}, u32[]{:S(2)}) collective-permute-start(bf16[256,1024]{1,0:T(8,128)(2,1)S(1)} %copy-done.40), channel_id=1, source_target_pairs={{0,1},{1,0},{2,3},{3,2},{4,5},{5,4},{6,7},{7,6},{8,9},{9,8},{10,11... | collective-permute-start | bytes 1572872 | tf_op jit(solution)/shard_map/ppermute | solution.py:364
  321.8 44.1 %collective-permute-start.32 = (bf16[256,1536]{1,0:T(8,128)(2,1)S(1)}, bf16[256,1536]{1,0:T(8,128)(2,1)S(1)}, u32[]{:S(2)}, u32[]{:S(2)}) collective-permute-start(bf16[256,1536]{1,0:T(8,128)(2,1)S(1)} %add_convert_fusion.a_ref), channel_id=1, source_target_pairs={{0,1},{1,0},{2,3},{3,2},{4,5},{5,4},{6,7},{7,6},{8,9},{9,8},{10,11... | collective-permute-start | bytes 2359304 | tf_op jit(solution)/shard_map/ppermute | solution.py:364
  350.5 29.2 %collective-permute-start.46 = (bf16[320,1024]{1,0:T(8,128)(2,1)S(1)}, bf16[320,1024]{1,0:T(8,128)(2,1)}, u32[]{:S(2)}, u32[]{:S(2)}) collective-permute-start(bf16[320,1024]{1,0:T(8,128)(2,1)S(1)} %add_convert_fusion.1), channel_id=1, source_target_pairs={{0,1},{1,0},{2,3},{3,2},{4,5},{5,4},{6,7},{7,6},{8,9},{9,8},{10,11... | collective-permute-start | bytes 1966088 | tf_op jit(solution)/shard_map/ppermute | solution.py:364
  393.6 5.6 %collective-permute-start.31 = (bf16[768,1024]{1,0:T(8,128)(2,1)S(1)}, bf16[768,1024]{1,0:T(8,128)(2,1)S(1)}, u32[]{:S(2)}, u32[]{:S(2)}) collective-permute-start(bf16[768,1024]{1,0:T(8,128)(2,1)S(1)} %fusion.25), channel_id=1, source_target_pairs={{0,4},{4,0},{8,12},{12,8},{16,20},{20,16},{24,28},{28,24},{1,5},{5... | collective-permute-start | bytes 4718600 | tf_op jit(solution)/shard_map/ppermute | solution.py:364
  399.1 14.3 %collective-permute-start.42 = (bf16[256,1024]{0,1:T(8,128)(2,1)S(1)}, bf16[256,1024]{0,1:T(8,128)(2,1)S(1)}, u32[]{:S(2)}, u32[]{:S(2)}) collective-permute-start(bf16[256,1024]{0,1:T(8,128)(2,1)S(1)} %select_convert_fusion), channel_id=1, source_target_pairs={{0,1},{1,0},{2,3},{3,2},{4,5},{5,4},{6,7},{7,6},{8,9},{9,8},{10,11... | collective-permute-start | bytes 1572872 | tf_op jit(solution)/shard_map/ppermute | solution.py:364
  400.0 3.1 collective-permute-start.35
  403.2 12.7 %collective-permute-start.38 = (f32[18,128]{1,0:T(8,128)S(1)}, f32[18,128]{1,0:T(8,128)S(1)}, u32[]{:S(2)}, u32[]{:S(2)}) collective-permute-start(f32[18,128]{1,0:T(8,128)S(1)} %fusion.47), channel_id=1, source_target_pairs={{0,24},{4,28},{8,16},{12,20},{16,8},{20,12},{24,0},{28,4},{1,25},{... | collective-permute-start | bytes 27656 | tf_op jit(solution)/shard_map/ppermute | solution.py:364
  405.0 10.9 %collective-permute-start.37 = (f32[18,128]{1,0:T(8,128)S(1)}, f32[18,128]{1,0:T(8,128)S(1)}, u32[]{:S(2)}, u32[]{:S(2)}) collective-permute-start(f32[18,128]{1,0:T(8,128)S(1)} %fusion.47), channel_id=1, source_target_pairs={{0,16},{4,20},{8,24},{12,28},{16,0},{20,4},{24,8},{28,12},{1,17},{... | collective-permute-start | bytes 27656 | tf_op jit(solution)/shard_map/ppermute | solution.py:364
  406.2 9.6 %collective-permute-start.36 = (f32[18,128]{1,0:T(8,128)S(1)}, f32[18,128]{1,0:T(8,128)S(1)}, u32[]{:S(2)}, u32[]{:S(2)}) collective-permute-start(f32[18,128]{1,0:T(8,128)S(1)} %fusion.47), channel_id=1, source_target_pairs={{0,8},{4,12},{8,0},{12,4},{16,24},{20,28},{24,16},{28,20},{1,9},{5... | collective-permute-start | bytes 27656 | tf_op jit(solution)/shard_map/ppermute | solution.py:364
  413.6 26.5 %collective-permute-start.43 = (bf16[256,1024]{0,1:T(8,128)(2,1)S(1)}, bf16[256,1024]{0,1:T(8,128)(2,1)S(1)}, u32[]{:S(2)}, u32[]{:S(2)}) collective-permute-start(bf16[256,1024]{0,1:T(8,128)(2,1)S(1)} %add_convert_fusion.3), channel_id=1, source_target_pairs={{0,2},{1,3},{2,0},{3,1},{4,6},{5,7},{6,4},{7,5},{8,10},{9,11},{10,... | collective-permute-start | bytes 1572872 | tf_op jit(solution)/shard_map/ppermute | solution.py:364
  416.0 11.1 %collective-permute-start.39 = (f32[4,128]{1,0:T(4,128)S(1)}, f32[4,128]{1,0:T(4,128)S(1)}, u32[]{:S(2)}, u32[]{:S(2)}) collective-permute-start(f32[4,128]{1,0:T(4,128)S(1)} %maximum_bitcast_fusion.1), channel_id=1, source_target_pairs={{0,1},{1,0},{2,3},{3,2},{4,5},{5,4},{6,7},{7,6},{8,9},{9,8},{10,11... | collective-permute-start | bytes 6152 | tf_op jit(solution)/shard_map/ppermute | solution.py:364
  418.9 32.7 %collective-permute-start.33 = (bf16[256,1024]{1,0:T(8,128)(2,1)S(1)}, bf16[256,1024]{1,0:T(8,128)(2,1)S(1)}, u32[]{:S(2)}, u32[]{:S(2)}) collective-permute-start(bf16[256,1024]{1,0:T(8,128)(2,1)S(1)} %slice.376), channel_id=1, source_target_pairs={{1,0},{2,1},{3,2},{5,4},{6,5},{7,6},{9,8},{10,9},{11,10},{13,12},{... | collective-permute-start | bytes 1572872 | tf_op jit(solution)/shard_map/ppermute | solution.py:367
  427.1 23.5 %collective-permute-start.40 = (f32[4,128]{1,0:T(4,128)S(1)}, f32[4,128]{1,0:T(4,128)S(1)}, u32[]{:S(2)}, u32[]{:S(2)}) collective-permute-start(f32[4,128]{1,0:T(4,128)S(1)} %fusion.46), channel_id=1, source_target_pairs={{0,2},{1,3},{2,0},{3,1},{4,6},{5,7},{6,4},{7,5},{8,10},{9,11},{10,... | collective-permute-start | bytes 6152 | tf_op jit(solution)/shard_map/ppermute | solution.py:364
  440.2 15.1 %collective-permute-start.44 = (bf16[256,1024]{0,1:T(8,128)(2,1)S(1)}, bf16[256,1024]{0,1:T(8,128)(2,1)S(1)}, u32[]{:S(2)}, u32[]{:S(2)}) collective-permute-start(bf16[256,1024]{0,1:T(8,128)(2,1)S(1)} %add_convert_fusion.2), channel_id=1, source_target_pairs={{0,1},{1,0},{2,3},{3,2},{4,5},{5,4},{6,7},{7,6},{8,9},{9,8},{10,11... | collective-permute-start | bytes 1572872 | tf_op jit(solution)/shard_map/ppermute | solution.py:364
  452.6 15.0 %collective-permute-start.34 = (bf16[256,1024]{1,0:T(8,128)(2,1)}, bf16[256,1024]{1,0:T(8,128)(2,1)}, u32[]{:S(2)}, u32[]{:S(2)}) collective-permute-start(bf16[256,1024]{1,0:T(8,128)(2,1)} %slice_add_fusion), channel_id=1, source_target_pairs={{1,0},{2,1},{3,2},{5,4},{6,5},{7,6},{9,8},{10,9},{11,10},{13,12},{... | collective-permute-start | bytes 1572872 | tf_op jit(solution)/shard_map/ppermute | solution.py:367
  (58 other events, 299.1 us)

commit v3 on v2

--- a/solution.py
+++ b/solution.py
@@ -550,15 +550,14 @@
         do_o = hop(do_z, "ctx", 1)
         o = hop(gu_z, "ctx", 1)
 
-        sent = (qkv_grads, do_s)
+        sent = (do_s,)
         own_rows = mm(after(dq, *sent), wq, 1, 1)
         attn_grad = mm(after(dkv, *sent), wkv, 1, 1).reshape(2, K, D)
         attn_grad = attn_grad + jnp.pad(own_rows.reshape(2, R, D), ((0, 0), (K - R, 0), (0, 0)))
-        attn_grad = attn_grad[0] + swap(attn_grad[1].astype(bf16)).astype(f32)
+        attn_grad = attn_grad[0] + swap(after(attn_grad[1].astype(bf16), qkv_grads)).astype(f32)
         attn_gain_term = jnp.sum(attn_grad * toks[0].astype(f32) * scale_attn[0], axis=0)
         carry = attn_grad[:R]
         for i in range(1, halos + 1):
-            carry = after(carry, o)
             carry = attn_grad[i * R : (i + 1) * R] + shift(carry.astype(bf16), -1).astype(f32)
         input_grad = middle_grad + row_norm_back(
             toks[0, K - R :].astype(f32), scale_attn[0, K - R :], carry

time: 480 us -> 459 us (0.956)
  waiting for transfers between devices: 213 us -> 177 us
  local copies, waits for them, and re-layouts: 43.1 us -> 55 us
    ppermute x43, waiting for transfers between devices: 162 us -> 136 us  [hop(): return lax.ppermute(x, axis, [(i, i ^ bit) for i in range(sizes[axis])])]
    unnamed x128 -> x146, local copies, waits for them, and re-layouts: 16.5 us -> 26.2 us
    ppermute x4, waiting for transfers between devices: 23.2 us -> 15 us  [shift(): lax.ppermute(x, 'ctx', [(i, i + by) for i in range(Z) if 0 <= i + by < Z])]
  transfers between devices with their start and end apart: 51 -> 51, of which waited for: 27 -> 25; matrix products, arithmetic and copies ran while one was open for 19% -> 25% of each run, Pallas kernels for 11% -> 12%
where the time goes in v3:
time: 459 us; the launch traced here: 452 us
  waiting for transfers between devices  177 us (39%)
  Pallas kernels  63.9 us (14%)
  starting transfers between devices  63.1 us (14%)
  local copies, waits for them, and re-layouts  55 us (12%)
  other arithmetic  54.6 us (12%)
  matrix products  36.3 us (8%)
    ppermute x43, waiting for transfers between devices, hop(): return lax.ppermute(x, axis, [(i, i ^ bit) for i in range(sizes[axis])])  136 us
    dot_general x11, matrix products, mm(): lax.dot_general(a, b, (((ca,), (cb,)), ((), ())), preferred_element_type=...  36.3 us
    ppermute x43, starting transfers between devices, hop(): return lax.ppermute(x, axis, [(i, i ^ bit) for i in range(sizes[axis])])  31.7 us
    unnamed x146, local copies, waits for them, and re-layouts  26.2 us
    all_to_all x2, waiting for transfers between devices, exchange(): out = lax.all_to_all(copies, 'fsdp', 0, 0, axis_index_groups=groups)  26 us
    pallas_call x1, Pallas kernels, attend_back(): pl.pallas_call(functools.partial(attend_back_kernel, group, keys - rows),...  24.8 us
    pallas_call x2, Pallas kernels, feed(): pl.pallas_call(body, grid_spec=pltpu.PrefetchScalarGridSpec(num_scalar_pr...  19.7 us
    ppermute x4, waiting for transfers between devices, shift(): lax.ppermute(x, 'ctx', [(i, i + by) for i in range(Z) if 0 <= i + by < Z])  15 us
  transfers between devices with their start and end apart: 51, of which 25 were waited for; matrix products, arithmetic and copies ran while one was open for 25% of the time, Pallas kernels for 12%

profile of v3, /device:TPU:0, one launch (start us, length us, event | category | flops | bytes accessed | tf_op | source)
XLA Modules:
  0.0 451.6 jit_solution(2899778124306090395)
XLA Ops:
  7.3 2.5 broadcast_in_dim.55
  9.8 4.6 %collective-permute-start.2 = (bf16[272,1024]{1,0:T(8,128)(2,1)S(1)}, bf16[272,1024]{1,0:T(8,128)(2,1)S(1)}, u32[]{:S(2)}, u32[]{:S(2)}) collective-permute-start(bf16[272,1024]{1,0:T(8,128)(2,1)S(1)} %fusion.35), channel_id=1, source_target_pairs={{0,1},{1,2},{2,3},{4,5},{5,6},{6,7},{8,9},{9,10},{10,11},{12,13},{... | collective-permute-start | bytes 1671176 | tf_op jit(solution)/shard_map/ppermute | solution.py:367
  14.4 4.5 collective-permute-start.1
  18.9 4.9 %all-to-all-start = ((bf16[4,256,2048]{2,1,0:T(8,128)(2,1)}), bf16[4,256,2048]{2,1,0:T(8,128)(2,1)}, u32[]{:S(2)}, u32[]{:S(2)}) async-start(bf16[4,256,2048]{2,1,0:T(8,128)(2,1)} %broadcast_in_dim.55), calls=%async_computation | async-start | bytes 8388608 | tf_op jit(solution)/shard_map/all_to_all | solution.py:386
  23.8 3.6 collective-permute-done.2
  27.4 11.4 %collective-permute-done.1 = bf16[272,1024]{1,0:T(8,128)(2,1)S(1)} collective-permute-done((bf16[272,1024]{1,0:T(8,128)(2,1)S(1)}, bf16[272,1024]{1,0:T(8,128)(2,1)S(1)}, u32[]{:S(2)}, u32[]{:S(2)}) %collective-permute-start.1) | collective-permute-done | bytes 557088 | tf_op jit(solution)/shard_map/ppermute | solution.py:367
  39.6 3.1 pad_maximum_fusion.3
  54.7 16.8 %all-to-all-done = bf16[4,256,2048]{2,1,0:T(8,128)(2,1)} async-done(((bf16[4,256,2048]{2,1,0:T(8,128)(2,1)}), bf16[4,256,2048]{2,1,0:T(8,128)(2,1)}, u32[]{:S(2)}, u32[]{:S(2)}) %all-to-all-start) | async-done | bytes 4194336 | tf_op jit(solution)/shard_map/all_to_all | solution.py:386
  73.8 2.9 fusion.20.q_ref
  76.6 4.9 %all-to-all-start.1 = ((bf16[4,256,1536]{2,1,0:T(8,128)(2,1)}), bf16[4,256,1536]{2,1,0:T(8,128)(2,1)}, u32[]{:S(2)}, u32[]{:S(2)}) async-start(bf16[4,256,1536]{2,1,0:T(8,128)(2,1)} %broadcast_in_dim.57), calls=%async_computation.1 | async-start | bytes 6291456 | tf_op jit(solution)/shard_map/all_to_all | solution.py:386
  86.2 6.0 %fusion.16.kv_ref = f32[1536,1024]{1,0:T(8,128)S(1)} fusion(bf16[1536,1024]{1,0:T(8,128)(2,1)} %bitcast.135, bf16[1024,2048]{1,0:T(8,128)(2,1)} %bitcast.10), kind=kOutput, calls=%fused_computation.34 | convolution fusion | flops 3221225472 | bytes 11534336 | tf_op jit(solution)/shard_map/dot_general | solution.py:22
  92.2 14.1 %attend.1 = bf16[512,1024]{1,0:T(8,128)(2,1)S(1)} custom-call(f32[512,1024]{1,0:T(8,128)S(1)} %fusion.20.q_ref, f32[1536,1024]{1,0:T(8,128)S(1)} %fusion.16.kv_ref, f32[768,128]{1,0:T(8,128)S(1)} %get-tuple-element.199.cos_ref, f32[768,128]{1,0:T(8,128)S(1)} %get-tuple-element.200.sin_ref, s32[2,256,1]{2,1,0:T(8,128)S(1)} %copy.31.segc_ref, ...), custom_call_target="tpu_custom_call" | custom-call | flops 1342177280 | bytes 9437184 | tf_op jit(solution)/shard_map/attend/pallas_call | solution.py:153
  106.2 2.6 copy-done
  109.8 9.2 %all-to-all-done.1 = bf16[4,256,1536]{2,1,0:T(8,128)(2,1)} async-done(((bf16[4,256,1536]{2,1,0:T(8,128)(2,1)}), bf16[4,256,1536]{2,1,0:T(8,128)(2,1)}, u32[]{:S(2)}, u32[]{:S(2)}) %all-to-all-start.1) | async-done | bytes 3145760 | tf_op jit(solution)/shard_map/all_to_all | solution.py:386
  119.1 11.2 %collective-permute-done.5 = bf16[256,1024]{1,0:T(8,128)(2,1)} collective-permute-done((bf16[256,1024]{1,0:T(8,128)(2,1)}, bf16[256,1024]{1,0:T(8,128)(2,1)}, u32[]{:S(2)}, u32[]{:S(2)}) %collective-permute-start.5) | collective-permute-done | bytes 524320 | tf_op jit(solution)/shard_map/ppermute | solution.py:364
  130.3 10.3 %collective-permute-done.7 = bf16[256,1024]{1,0:T(8,128)(2,1)} collective-permute-done((bf16[256,1024]{1,0:T(8,128)(2,1)}, bf16[256,1024]{1,0:T(8,128)(2,1)}, u32[]{:S(2)}, u32[]{:S(2)}) %collective-permute-start.7) | collective-permute-done | bytes 524320 | tf_op jit(solution)/shard_map/ppermute | solution.py:364
  151.6 5.7 %collective-permute-done.11.refs_7_ = bf16[192,1024]{1,0:T(8,128)(2,1)S(1)} collective-permute-done((bf16[192,1024]{1,0:T(8,128)(2,1)S(1)}, bf16[192,1024]{1,0:T(8,128)(2,1)S(1)}, u32[]{:S(2)}, u32[]{:S(2)}) %collective-permute-start.11) | collective-permute-done | bytes 393248 | tf_op jit(solution)/shard_map/ppermute | solution.py:364
  157.9 13.0 %collective-permute-done.12.refs_8_ = bf16[192,1024]{1,0:T(8,128)(2,1)S(1)} collective-permute-done((bf16[192,1024]{1,0:T(8,128)(2,1)S(1)}, bf16[192,1024]{1,0:T(8,128)(2,1)S(1)}, u32[]{:S(2)}, u32[]{:S(2)}) %collective-permute-start.12) | collective-permute-done | bytes 393248 | tf_op jit(solution)/shard_map/ppermute | solution.py:364
  172.9 9.9 %feed.2 = (bf16[1024,768]{1,0:T(8,128)(2,1)}, bf16[1024,1536]{1,0:T(8,128)(2,1)}, bf16[512,1024]{1,0:T(8,128)(2,1)}, bf16[512,1024]{1,0:T(8,128)(2,1)}) custom-call(s32[1]{0:T(128)} %bitcast.20.refs_0_, bf16[256,1024]{1,0:T(8,128)(2,1)} %multiply_convert_fusion.refs_1_, bf16[256,1024]{1,0:T(8,128)(2,1)} %collective-permute-done.9.refs_2_, ...), custom_call_target="tpu_custom_call" | custom-call | flops 5637144576 | bytes 11272192 | tf_op jit(solution)/shard_map/feed/pallas_call | solution.py:323
  186.8 9.9 %feed.3 = (bf16[1024,768]{1,0:T(8,128)(2,1)}, bf16[1024,1536]{1,0:T(8,128)(2,1)}, bf16[512,1024]{1,0:T(8,128)(2,1)}, bf16[512,1024]{1,0:T(8,128)(2,1)}) custom-call(s32[1]{0:T(128)} %bitcast.20.refs_0_, bf16[256,1024]{1,0:T(8,128)(2,1)} %collective-permute-done.15.refs_1_, ...), custom_call_target="tpu_custom_call", output_to_operand_aliasing={{0}: (10, {}), {1}: (11, {})} | custom-call | flops 5637144576 | bytes 11272192 | tf_op jit(solution)/shard_map/feed/pallas_call | solution.py:323
  205.0 5.0 %convolution_convert_fusion = bf16[1024,1536]{1,0:T(8,128)(2,1)} fusion(bf16[1024,1024]{1,0:T(8,128)(2,1)S(1)} %pad_maximum_fusion.2, bf16[1024,1536]{1,0:T(8,128)(2,1)S(1)} %copy-done.59), kind=kOutput, calls=%fused_computation.9 | convolution fusion | flops 3222798336 | bytes 8388608 | tf_op jit(solution)/shard_map/dot_general | solution.py:22
  210.0 5.0 %all-to-all-start.2 = ((bf16[4,256,1536]{2,1,0:T(8,128)(2,1)}), bf16[4,256,1536]{2,1,0:T(8,128)(2,1)}, u32[]{:S(2)}, u32[]{:S(2)}) async-start(bf16[4,256,1536]{2,1,0:T(8,128)(2,1)} %bitcast.137), calls=%async_computation.2 | async-start | bytes 6291456 | tf_op jit(solution)/shard_map/all_to_all | solution.py:393
  215.0 4.0 fusion.22
  220.7 2.7 fusion.52
  232.3 24.8 %attend_back.1 = (bf16[512,1024]{1,0:T(8,128)(2,1)S(1)}, bf16[1536,1024]{1,0:T(8,128)(2,1)S(1)}, f32[1,128]{1,0:T(1,128)S(1)}, f32[1,128]{1,0:T(1,128)S(1)}) custom-call(f32[512,1024]{1,0:T(8,128)S(1)} %fusion.20.q_ref, f32[1536,1024]{1,0:T(8,128)S(1)} %bitcast.114, bf16[512,1024]{1,0:T(8,128)(2,1)S(1)} %convolution_convert_fusion.4.dc_ref, ...), custom_call_target="tpu_custom_call" | custom-call | flops 3355443200 | bytes 13631488 | tf_op jit(solution)/shard_map/attend_back/pallas_call | solution.py:172
  259.8 2.5 convert_reduce_fusion.1
  269.2 2.9 collective-permute-start.29
  274.7 3.9 convolution_convert_fusion.1
  282.7 4.8 %all-to-all-start.3 = ((bf16[4,256,2048]{1,2,0:T(8,128)(2,1)}), bf16[4,256,2048]{1,2,0:T(8,128)(2,1)}, u32[]{:S(2)}, u32[]{:S(2)}) async-start(bf16[4,256,2048]{1,2,0:T(8,128)(2,1)} %bitcast.131), calls=%async_computation.3 | async-start | bytes 8388608 | tf_op jit(solution)/shard_map/all_to_all | solution.py:393
  287.6 24.1 %collective-permute-done.26 = bf16[256,1536]{1,0:T(8,128)(2,1)} collective-permute-done((bf16[256,1536]{1,0:T(8,128)(2,1)}, bf16[256,1536]{1,0:T(8,128)(2,1)}, u32[]{:S(2)}, u32[]{:S(2)}) %collective-permute-start.26) | collective-permute-done | bytes 786464 | tf_op jit(solution)/shard_map/ppermute | solution.py:364
  313.9 2.6 convert_add_fusion
  317.6 2.3 fusion.36
  321.1 4.7 %collective-permute-done.30 = bf16[128,1024]{1,0:T(8,128)(2,1)S(1)} collective-permute-done((bf16[128,1024]{1,0:T(8,128)(2,1)S(1)}, bf16[128,1024]{1,0:T(8,128)(2,1)S(1)}, u32[]{:S(2)}, u32[]{:S(2)}) %collective-permute-start.30) | collective-permute-done | bytes 262176 | tf_op jit(solution)/shard_map/ppermute | solution.py:364
  326.1 4.2 fusion.18
  330.3 5.1 %fusion.14 = f32[1536,1024]{1,0:T(8,128)S(1)} fusion(bf16[1536,1024]{1,0:T(8,128)(2,1)S(1)} %copy-done.13, bf16[1024,2048]{1,0:T(8,128)(2,1)} %bitcast.10), kind=kOutput, calls=%fused_computation.32 | convolution fusion | flops 3221225472 | bytes 11534336 | tf_op jit(solution)/shard_map/dot_general | solution.py:22
  335.4 18.1 %collective-permute-done.44 = bf16[320,1024]{1,0:T(8,128)(2,1)S(1)} collective-permute-done((bf16[320,1024]{1,0:T(8,128)(2,1)S(1)}, bf16[320,1024]{1,0:T(8,128)(2,1)S(1)}, u32[]{:S(2)}, u32[]{:S(2)}) %collective-permute-start.44) | collective-permute-done | bytes 655392 | tf_op jit(solution)/shard_map/ppermute | solution.py:364
  355.4 3.0 pad_add_fusion
  360.0 3.1 place_units.1
  363.1 6.0 %collective-permute-done.45 = bf16[320,1024]{1,0:T(8,128)(2,1)S(1)} collective-permute-done((bf16[320,1024]{1,0:T(8,128)(2,1)S(1)}, bf16[320,1024]{1,0:T(8,128)(2,1)S(1)}, u32[]{:S(2)}, u32[]{:S(2)}) %collective-permute-start.45) | collective-permute-done | bytes 655392 | tf_op jit(solution)/shard_map/ppermute | solution.py:364
  371.0 3.1 convert_reduce_fusion
  386.2 4.6 %collective-permute-done.41 = bf16[256,1024]{0,1:T(8,128)(2,1)S(1)} collective-permute-done((bf16[256,1024]{0,1:T(8,128)(2,1)S(1)}, bf16[256,1024]{0,1:T(8,128)(2,1)S(1)}, u32[]{:S(2)}, u32[]{:S(2)}) %collective-permute-start.41) | collective-permute-done | bytes 524320 | tf_op jit(solution)/shard_map/ppermute | solution.py:364
  391.0 3.3 collective-permute-start.42
  397.2 8.0 %collective-permute-done.38 = f32[4,128]{1,0:T(4,128)S(1)} collective-permute-done((f32[4,128]{1,0:T(4,128)S(1)}, f32[4,128]{1,0:T(4,128)S(1)}, u32[]{:S(2)}, u32[]{:S(2)}) %collective-permute-start.38) | collective-permute-done | bytes 2080 | tf_op jit(solution)/shard_map/ppermute | solution.py:364
  405.3 3.0 collective-permute-start.39
  408.3 9.3 %collective-permute-done.42 = bf16[256,1024]{0,1:T(8,128)(2,1)S(1)} collective-permute-done((bf16[256,1024]{0,1:T(8,128)(2,1)S(1)}, bf16[256,1024]{0,1:T(8,128)(2,1)S(1)}, u32[]{:S(2)}, u32[]{:S(2)}) %collective-permute-start.42) | collective-permute-done | bytes 524320 | tf_op jit(solution)/shard_map/ppermute | solution.py:364
  417.8 10.8 %collective-permute-done.39 = f32[4,128]{1,0:T(4,128)S(1)} collective-permute-done((f32[4,128]{1,0:T(4,128)S(1)}, f32[4,128]{1,0:T(4,128)S(1)}, u32[]{:S(2)}, u32[]{:S(2)}) %collective-permute-start.39) | collective-permute-done | bytes 2080 | tf_op jit(solution)/shard_map/ppermute | solution.py:364
  437.6 2.5 copy.35
  448.8 2.5 fusion.31
  (319 shorter events, 122.4 us)
Async XLA Ops:
  4.7 2.3 collective-permute-start
  9.8 17.6 %collective-permute-start.2 = (bf16[272,1024]{1,0:T(8,128)(2,1)S(1)}, bf16[272,1024]{1,0:T(8,128)(2,1)S(1)}, u32[]{:S(2)}, u32[]{:S(2)}) collective-permute-start(bf16[272,1024]{1,0:T(8,128)(2,1)S(1)} %fusion.35), channel_id=1, source_target_pairs={{0,1},{1,2},{2,3},{4,5},{5,6},{6,7},{8,9},{9,10},{10,11},{12,13},{... | collective-permute-start | bytes 1671176 | tf_op jit(solution)/shard_map/ppermute | solution.py:367
  14.4 24.4 %collective-permute-start.1 = (bf16[272,1024]{1,0:T(8,128)(2,1)S(1)}, bf16[272,1024]{1,0:T(8,128)(2,1)S(1)}, u32[]{:S(2)}, u32[]{:S(2)}) collective-permute-start(bf16[272,1024]{1,0:T(8,128)(2,1)S(1)} %fusion.35), channel_id=1, source_target_pairs={{0,2},{1,3},{4,6},{5,7},{8,10},{9,11},{12,14},{13,15},{16,18},{17,... | collective-permute-start | bytes 1671176 | tf_op jit(solution)/shard_map/ppermute | solution.py:367
  18.9 52.6 %all-to-all-start = ((bf16[4,256,2048]{2,1,0:T(8,128)(2,1)}), bf16[4,256,2048]{2,1,0:T(8,128)(2,1)}, u32[]{:S(2)}, u32[]{:S(2)}) async-start(bf16[4,256,2048]{2,1,0:T(8,128)(2,1)} %broadcast_in_dim.55), calls=%async_computation | async-start | bytes 8388608 | tf_op jit(solution)/shard_map/all_to_all | solution.py:386
  42.7 5.3 %collective-permute-start.3 = (bf16[3,272,1024]{2,1,0:T(8,128)(2,1)}, bf16[3,272,1024]{2,1,0:T(8,128)(2,1)}, u32[]{:S(2)}, u32[]{:S(2)}) collective-permute-start(bf16[3,272,1024]{2,1,0:T(8,128)(2,1)} %get-tuple-element.162), channel_id=1, source_target_pairs={{0,4},{4,0},{8,12},{12,8},{16,20},{20,16},{24,28},{28,24},{1,5},{5... | collective-permute-start | bytes 5013512 | tf_op jit(solution)/shard_map/ppermute | solution.py:364
  44.5 2.5 collective-permute-start.4
  76.6 42.4 %all-to-all-start.1 = ((bf16[4,256,1536]{2,1,0:T(8,128)(2,1)}), bf16[4,256,1536]{2,1,0:T(8,128)(2,1)}, u32[]{:S(2)}, u32[]{:S(2)}) async-start(bf16[4,256,1536]{2,1,0:T(8,128)(2,1)} %broadcast_in_dim.57), calls=%async_computation.1 | async-start | bytes 6291456 | tf_op jit(solution)/shard_map/all_to_all | solution.py:386
  82.6 47.7 %collective-permute-start.5 = (bf16[256,1024]{1,0:T(8,128)(2,1)}, bf16[256,1024]{1,0:T(8,128)(2,1)}, u32[]{:S(2)}, u32[]{:S(2)}) collective-permute-start(bf16[256,1024]{1,0:T(8,128)(2,1)} %param.23), channel_id=1, source_target_pairs={{0,8},{4,12},{8,0},{12,4},{16,24},{20,28},{24,16},{28,20},{1,9},{5... | collective-permute-start | bytes 1572872 | tf_op jit(solution)/shard_map/ppermute | solution.py:364
  84.6 45.7 %collective-permute-start.6 = (bf16[256,1024]{1,0:T(8,128)(2,1)}, bf16[256,1024]{1,0:T(8,128)(2,1)}, u32[]{:S(2)}, u32[]{:S(2)}) collective-permute-start(bf16[256,1024]{1,0:T(8,128)(2,1)} %param.23), channel_id=1, source_target_pairs={{0,16},{4,20},{8,24},{12,28},{16,0},{20,4},{24,8},{28,12},{1,17},{... | collective-permute-start | bytes 1572872 | tf_op jit(solution)/shard_map/ppermute | solution.py:364
  86.1 54.5 %collective-permute-start.7 = (bf16[256,1024]{1,0:T(8,128)(2,1)}, bf16[256,1024]{1,0:T(8,128)(2,1)}, u32[]{:S(2)}, u32[]{:S(2)}) collective-permute-start(bf16[256,1024]{1,0:T(8,128)(2,1)} %param.23), channel_id=1, source_target_pairs={{0,24},{4,28},{8,16},{12,20},{16,8},{20,12},{24,0},{28,4},{1,25},{... | collective-permute-start | bytes 1572872 | tf_op jit(solution)/shard_map/ppermute | solution.py:364
  145.8 11.5 %collective-permute-start.11 = (bf16[192,1024]{1,0:T(8,128)(2,1)S(1)}, bf16[192,1024]{1,0:T(8,128)(2,1)S(1)}, u32[]{:S(2)}, u32[]{:S(2)}) collective-permute-start(bf16[192,1024]{1,0:T(8,128)(2,1)S(1)} %copy-done.52), channel_id=1, source_target_pairs={{0,8},{4,12},{8,0},{12,4},{16,24},{20,28},{24,16},{28,20},{1,9},{5... | collective-permute-start | bytes 1179656 | tf_op jit(solution)/shard_map/ppermute | solution.py:364
  146.5 25.4 %collective-permute-start.10 = (bf16[256,1024]{1,0:T(8,128)(2,1)S(1)}, bf16[256,1024]{1,0:T(8,128)(2,1)S(1)}, u32[]{:S(2)}, u32[]{:S(2)}) collective-permute-start(bf16[256,1024]{1,0:T(8,128)(2,1)S(1)} %bitcast.148), channel_id=1, source_target_pairs={{0,4},{4,0},{8,12},{12,8},{16,20},{20,16},{24,28},{28,24},{1,5},{5... | collective-permute-start | bytes 1572872 | tf_op jit(solution)/shard_map/ppermute | solution.py:364
  146.6 25.2 %collective-permute-start.17 = (bf16[256,1024]{1,0:T(8,128)(2,1)S(1)}, bf16[256,1024]{1,0:T(8,128)(2,1)}, u32[]{:S(2)}, u32[]{:S(2)}) collective-permute-start(bf16[256,1024]{1,0:T(8,128)(2,1)S(1)} %bitcast.149), channel_id=1, source_target_pairs={{0,1},{1,0},{2,3},{3,2},{4,5},{5,4},{6,7},{7,6},{8,9},{9,8},{10,11... | collective-permute-start | bytes 1572872 | tf_op jit(solution)/shard_map/ppermute | solution.py:364
  151.0 21.8 %collective-permute-start.9 = (bf16[256,1024]{1,0:T(8,128)(2,1)}, bf16[256,1024]{1,0:T(8,128)(2,1)}, u32[]{:S(2)}, u32[]{:S(2)}) collective-permute-start(bf16[256,1024]{1,0:T(8,128)(2,1)} %multiply_convert_fusion.refs_1_), channel_id=1, source_target_pairs={{0,4},{4,0},{8,12},{12,8},{16,20},{20,16},{24,28},{28,24},{1,5},{5... | collective-permute-start | bytes 1572872 | tf_op jit(solution)/shard_map/ppermute | solution.py:364
  151.1 19.8 %collective-permute-start.12 = (bf16[192,1024]{1,0:T(8,128)(2,1)S(1)}, bf16[192,1024]{1,0:T(8,128)(2,1)S(1)}, u32[]{:S(2)}, u32[]{:S(2)}) collective-permute-start(bf16[192,1024]{1,0:T(8,128)(2,1)S(1)} %copy-done.52), channel_id=1, source_target_pairs={{0,16},{4,20},{8,24},{12,28},{16,0},{20,4},{24,8},{28,12},{1,17},{... | collective-permute-start | bytes 1179656 | tf_op jit(solution)/shard_map/ppermute | solution.py:364
  157.3 14.5 %collective-permute-start.13 = (bf16[192,1024]{1,0:T(8,128)(2,1)S(1)}, bf16[192,1024]{1,0:T(8,128)(2,1)S(1)}, u32[]{:S(2)}, u32[]{:S(2)}) collective-permute-start(bf16[192,1024]{1,0:T(8,128)(2,1)S(1)} %copy-done.52), channel_id=1, source_target_pairs={{0,24},{4,28},{8,16},{12,20},{16,8},{20,12},{24,0},{28,4},{1,25},{... | collective-permute-start | bytes 1179656 | tf_op jit(solution)/shard_map/ppermute | solution.py:364
  170.9 13.7 %collective-permute-start.15 = (bf16[256,1024]{1,0:T(8,128)(2,1)}, bf16[256,1024]{1,0:T(8,128)(2,1)}, u32[]{:S(2)}, u32[]{:S(2)}) collective-permute-start(bf16[256,1024]{1,0:T(8,128)(2,1)} %multiply_convert_fusion.refs_1_), channel_id=1, source_target_pairs={{0,1},{1,0},{2,3},{3,2},{4,5},{5,4},{6,7},{7,6},{8,9},{9,8},{10,11... | collective-permute-start | bytes 1572872 | tf_op jit(solution)/shard_map/ppermute | solution.py:364
  171.8 12.7 %collective-permute-start.18 = (bf16[256,1024]{1,0:T(8,128)(2,1)}, bf16[256,1024]{1,0:T(8,128)(2,1)}, u32[]{:S(2)}, u32[]{:S(2)}) collective-permute-start(bf16[256,1024]{1,0:T(8,128)(2,1)} %collective-permute-done.17.refs_3_), channel_id=1, source_target_pairs={{0,4},{4,0},{8,12},{12,8},{16,20},{20,16},{24,28},{28,24},{1,5},{5... | collective-permute-start | bytes 1572872 | tf_op jit(solution)/shard_map/ppermute | solution.py:364
  184.6 2.3 collective-permute-start.16
  197.9 5.2 %collective-permute-start.20 = (bf16[256,1024]{1,0:T(8,128)(2,1)S(1)}, bf16[256,1024]{1,0:T(8,128)(2,1)S(1)}, u32[]{:S(2)}, u32[]{:S(2)}) collective-permute-start(bf16[256,1024]{1,0:T(8,128)(2,1)S(1)} %slice.299), channel_id=1, source_target_pairs={{0,4},{4,0},{8,12},{12,8},{16,20},{20,16},{24,28},{28,24},{1,5},{5... | collective-permute-start | bytes 1572872 | tf_op jit(solution)/shard_map/ppermute | solution.py:364
  200.0 19.0 %collective-permute-start.19 = (bf16[256,1024]{1,0:T(8,128)(2,1)}, bf16[256,1024]{1,0:T(8,128)(2,1)}, u32[]{:S(2)}, u32[]{:S(2)}) collective-permute-start(bf16[256,1024]{1,0:T(8,128)(2,1)} %slice.297), channel_id=1, source_target_pairs={{0,4},{4,0},{8,12},{12,8},{16,20},{20,16},{24,28},{28,24},{1,5},{5... | collective-permute-start | bytes 1572872 | tf_op jit(solution)/shard_map/ppermute | solution.py:364
  204.0 15.0 %collective-permute-start.21 = (bf16[256,1024]{1,0:T(8,128)(2,1)}, bf16[256,1024]{1,0:T(8,128)(2,1)}, u32[]{:S(2)}, u32[]{:S(2)}) collective-permute-start(bf16[256,1024]{1,0:T(8,128)(2,1)} %add_convert_fusion.6), channel_id=1, source_target_pairs={{0,1},{1,0},{2,3},{3,2},{4,5},{5,4},{6,7},{7,6},{8,9},{9,8},{10,11... | collective-permute-start | bytes 1572872 | tf_op jit(solution)/shard_map/ppermute | solution.py:364
  210.0 49.8 %all-to-all-start.2 = ((bf16[4,256,1536]{2,1,0:T(8,128)(2,1)}), bf16[4,256,1536]{2,1,0:T(8,128)(2,1)}, u32[]{:S(2)}, u32[]{:S(2)}) async-start(bf16[4,256,1536]{2,1,0:T(8,128)(2,1)} %bitcast.137), calls=%async_computation.2 | async-start | bytes 6291456 | tf_op jit(solution)/shard_map/all_to_all | solution.py:393
  223.5 4.0 collective-permute-start.24
  226.4 46.3 %collective-permute-start.23 = (bf16[256,1024]{1,0:T(8,128)(2,1)}, bf16[256,1024]{1,0:T(8,128)(2,1)}, u32[]{:S(2)}, u32[]{:S(2)}) collective-permute-start(bf16[256,1024]{1,0:T(8,128)(2,1)} %add_convert_fusion.5), channel_id=1, source_target_pairs={{0,1},{1,0},{2,3},{3,2},{4,5},{5,4},{6,7},{7,6},{8,9},{9,8},{10,11... | collective-permute-start | bytes 1572872 | tf_op jit(solution)/shard_map/ppermute | solution.py:364
  263.2 9.5 %collective-permute-start.25 = (bf16[128,1536]{1,0:T(8,128)(2,1)}, bf16[128,1536]{1,0:T(8,128)(2,1)}, u32[]{:S(2)}, u32[]{:S(2)}) collective-permute-start(bf16[128,1536]{1,0:T(8,128)(2,1)} %get-tuple-element.169), channel_id=1, source_target_pairs={{0,4},{4,0},{8,12},{12,8},{16,20},{20,16},{24,28},{28,24},{1,5},{5... | collective-permute-start | bytes 1179656 | tf_op jit(solution)/shard_map/ppermute | solution.py:364
  266.8 50.8 %collective-permute-start.14 = (bf16[256,1024]{1,0:T(8,128)(2,1)}, bf16[256,1024]{1,0:T(8,128)(2,1)}, u32[]{:S(2)}, u32[]{:S(2)}) collective-permute-start(bf16[256,1024]{1,0:T(8,128)(2,1)} %slice.293), channel_id=1, source_target_pairs={{0,4},{4,0},{8,12},{12,8},{16,20},{20,16},{24,28},{28,24},{1,5},{5... | collective-permute-start | bytes 1572872 | tf_op jit(solution)/shard_map/ppermute | solution.py:364
  269.2 44.0 %collective-permute-start.29 = (bf16[448,1024]{1,0:T(8,128)(2,1)}, bf16[448,1024]{1,0:T(8,128)(2,1)}, u32[]{:S(2)}, u32[]{:S(2)}) collective-permute-start(bf16[448,1024]{1,0:T(8,128)(2,1)} %get-tuple-element.155), channel_id=1, source_target_pairs={{0,24},{4,28},{8,16},{12,20},{16,8},{20,12},{24,0},{28,4},{1,25},{... | collective-permute-start | bytes 2752520 | tf_op jit(solution)/shard_map/ppermute | solution.py:364
  272.1 41.3 %collective-permute-start.28 = (bf16[448,1024]{1,0:T(8,128)(2,1)}, bf16[448,1024]{1,0:T(8,128)(2,1)}, u32[]{:S(2)}, u32[]{:S(2)}) collective-permute-start(bf16[448,1024]{1,0:T(8,128)(2,1)} %get-tuple-element.156), channel_id=1, source_target_pairs={{0,16},{4,20},{8,24},{12,28},{16,0},{20,4},{24,8},{28,12},{1,17},{... | collective-permute-start | bytes 2752520 | tf_op jit(solution)/shard_map/ppermute | solution.py:364
  272.7 41.2 %collective-permute-start.27 = (bf16[448,1024]{1,0:T(8,128)(2,1)}, bf16[448,1024]{1,0:T(8,128)(2,1)}, u32[]{:S(2)}, u32[]{:S(2)}) collective-permute-start(bf16[448,1024]{1,0:T(8,128)(2,1)} %get-tuple-element.157), channel_id=1, source_target_pairs={{0,8},{4,12},{8,0},{12,4},{16,24},{20,28},{24,16},{28,20},{1,9},{5... | collective-permute-start | bytes 2752520 | tf_op jit(solution)/shard_map/ppermute | solution.py:364
  274.7 37.0 %collective-permute-start.26 = (bf16[256,1536]{1,0:T(8,128)(2,1)}, bf16[256,1536]{1,0:T(8,128)(2,1)}, u32[]{:S(2)}, u32[]{:S(2)}) collective-permute-start(bf16[256,1536]{1,0:T(8,128)(2,1)} %pad_maximum_fusion.7), channel_id=1, source_target_pairs={{0,2},{1,3},{2,0},{3,1},{4,6},{5,7},{6,4},{7,5},{8,10},{9,11},{10,... | collective-permute-start | bytes 2359304 | tf_op jit(solution)/shard_map/ppermute | solution.py:364
  282.7 88.2 %all-to-all-start.3 = ((bf16[4,256,2048]{1,2,0:T(8,128)(2,1)}), bf16[4,256,2048]{1,2,0:T(8,128)(2,1)}, u32[]{:S(2)}, u32[]{:S(2)}) async-start(bf16[4,256,2048]{1,2,0:T(8,128)(2,1)} %bitcast.131), calls=%async_computation.3 | async-start | bytes 8388608 | tf_op jit(solution)/shard_map/all_to_all | solution.py:393
  316.6 9.2 %collective-permute-start.30 = (bf16[128,1024]{1,0:T(8,128)(2,1)S(1)}, bf16[128,1024]{1,0:T(8,128)(2,1)S(1)}, u32[]{:S(2)}, u32[]{:S(2)}) collective-permute-start(bf16[128,1024]{1,0:T(8,128)(2,1)S(1)} %select_convert_fusion.4), channel_id=1, source_target_pairs={{0,1},{1,0},{2,3},{3,2},{4,5},{5,4},{6,7},{7,6},{8,9},{9,8},{10,11... | collective-permute-start | bytes 786440 | tf_op jit(solution)/shard_map/ppermute | solution.py:364
  320.0 40.1 %collective-permute-start.46 = (bf16[256,1536]{1,0:T(8,128)(2,1)S(1)}, bf16[256,1536]{1,0:T(8,128)(2,1)S(1)}, u32[]{:S(2)}, u32[]{:S(2)}) collective-permute-start(bf16[256,1536]{1,0:T(8,128)(2,1)S(1)} %add_convert_fusion.a_ref), channel_id=1, source_target_pairs={{0,1},{1,0},{2,3},{3,2},{4,5},{5,4},{6,7},{7,6},{8,9},{9,8},{10,11... | collective-permute-start | bytes 2359304 | tf_op jit(solution)/shard_map/ppermute | solution.py:364
  325.9 27.6 %collective-permute-start.44 = (bf16[320,1024]{1,0:T(8,128)(2,1)S(1)}, bf16[320,1024]{1,0:T(8,128)(2,1)S(1)}, u32[]{:S(2)}, u32[]{:S(2)}) collective-permute-start(bf16[320,1024]{1,0:T(8,128)(2,1)S(1)} %pad_maximum_fusion.8), channel_id=1, source_target_pairs={{0,2},{1,3},{2,0},{3,1},{4,6},{5,7},{6,4},{7,5},{8,10},{9,11},{10,... | collective-permute-start | bytes 1966088 | tf_op jit(solution)/shard_map/ppermute | solution.py:364
  353.8 15.3 %collective-permute-start.45 = (bf16[320,1024]{1,0:T(8,128)(2,1)S(1)}, bf16[320,1024]{1,0:T(8,128)(2,1)S(1)}, u32[]{:S(2)}, u32[]{:S(2)}) collective-permute-start(bf16[320,1024]{1,0:T(8,128)(2,1)S(1)} %add_convert_fusion.1), channel_id=1, source_target_pairs={{0,1},{1,0},{2,3},{3,2},{4,5},{5,4},{6,7},{7,6},{8,9},{9,8},{10,11... | collective-permute-start | bytes 1966088 | tf_op jit(solution)/shard_map/ppermute | solution.py:364
  370.9 7.1 %collective-permute-start.31 = (bf16[768,1024]{1,0:T(8,128)(2,1)}, bf16[768,1024]{1,0:T(8,128)(2,1)S(1)}, u32[]{:S(2)}, u32[]{:S(2)}) collective-permute-start(bf16[768,1024]{1,0:T(8,128)(2,1)} %fusion.25), channel_id=1, source_target_pairs={{0,4},{4,0},{8,12},{12,8},{16,20},{20,16},{24,28},{28,24},{1,5},{5... | collective-permute-start | bytes 4718600 | tf_op jit(solution)/shard_map/ppermute | solution.py:364
  376.5 14.3 %collective-permute-start.41 = (bf16[256,1024]{0,1:T(8,128)(2,1)S(1)}, bf16[256,1024]{0,1:T(8,128)(2,1)S(1)}, u32[]{:S(2)}, u32[]{:S(2)}) collective-permute-start(bf16[256,1024]{0,1:T(8,128)(2,1)S(1)} %select_convert_fusion), channel_id=1, source_target_pairs={{0,1},{1,0},{2,3},{3,2},{4,5},{5,4},{6,7},{7,6},{8,9},{9,8},{10,11... | collective-permute-start | bytes 1572872 | tf_op jit(solution)/shard_map/ppermute | solution.py:364
  378.7 3.4 collective-permute-start.34
  382.2 12.1 %collective-permute-start.37 = (f32[18,128]{1,0:T(8,128)S(1)}, f32[18,128]{1,0:T(8,128)S(1)}, u32[]{:S(2)}, u32[]{:S(2)}) collective-permute-start(f32[18,128]{1,0:T(8,128)S(1)} %fusion.48), channel_id=1, source_target_pairs={{0,24},{4,28},{8,16},{12,20},{16,8},{20,12},{24,0},{28,4},{1,25},{... | collective-permute-start | bytes 27656 | tf_op jit(solution)/shard_map/ppermute | solution.py:364
  384.5 9.9 %collective-permute-start.36 = (f32[18,128]{1,0:T(8,128)S(1)}, f32[18,128]{1,0:T(8,128)S(1)}, u32[]{:S(2)}, u32[]{:S(2)}) collective-permute-start(f32[18,128]{1,0:T(8,128)S(1)} %fusion.48), channel_id=1, source_target_pairs={{0,16},{4,20},{8,24},{12,28},{16,0},{20,4},{24,8},{28,12},{1,17},{... | collective-permute-start | bytes 27656 | tf_op jit(solution)/shard_map/ppermute | solution.py:364
  384.8 9.5 %collective-permute-start.35 = (f32[18,128]{1,0:T(8,128)S(1)}, f32[18,128]{1,0:T(8,128)S(1)}, u32[]{:S(2)}, u32[]{:S(2)}) collective-permute-start(f32[18,128]{1,0:T(8,128)S(1)} %fusion.48), channel_id=1, source_target_pairs={{0,8},{4,12},{8,0},{12,4},{16,24},{20,28},{24,16},{28,20},{1,9},{5... | collective-permute-start | bytes 27656 | tf_op jit(solution)/shard_map/ppermute | solution.py:364
  391.0 26.6 %collective-permute-start.42 = (bf16[256,1024]{0,1:T(8,128)(2,1)S(1)}, bf16[256,1024]{0,1:T(8,128)(2,1)S(1)}, u32[]{:S(2)}, u32[]{:S(2)}) collective-permute-start(bf16[256,1024]{0,1:T(8,128)(2,1)S(1)} %add_convert_fusion.3), channel_id=1, source_target_pairs={{0,2},{1,3},{2,0},{3,1},{4,6},{5,7},{6,4},{7,5},{8,10},{9,11},{10,... | collective-permute-start | bytes 1572872 | tf_op jit(solution)/shard_map/ppermute | solution.py:364
  394.4 10.8 %collective-permute-start.38 = (f32[4,128]{1,0:T(4,128)S(1)}, f32[4,128]{1,0:T(4,128)S(1)}, u32[]{:S(2)}, u32[]{:S(2)}) collective-permute-start(f32[4,128]{1,0:T(4,128)S(1)} %maximum_bitcast_fusion.1), channel_id=1, source_target_pairs={{0,1},{1,0},{2,3},{3,2},{4,5},{5,4},{6,7},{7,6},{8,9},{9,8},{10,11... | collective-permute-start | bytes 6152 | tf_op jit(solution)/shard_map/ppermute | solution.py:364
  395.9 33.7 %collective-permute-start.32 = (bf16[256,1024]{1,0:T(8,128)(2,1)S(1)}, bf16[256,1024]{1,0:T(8,128)(2,1)S(1)}, u32[]{:S(2)}, u32[]{:S(2)}) collective-permute-start(bf16[256,1024]{1,0:T(8,128)(2,1)S(1)} %slice.534), channel_id=1, source_target_pairs={{1,0},{2,1},{3,2},{5,4},{6,5},{7,6},{9,8},{10,9},{11,10},{13,12},{... | collective-permute-start | bytes 1572872 | tf_op jit(solution)/shard_map/ppermute | solution.py:367
  405.3 23.3 %collective-permute-start.39 = (f32[4,128]{1,0:T(4,128)S(1)}, f32[4,128]{1,0:T(4,128)S(1)}, u32[]{:S(2)}, u32[]{:S(2)}) collective-permute-start(f32[4,128]{1,0:T(4,128)S(1)} %fusion.47), channel_id=1, source_target_pairs={{0,2},{1,3},{2,0},{3,1},{4,6},{5,7},{6,4},{7,5},{8,10},{9,11},{10,... | collective-permute-start | bytes 6152 | tf_op jit(solution)/shard_map/ppermute | solution.py:364
  417.7 15.0 %collective-permute-start.43 = (bf16[256,1024]{0,1:T(8,128)(2,1)S(1)}, bf16[256,1024]{0,1:T(8,128)(2,1)S(1)}, u32[]{:S(2)}, u32[]{:S(2)}) collective-permute-start(bf16[256,1024]{0,1:T(8,128)(2,1)S(1)} %add_convert_fusion.2), channel_id=1, source_target_pairs={{0,1},{1,0},{2,3},{3,2},{4,5},{5,4},{6,7},{7,6},{8,9},{9,8},{10,11... | collective-permute-start | bytes 1572872 | tf_op jit(solution)/shard_map/ppermute | solution.py:364
  430.6 16.6 %collective-permute-start.33 = (bf16[256,1024]{1,0:T(8,128)(2,1)}, bf16[256,1024]{1,0:T(8,128)(2,1)}, u32[]{:S(2)}, u32[]{:S(2)}) collective-permute-start(bf16[256,1024]{1,0:T(8,128)(2,1)} %fusion.32), channel_id=1, source_target_pairs={{1,0},{2,1},{3,2},{5,4},{6,5},{7,6},{9,8},{10,9},{11,10},{13,12},{... | collective-permute-start | bytes 1572872 | tf_op jit(solution)/shard_map/ppermute | solution.py:367
  (67 other events, 253.0 us)

commit v4 on v3

--- a/solution.py
+++ b/solution.py
@@ -482,11 +482,10 @@
         normed_all = normed.reshape(2 * K, D)
         kv_raw = mm(normed_all, wkv, 1, 0)
         q_raw = mm(normed_own, wq, 1, 0)
-        w_gu = exchange(after(gu_copies, q_raw))
-        d_parts = spread(after(d_piece, q_raw))
+        w_gu = exchange(after(gu_copies, qkv))
+        d_parts = spread(after(d_piece, qkv))
         context = attend(q_raw, after(kv_raw, q_raw), tables, 2, R, K, group, hd)
-        context = after(context, w_gu)
-        cot = after(cotangent[0], context)
+        cot = after(cotangent[0], q_raw)
         cot_z = hop(cot, "ctx", 1)
         us = [cot, swap(cot), cot_z, swap(cot_z)]
         w_o = by_chip([after(p, context) for p in o_parts], c)
@@ -494,7 +493,7 @@
         middle = toks[0, K - R :].astype(f32) + part[:R] + swap(part[R:].astype(bf16)).astype(f32)
 
         nf, scale_ffn = row_norm(middle)
-        nf_z = hop(nf, "ctx", 1)
+        nf_z = hop(after(nf, w_gu), "ctx", 1)
         xs = [nf, swap(nf)]
         hidden, gug, ng_own, out_own = feed(xs, us[:2], w_gu, d_parts, c, 0, 4)
         xs += [nf_z, swap(after(nf_z, ng_own))]

time: 459 us -> 445 us (0.969)
  waiting for transfers between devices: 177 us -> 146 us
  starting transfers between devices: 63.1 us -> 80.9 us
  local copies, waits for them, and re-layouts: 55 us -> 49.9 us
    ppermute x43, starting transfers between devices: 31.7 us -> 49.5 us  [hop(): return lax.ppermute(x, axis, [(i, i ^ bit) for i in range(sizes[axis])])]
    ppermute x43, waiting for transfers between devices: 136 us -> 119 us  [hop(): return lax.ppermute(x, axis, [(i, i ^ bit) for i in range(sizes[axis])])]
    all_to_all x2, waiting for transfers between devices: 26 us -> 12.2 us  [exchange(): out = lax.all_to_all(copies, 'fsdp', 0, 0, axis_index_groups=groups)]
    unnamed x146 -> x132, local copies, waits for them, and re-layouts: 26.2 us -> 22.9 us
  transfers between devices with their start and end apart: 51 -> 51, of which waited for: 25 -> 16; matrix products, arithmetic and copies ran while one was open for 25% -> 29% of each run, Pallas kernels for 12% -> 12%
where the time goes in v4:
time: 445 us; the launch traced here: 440 us
  waiting for transfers between devices  146 us (33%)
  starting transfers between devices  80.9 us (18%)
  Pallas kernels  64.6 us (15%)
  other arithmetic  57.8 us (13%)
  local copies, waits for them, and re-layouts  49.9 us (11%)
  matrix products  38.4 us (9%)
    ppermute x43, waiting for transfers between devices, hop(): return lax.ppermute(x, axis, [(i, i ^ bit) for i in range(sizes[axis])])  119 us
    ppermute x43, starting transfers between devices, hop(): return lax.ppermute(x, axis, [(i, i ^ bit) for i in range(sizes[axis])])  49.5 us
    dot_general x11, matrix products, mm(): lax.dot_general(a, b, (((ca,), (cb,)), ((), ())), preferred_element_type=...  38.4 us
    pallas_call x1, Pallas kernels, attend_back(): pl.pallas_call(functools.partial(attend_back_kernel, group, keys - rows),...  24.8 us
    unnamed x132, local copies, waits for them, and re-layouts  22.9 us
    pallas_call x2, Pallas kernels, feed(): pl.pallas_call(body, grid_spec=pltpu.PrefetchScalarGridSpec(num_scalar_pr...  19.8 us
    ppermute x4, waiting for transfers between devices, shift(): lax.ppermute(x, 'ctx', [(i, i + by) for i in range(Z) if 0 <= i + by < Z])  15 us
    pallas_call x1, Pallas kernels, attend(): pl.pallas_call(functools.partial(attend_kernel, group, keys - rows), grid...  14.1 us
  transfers between devices with their start and end apart: 51, of which 16 were waited for; matrix products, arithmetic and copies ran while one was open for 29% of the time, Pallas kernels for 12%

profile of v4, /device:TPU:0, one launch (start us, length us, event | category | flops | bytes accessed | tf_op | source)
XLA Modules:
  0.0 440.0 jit_solution(13025705695307347478)
XLA Ops:
  7.3 2.5 broadcast_in_dim.55
  9.8 4.6 %collective-permute-start.2 = (bf16[272,1024]{1,0:T(8,128)(2,1)S(1)}, bf16[272,1024]{1,0:T(8,128)(2,1)S(1)}, u32[]{:S(2)}, u32[]{:S(2)}) collective-permute-start(bf16[272,1024]{1,0:T(8,128)(2,1)S(1)} %fusion.35), channel_id=1, source_target_pairs={{0,1},{1,2},{2,3},{4,5},{5,6},{6,7},{8,9},{9,10},{10,11},{12,13},{... | collective-permute-start | bytes 1671176 | tf_op jit(solution)/shard_map/ppermute | solution.py:367
  14.4 4.5 %collective-permute-start.1 = (bf16[272,1024]{1,0:T(8,128)(2,1)S(1)}, bf16[272,1024]{1,0:T(8,128)(2,1)S(1)}, u32[]{:S(2)}, u32[]{:S(2)}) collective-permute-start(bf16[272,1024]{1,0:T(8,128)(2,1)S(1)} %fusion.35), channel_id=1, source_target_pairs={{0,2},{1,3},{4,6},{5,7},{8,10},{9,11},{12,14},{13,15},{16,18},{17,... | collective-permute-start | bytes 1671176 | tf_op jit(solution)/shard_map/ppermute | solution.py:367
  18.9 4.9 %all-to-all-start = ((bf16[4,256,2048]{2,1,0:T(8,128)(2,1)}), bf16[4,256,2048]{2,1,0:T(8,128)(2,1)}, u32[]{:S(2)}, u32[]{:S(2)}) async-start(bf16[4,256,2048]{2,1,0:T(8,128)(2,1)} %broadcast_in_dim.55), calls=%async_computation | async-start | bytes 8388608 | tf_op jit(solution)/shard_map/all_to_all | solution.py:386
  23.8 3.6 collective-permute-done.2
  27.4 11.4 %collective-permute-done.1 = bf16[272,1024]{1,0:T(8,128)(2,1)S(1)} collective-permute-done((bf16[272,1024]{1,0:T(8,128)(2,1)S(1)}, bf16[272,1024]{1,0:T(8,128)(2,1)S(1)}, u32[]{:S(2)}, u32[]{:S(2)}) %collective-permute-start.1) | collective-permute-done | bytes 557088 | tf_op jit(solution)/shard_map/ppermute | solution.py:367
  39.6 3.1 pad_maximum_fusion.3
  48.4 2.9 fusion.2
  54.2 2.7 fusion
  59.3 12.2 %all-to-all-done = bf16[4,256,2048]{2,1,0:T(8,128)(2,1)} async-done(((bf16[4,256,2048]{2,1,0:T(8,128)(2,1)}), bf16[4,256,2048]{2,1,0:T(8,128)(2,1)}, u32[]{:S(2)}, u32[]{:S(2)}) %all-to-all-start) | async-done | bytes 4194336 | tf_op jit(solution)/shard_map/all_to_all | solution.py:386
  76.3 6.4 %fusion.16.kv_ref = f32[1536,1024]{1,0:T(8,128)S(1)} fusion(bf16[1536,1024]{1,0:T(8,128)(2,1)} %bitcast.135, bf16[1024,2048]{1,0:T(8,128)(2,1)} %bitcast.10), kind=kOutput, calls=%fused_computation.34 | convolution fusion | flops 3221225472 | bytes 11534336 | tf_op jit(solution)/shard_map/dot_general | solution.py:22
  82.7 4.4 %fusion.20.q_ref = f32[512,1024]{1,0:T(8,128)S(1)} fusion(bf16[512,1024]{1,0:T(8,128)(2,1)S(1)} %bitcast.142, bf16[1024,2048]{1,0:T(8,128)(2,1)} %bitcast.10), kind=kOutput, calls=%fused_computation.38 | convolution fusion | flops 1073741824 | bytes 5242880 | tf_op jit(solution)/shard_map/dot_general | solution.py:22
  87.2 14.1 %attend.1 = bf16[512,1024]{1,0:T(8,128)(2,1)S(1)} custom-call(f32[512,1024]{1,0:T(8,128)S(1)} %fusion.20.q_ref, f32[1536,1024]{1,0:T(8,128)S(1)} %fusion.16.kv_ref, f32[768,128]{1,0:T(8,128)S(1)} %get-tuple-element.199.cos_ref, f32[768,128]{1,0:T(8,128)S(1)} %get-tuple-element.200.sin_ref, s32[2,256,1]{2,1,0:T(8,128)S(1)} %copy.31.segc_ref, ...), custom_call_target="tpu_custom_call" | custom-call | flops 1342177280 | bytes 9437184 | tf_op jit(solution)/shard_map/attend/pallas_call | solution.py:153
  102.2 5.2 %all-to-all-start.1 = ((bf16[4,256,1536]{2,1,0:T(8,128)(2,1)}), bf16[4,256,1536]{2,1,0:T(8,128)(2,1)}, u32[]{:S(2)}, u32[]{:S(2)}) async-start(bf16[4,256,1536]{2,1,0:T(8,128)(2,1)} %broadcast_in_dim.57), calls=%async_computation.1 | async-start | bytes 6291456 | tf_op jit(solution)/shard_map/all_to_all | solution.py:386
  122.2 28.4 %collective-permute-done.11.refs_7_ = bf16[192,1024]{1,0:T(8,128)(2,1)} collective-permute-done((bf16[192,1024]{1,0:T(8,128)(2,1)}, bf16[192,1024]{1,0:T(8,128)(2,1)}, u32[]{:S(2)}, u32[]{:S(2)}) %collective-permute-start.11) | collective-permute-done | bytes 393248 | tf_op jit(solution)/shard_map/ppermute | solution.py:364
  154.5 5.8 %collective-permute-done.13.refs_9_ = bf16[192,1024]{1,0:T(8,128)(2,1)} collective-permute-done((bf16[192,1024]{1,0:T(8,128)(2,1)}, bf16[192,1024]{1,0:T(8,128)(2,1)}, u32[]{:S(2)}, u32[]{:S(2)}) %collective-permute-start.13) | collective-permute-done | bytes 393248 | tf_op jit(solution)/shard_map/ppermute | solution.py:364
  160.3 9.9 %feed.2 = (bf16[1024,768]{1,0:T(8,128)(2,1)}, bf16[1024,1536]{1,0:T(8,128)(2,1)}, bf16[512,1024]{1,0:T(8,128)(2,1)}, bf16[512,1024]{1,0:T(8,128)(2,1)}) custom-call(s32[1]{0:T(128)} %bitcast.19.refs_0_, bf16[256,1024]{1,0:T(8,128)(2,1)} %multiply_convert_fusion.refs_1_, bf16[256,1024]{1,0:T(8,128)(2,1)} %collective-permute-done.9.refs_2_, ...), custom_call_target="tpu_custom_call" | custom-call | flops 5637144576 | bytes 11272192 | tf_op jit(solution)/shard_map/feed/pallas_call | solution.py:323
  172.6 9.9 %feed.3 = (bf16[1024,768]{1,0:T(8,128)(2,1)}, bf16[1024,1536]{1,0:T(8,128)(2,1)}, bf16[512,1024]{1,0:T(8,128)(2,1)}, bf16[512,1024]{1,0:T(8,128)(2,1)}) custom-call(s32[1]{0:T(128)} %bitcast.19.refs_0_, bf16[256,1024]{1,0:T(8,128)(2,1)} %collective-permute-done.15.refs_1_, ...), custom_call_target="tpu_custom_call", output_to_operand_aliasing={{0}: (10, {}), {1}: (11, {})} | custom-call | flops 5637144576 | bytes 11272192 | tf_op jit(solution)/shard_map/feed/pallas_call | solution.py:323
  189.8 3.3 collective-permute-start.21
  193.0 5.1 %convolution_convert_fusion = bf16[1024,1536]{1,0:T(8,128)(2,1)} fusion(bf16[1024,1024]{1,0:T(8,128)(2,1)S(1)} %pad_maximum_fusion.2, bf16[1024,1536]{1,0:T(8,128)(2,1)S(1)} %copy-done.52), kind=kOutput, calls=%fused_computation.9 | convolution fusion | flops 3222798336 | bytes 8388608 | tf_op jit(solution)/shard_map/dot_general | solution.py:22
  198.1 4.8 %all-to-all-start.2 = ((bf16[4,256,1536]{2,1,0:T(8,128)(2,1)}), bf16[4,256,1536]{2,1,0:T(8,128)(2,1)}, u32[]{:S(2)}, u32[]{:S(2)}) async-start(bf16[4,256,1536]{2,1,0:T(8,128)(2,1)} %bitcast.137), calls=%async_computation.2 | async-start | bytes 6291456 | tf_op jit(solution)/shard_map/all_to_all | solution.py:393
  203.0 4.0 fusion.22
  208.6 2.8 fusion.52
  219.6 24.8 %attend_back.1 = (bf16[512,1024]{1,0:T(8,128)(2,1)S(1)}, bf16[1536,1024]{1,0:T(8,128)(2,1)S(1)}, f32[1,128]{1,0:T(1,128)S(1)}, f32[1,128]{1,0:T(1,128)S(1)}) custom-call(f32[512,1024]{1,0:T(8,128)S(1)} %fusion.20.q_ref, f32[1536,1024]{1,0:T(8,128)S(1)} %bitcast.114, bf16[512,1024]{1,0:T(8,128)(2,1)S(1)} %convolution_convert_fusion.4.dc_ref, ...), custom_call_target="tpu_custom_call" | custom-call | flops 3355443200 | bytes 13631488 | tf_op jit(solution)/shard_map/attend_back/pallas_call | solution.py:172
  247.0 2.5 convert_reduce_fusion.1
  255.3 2.7 collective-permute-start.29
  260.7 3.4 collective-permute-start.26
  264.1 4.0 convolution_convert_fusion.1
  272.3 4.9 %all-to-all-start.3 = ((bf16[4,256,2048]{1,2,0:T(8,128)(2,1)}), bf16[4,256,2048]{1,2,0:T(8,128)(2,1)}, u32[]{:S(2)}, u32[]{:S(2)}) async-start(bf16[4,256,2048]{1,2,0:T(8,128)(2,1)} %bitcast.131), calls=%async_computation.3 | async-start | bytes 8388608 | tf_op jit(solution)/shard_map/all_to_all | solution.py:393
  277.1 21.4 %collective-permute-done.26 = bf16[256,1536]{1,0:T(8,128)(2,1)} collective-permute-done((bf16[256,1536]{1,0:T(8,128)(2,1)}, bf16[256,1536]{1,0:T(8,128)(2,1)}, u32[]{:S(2)}, u32[]{:S(2)}) %collective-permute-start.26) | collective-permute-done | bytes 786464 | tf_op jit(solution)/shard_map/ppermute | solution.py:364
  307.1 4.8 %collective-permute-done.30 = bf16[128,1024]{1,0:T(8,128)(2,1)S(1)} collective-permute-done((bf16[128,1024]{1,0:T(8,128)(2,1)S(1)}, bf16[128,1024]{1,0:T(8,128)(2,1)S(1)}, u32[]{:S(2)}, u32[]{:S(2)}) %collective-permute-start.30) | collective-permute-done | bytes 262176 | tf_op jit(solution)/shard_map/ppermute | solution.py:364
  312.0 3.0 collective-permute-start.44
  315.0 4.2 fusion.18
  319.3 5.1 %fusion.14 = f32[1536,1024]{1,0:T(8,128)S(1)} fusion(bf16[1536,1024]{1,0:T(8,128)(2,1)S(1)} %copy-done.13, bf16[1024,2048]{1,0:T(8,128)(2,1)} %bitcast.10), kind=kOutput, calls=%fused_computation.32 | convolution fusion | flops 3221225472 | bytes 11534336 | tf_op jit(solution)/shard_map/dot_general | solution.py:22
  324.4 15.8 %collective-permute-done.44 = bf16[320,1024]{1,0:T(8,128)(2,1)S(1)} collective-permute-done((bf16[320,1024]{1,0:T(8,128)(2,1)S(1)}, bf16[320,1024]{1,0:T(8,128)(2,1)S(1)}, u32[]{:S(2)}, u32[]{:S(2)}) %collective-permute-start.44) | collective-permute-done | bytes 655392 | tf_op jit(solution)/shard_map/ppermute | solution.py:364
  340.4 4.2 collective-permute-start.45
  344.6 3.0 pad_add_fusion
  347.9 3.4 place_units.1
  351.4 6.9 %collective-permute-done.45 = bf16[320,1024]{1,0:T(8,128)(2,1)S(1)} collective-permute-done((bf16[320,1024]{1,0:T(8,128)(2,1)S(1)}, bf16[320,1024]{1,0:T(8,128)(2,1)S(1)}, u32[]{:S(2)}, u32[]{:S(2)}) %collective-permute-start.45) | collective-permute-done | bytes 655392 | tf_op jit(solution)/shard_map/ppermute | solution.py:364
  360.8 3.1 convert_reduce_fusion
  372.3 3.3 collective-permute-start.37
  376.3 4.3 collective-permute-done.41
  385.3 7.3 %collective-permute-done.38 = f32[4,128]{1,0:T(4,128)S(1)} collective-permute-done((f32[4,128]{1,0:T(4,128)S(1)}, f32[4,128]{1,0:T(4,128)S(1)}, u32[]{:S(2)}, u32[]{:S(2)}) %collective-permute-start.38) | collective-permute-done | bytes 2080 | tf_op jit(solution)/shard_map/ppermute | solution.py:364
  392.6 5.8 %collective-permute-start.39 = (f32[4,128]{1,0:T(4,128)S(1)}, f32[4,128]{1,0:T(4,128)S(1)}, u32[]{:S(2)}, u32[]{:S(2)}) collective-permute-start(f32[4,128]{1,0:T(4,128)S(1)} %fusion.47), channel_id=1, source_target_pairs={{0,2},{1,3},{2,0},{3,1},{4,6},{5,7},{6,4},{7,5},{8,10},{9,11},{10,... | collective-permute-start | bytes 6152 | tf_op jit(solution)/shard_map/ppermute | solution.py:364
  398.4 9.3 %collective-permute-done.42 = bf16[256,1024]{0,1:T(8,128)(2,1)S(1)} collective-permute-done((bf16[256,1024]{0,1:T(8,128)(2,1)S(1)}, bf16[256,1024]{0,1:T(8,128)(2,1)S(1)}, u32[]{:S(2)}, u32[]{:S(2)}) %collective-permute-start.42) | collective-permute-done | bytes 524320 | tf_op jit(solution)/shard_map/ppermute | solution.py:364
  408.0 9.9 %collective-permute-done.39 = f32[4,128]{1,0:T(4,128)S(1)} collective-permute-done((f32[4,128]{1,0:T(4,128)S(1)}, f32[4,128]{1,0:T(4,128)S(1)}, u32[]{:S(2)}, u32[]{:S(2)}) %collective-permute-start.39) | collective-permute-done | bytes 2080 | tf_op jit(solution)/shard_map/ppermute | solution.py:364
  426.0 2.5 copy.35
  437.2 2.5 fusion.31
  (305 shorter events, 119.1 us)
Async XLA Ops:
  4.7 2.3 collective-permute-start
  9.8 17.6 %collective-permute-start.2 = (bf16[272,1024]{1,0:T(8,128)(2,1)S(1)}, bf16[272,1024]{1,0:T(8,128)(2,1)S(1)}, u32[]{:S(2)}, u32[]{:S(2)}) collective-permute-start(bf16[272,1024]{1,0:T(8,128)(2,1)S(1)} %fusion.35), channel_id=1, source_target_pairs={{0,1},{1,2},{2,3},{4,5},{5,6},{6,7},{8,9},{9,10},{10,11},{12,13},{... | collective-permute-start | bytes 1671176 | tf_op jit(solution)/shard_map/ppermute | solution.py:367
  14.4 24.4 %collective-permute-start.1 = (bf16[272,1024]{1,0:T(8,128)(2,1)S(1)}, bf16[272,1024]{1,0:T(8,128)(2,1)S(1)}, u32[]{:S(2)}, u32[]{:S(2)}) collective-permute-start(bf16[272,1024]{1,0:T(8,128)(2,1)S(1)} %fusion.35), channel_id=1, source_target_pairs={{0,2},{1,3},{4,6},{5,7},{8,10},{9,11},{12,14},{13,15},{16,18},{17,... | collective-permute-start | bytes 1671176 | tf_op jit(solution)/shard_map/ppermute | solution.py:367
  18.9 52.5 %all-to-all-start = ((bf16[4,256,2048]{2,1,0:T(8,128)(2,1)}), bf16[4,256,2048]{2,1,0:T(8,128)(2,1)}, u32[]{:S(2)}, u32[]{:S(2)}) async-start(bf16[4,256,2048]{2,1,0:T(8,128)(2,1)} %broadcast_in_dim.55), calls=%async_computation | async-start | bytes 8388608 | tf_op jit(solution)/shard_map/all_to_all | solution.py:386
  42.8 5.4 %collective-permute-start.3 = (bf16[3,272,1024]{2,1,0:T(8,128)(2,1)}, bf16[3,272,1024]{2,1,0:T(8,128)(2,1)}, u32[]{:S(2)}, u32[]{:S(2)}) collective-permute-start(bf16[3,272,1024]{2,1,0:T(8,128)(2,1)} %get-tuple-element.162), channel_id=1, source_target_pairs={{0,4},{4,0},{8,12},{12,8},{16,20},{20,16},{24,28},{28,24},{1,5},{5... | collective-permute-start | bytes 5013512 | tf_op jit(solution)/shard_map/ppermute | solution.py:364
  71.5 37.4 %collective-permute-start.5 = (bf16[256,1024]{1,0:T(8,128)(2,1)}, bf16[256,1024]{1,0:T(8,128)(2,1)}, u32[]{:S(2)}, u32[]{:S(2)}) collective-permute-start(bf16[256,1024]{1,0:T(8,128)(2,1)} %param.23), channel_id=1, source_target_pairs={{0,8},{4,12},{8,0},{12,4},{16,24},{20,28},{24,16},{28,20},{1,9},{5... | collective-permute-start | bytes 1572872 | tf_op jit(solution)/shard_map/ppermute | solution.py:364
  72.9 36.0 %collective-permute-start.6 = (bf16[256,1024]{1,0:T(8,128)(2,1)}, bf16[256,1024]{1,0:T(8,128)(2,1)}, u32[]{:S(2)}, u32[]{:S(2)}) collective-permute-start(bf16[256,1024]{1,0:T(8,128)(2,1)} %param.23), channel_id=1, source_target_pairs={{0,16},{4,20},{8,24},{12,28},{16,0},{20,4},{24,8},{28,12},{1,17},{... | collective-permute-start | bytes 1572872 | tf_op jit(solution)/shard_map/ppermute | solution.py:364
  73.5 37.6 %collective-permute-start.7 = (bf16[256,1024]{1,0:T(8,128)(2,1)}, bf16[256,1024]{1,0:T(8,128)(2,1)}, u32[]{:S(2)}, u32[]{:S(2)}) collective-permute-start(bf16[256,1024]{1,0:T(8,128)(2,1)} %param.23), channel_id=1, source_target_pairs={{0,24},{4,28},{8,16},{12,20},{16,8},{20,12},{24,0},{28,4},{1,25},{... | collective-permute-start | bytes 1572872 | tf_op jit(solution)/shard_map/ppermute | solution.py:364
  102.2 49.9 %all-to-all-start.1 = ((bf16[4,256,1536]{2,1,0:T(8,128)(2,1)}), bf16[4,256,1536]{2,1,0:T(8,128)(2,1)}, u32[]{:S(2)}, u32[]{:S(2)}) async-start(bf16[4,256,1536]{2,1,0:T(8,128)(2,1)} %broadcast_in_dim.57), calls=%async_computation.1 | async-start | bytes 6291456 | tf_op jit(solution)/shard_map/all_to_all | solution.py:386
  113.7 3.9 collective-permute-start.8
  113.7 46.6 %collective-permute-start.10 = (bf16[256,1024]{1,0:T(8,128)(2,1)}, bf16[256,1024]{1,0:T(8,128)(2,1)}, u32[]{:S(2)}, u32[]{:S(2)}) collective-permute-start(bf16[256,1024]{1,0:T(8,128)(2,1)} %bitcast.20.refs_3_), channel_id=1, source_target_pairs={{0,4},{4,0},{8,12},{12,8},{16,20},{20,16},{24,28},{28,24},{1,5},{5... | collective-permute-start | bytes 1572872 | tf_op jit(solution)/shard_map/ppermute | solution.py:364
  114.2 37.9 %collective-permute-start.17 = (bf16[256,1024]{1,0:T(8,128)(2,1)}, bf16[256,1024]{1,0:T(8,128)(2,1)}, u32[]{:S(2)}, u32[]{:S(2)}) collective-permute-start(bf16[256,1024]{1,0:T(8,128)(2,1)} %bitcast.20.refs_3_), channel_id=1, source_target_pairs={{0,1},{1,0},{2,3},{3,2},{4,5},{5,4},{6,7},{7,6},{8,9},{9,8},{10,11... | collective-permute-start | bytes 1572872 | tf_op jit(solution)/shard_map/ppermute | solution.py:364
  115.5 35.1 %collective-permute-start.11 = (bf16[192,1024]{1,0:T(8,128)(2,1)}, bf16[192,1024]{1,0:T(8,128)(2,1)}, u32[]{:S(2)}, u32[]{:S(2)}) collective-permute-start(bf16[192,1024]{1,0:T(8,128)(2,1)} %slice_select_fusion.1.refs_6_), channel_id=1, source_target_pairs={{0,8},{4,12},{8,0},{12,4},{16,24},{20,28},{24,16},{28,20},{1,9},{5... | collective-permute-start | bytes 1179656 | tf_op jit(solution)/shard_map/ppermute | solution.py:364
  120.8 39.6 %collective-permute-start.9 = (bf16[256,1024]{1,0:T(8,128)(2,1)}, bf16[256,1024]{1,0:T(8,128)(2,1)}, u32[]{:S(2)}, u32[]{:S(2)}) collective-permute-start(bf16[256,1024]{1,0:T(8,128)(2,1)} %multiply_convert_fusion.refs_1_), channel_id=1, source_target_pairs={{0,4},{4,0},{8,12},{12,8},{16,20},{20,16},{24,28},{28,24},{1,5},{5... | collective-permute-start | bytes 1572872 | tf_op jit(solution)/shard_map/ppermute | solution.py:364
  120.8 31.4 %collective-permute-start.12 = (bf16[192,1024]{1,0:T(8,128)(2,1)}, bf16[192,1024]{1,0:T(8,128)(2,1)}, u32[]{:S(2)}, u32[]{:S(2)}) collective-permute-start(bf16[192,1024]{1,0:T(8,128)(2,1)} %slice_select_fusion.1.refs_6_), channel_id=1, source_target_pairs={{0,16},{4,20},{8,24},{12,28},{16,0},{20,4},{24,8},{28,12},{1,17},{... | collective-permute-start | bytes 1179656 | tf_op jit(solution)/shard_map/ppermute | solution.py:364
  150.7 9.7 %collective-permute-start.13 = (bf16[192,1024]{1,0:T(8,128)(2,1)}, bf16[192,1024]{1,0:T(8,128)(2,1)}, u32[]{:S(2)}, u32[]{:S(2)}) collective-permute-start(bf16[192,1024]{1,0:T(8,128)(2,1)} %slice_select_fusion.1.refs_6_), channel_id=1, source_target_pairs={{0,24},{4,28},{8,16},{12,20},{16,8},{20,12},{24,0},{28,4},{1,25},{... | collective-permute-start | bytes 1179656 | tf_op jit(solution)/shard_map/ppermute | solution.py:364
  152.2 18.2 %collective-permute-start.18 = (bf16[256,1024]{1,0:T(8,128)(2,1)}, bf16[256,1024]{1,0:T(8,128)(2,1)}, u32[]{:S(2)}, u32[]{:S(2)}) collective-permute-start(bf16[256,1024]{1,0:T(8,128)(2,1)} %collective-permute-done.17.refs_3_), channel_id=1, source_target_pairs={{0,4},{4,0},{8,12},{12,8},{16,20},{20,16},{24,28},{28,24},{1,5},{5... | collective-permute-start | bytes 1572872 | tf_op jit(solution)/shard_map/ppermute | solution.py:364
  152.2 18.1 %collective-permute-start.15 = (bf16[256,1024]{1,0:T(8,128)(2,1)}, bf16[256,1024]{1,0:T(8,128)(2,1)}, u32[]{:S(2)}, u32[]{:S(2)}) collective-permute-start(bf16[256,1024]{1,0:T(8,128)(2,1)} %multiply_convert_fusion.refs_1_), channel_id=1, source_target_pairs={{0,1},{1,0},{2,3},{3,2},{4,5},{5,4},{6,7},{7,6},{8,9},{9,8},{10,11... | collective-permute-start | bytes 1572872 | tf_op jit(solution)/shard_map/ppermute | solution.py:364
  170.3 2.3 collective-permute-start.16
  183.6 5.1 %collective-permute-start.20 = (bf16[256,1024]{1,0:T(8,128)(2,1)S(1)}, bf16[256,1024]{1,0:T(8,128)(2,1)S(1)}, u32[]{:S(2)}, u32[]{:S(2)}) collective-permute-start(bf16[256,1024]{1,0:T(8,128)(2,1)S(1)} %slice.299), channel_id=1, source_target_pairs={{0,4},{4,0},{8,12},{12,8},{16,20},{20,16},{24,28},{28,24},{1,5},{5... | collective-permute-start | bytes 1572872 | tf_op jit(solution)/shard_map/ppermute | solution.py:364
  185.7 21.3 %collective-permute-start.19 = (bf16[256,1024]{1,0:T(8,128)(2,1)}, bf16[256,1024]{1,0:T(8,128)(2,1)}, u32[]{:S(2)}, u32[]{:S(2)}) collective-permute-start(bf16[256,1024]{1,0:T(8,128)(2,1)} %slice.297), channel_id=1, source_target_pairs={{0,4},{4,0},{8,12},{12,8},{16,20},{20,16},{24,28},{28,24},{1,5},{5... | collective-permute-start | bytes 1572872 | tf_op jit(solution)/shard_map/ppermute | solution.py:364
  189.8 17.2 %collective-permute-start.21 = (bf16[256,1024]{1,0:T(8,128)(2,1)}, bf16[256,1024]{1,0:T(8,128)(2,1)}, u32[]{:S(2)}, u32[]{:S(2)}) collective-permute-start(bf16[256,1024]{1,0:T(8,128)(2,1)} %add_convert_fusion.6), channel_id=1, source_target_pairs={{0,1},{1,0},{2,3},{3,2},{4,5},{5,4},{6,7},{7,6},{8,9},{9,8},{10,11... | collective-permute-start | bytes 1572872 | tf_op jit(solution)/shard_map/ppermute | solution.py:364
  198.1 48.9 %all-to-all-start.2 = ((bf16[4,256,1536]{2,1,0:T(8,128)(2,1)}), bf16[4,256,1536]{2,1,0:T(8,128)(2,1)}, u32[]{:S(2)}, u32[]{:S(2)}) async-start(bf16[4,256,1536]{2,1,0:T(8,128)(2,1)} %bitcast.137), calls=%async_computation.2 | async-start | bytes 6291456 | tf_op jit(solution)/shard_map/all_to_all | solution.py:393
  211.5 3.2 collective-permute-start.24
  214.4 44.1 %collective-permute-start.23 = (bf16[256,1024]{1,0:T(8,128)(2,1)}, bf16[256,1024]{1,0:T(8,128)(2,1)}, u32[]{:S(2)}, u32[]{:S(2)}) collective-permute-start(bf16[256,1024]{1,0:T(8,128)(2,1)} %add_convert_fusion.5), channel_id=1, source_target_pairs={{0,1},{1,0},{2,3},{3,2},{4,5},{5,4},{6,7},{7,6},{8,9},{9,8},{10,11... | collective-permute-start | bytes 1572872 | tf_op jit(solution)/shard_map/ppermute | solution.py:364
  250.4 8.4 %collective-permute-start.25 = (bf16[128,1536]{1,0:T(8,128)(2,1)}, bf16[128,1536]{1,0:T(8,128)(2,1)}, u32[]{:S(2)}, u32[]{:S(2)}) collective-permute-start(bf16[128,1536]{1,0:T(8,128)(2,1)} %get-tuple-element.169), channel_id=1, source_target_pairs={{0,4},{4,0},{8,12},{12,8},{16,20},{20,16},{24,28},{28,24},{1,5},{5... | collective-permute-start | bytes 1179656 | tf_op jit(solution)/shard_map/ppermute | solution.py:364
  252.6 51.6 %collective-permute-start.14 = (bf16[256,1024]{1,0:T(8,128)(2,1)}, bf16[256,1024]{1,0:T(8,128)(2,1)}, u32[]{:S(2)}, u32[]{:S(2)}) collective-permute-start(bf16[256,1024]{1,0:T(8,128)(2,1)} %slice.293), channel_id=1, source_target_pairs={{0,4},{4,0},{8,12},{12,8},{16,20},{20,16},{24,28},{28,24},{1,5},{5... | collective-permute-start | bytes 1572872 | tf_op jit(solution)/shard_map/ppermute | solution.py:364
  255.3 44.8 %collective-permute-start.29 = (bf16[448,1024]{1,0:T(8,128)(2,1)}, bf16[448,1024]{1,0:T(8,128)(2,1)}, u32[]{:S(2)}, u32[]{:S(2)}) collective-permute-start(bf16[448,1024]{1,0:T(8,128)(2,1)} %get-tuple-element.155), channel_id=1, source_target_pairs={{0,24},{4,28},{8,16},{12,20},{16,8},{20,12},{24,0},{28,4},{1,25},{... | collective-permute-start | bytes 2752520 | tf_op jit(solution)/shard_map/ppermute | solution.py:364
  257.9 42.1 %collective-permute-start.28 = (bf16[448,1024]{1,0:T(8,128)(2,1)}, bf16[448,1024]{1,0:T(8,128)(2,1)}, u32[]{:S(2)}, u32[]{:S(2)}) collective-permute-start(bf16[448,1024]{1,0:T(8,128)(2,1)} %get-tuple-element.156), channel_id=1, source_target_pairs={{0,16},{4,20},{8,24},{12,28},{16,0},{20,4},{24,8},{28,12},{1,17},{... | collective-permute-start | bytes 2752520 | tf_op jit(solution)/shard_map/ppermute | solution.py:364
  258.5 41.6 %collective-permute-start.27 = (bf16[448,1024]{1,0:T(8,128)(2,1)}, bf16[448,1024]{1,0:T(8,128)(2,1)}, u32[]{:S(2)}, u32[]{:S(2)}) collective-permute-start(bf16[448,1024]{1,0:T(8,128)(2,1)} %get-tuple-element.157), channel_id=1, source_target_pairs={{0,8},{4,12},{8,0},{12,4},{16,24},{20,28},{24,16},{28,20},{1,9},{5... | collective-permute-start | bytes 2752520 | tf_op jit(solution)/shard_map/ppermute | solution.py:364
  260.7 37.8 %collective-permute-start.26 = (bf16[256,1536]{1,0:T(8,128)(2,1)}, bf16[256,1536]{1,0:T(8,128)(2,1)}, u32[]{:S(2)}, u32[]{:S(2)}) collective-permute-start(bf16[256,1536]{1,0:T(8,128)(2,1)} %pad_maximum_fusion.7), channel_id=1, source_target_pairs={{0,2},{1,3},{2,0},{3,1},{4,6},{5,7},{6,4},{7,5},{8,10},{9,11},{10,... | collective-permute-start | bytes 2359304 | tf_op jit(solution)/shard_map/ppermute | solution.py:364
  272.3 88.5 %all-to-all-start.3 = ((bf16[4,256,2048]{1,2,0:T(8,128)(2,1)}), bf16[4,256,2048]{1,2,0:T(8,128)(2,1)}, u32[]{:S(2)}, u32[]{:S(2)}) async-start(bf16[4,256,2048]{1,2,0:T(8,128)(2,1)} %bitcast.131), calls=%async_computation.3 | async-start | bytes 8388608 | tf_op jit(solution)/shard_map/all_to_all | solution.py:393
  302.6 9.2 %collective-permute-start.30 = (bf16[128,1024]{1,0:T(8,128)(2,1)S(1)}, bf16[128,1024]{1,0:T(8,128)(2,1)S(1)}, u32[]{:S(2)}, u32[]{:S(2)}) collective-permute-start(bf16[128,1024]{1,0:T(8,128)(2,1)S(1)} %select_convert_fusion.4), channel_id=1, source_target_pairs={{0,1},{1,0},{2,3},{3,2},{4,5},{5,4},{6,7},{7,6},{8,9},{9,8},{10,11... | collective-permute-start | bytes 786440 | tf_op jit(solution)/shard_map/ppermute | solution.py:364
  306.5 41.4 %collective-permute-start.46 = (bf16[256,1536]{1,0:T(8,128)(2,1)S(1)}, bf16[256,1536]{1,0:T(8,128)(2,1)S(1)}, u32[]{:S(2)}, u32[]{:S(2)}) collective-permute-start(bf16[256,1536]{1,0:T(8,128)(2,1)S(1)} %add_convert_fusion.a_ref), channel_id=1, source_target_pairs={{0,1},{1,0},{2,3},{3,2},{4,5},{5,4},{6,7},{7,6},{8,9},{9,8},{10,11... | collective-permute-start | bytes 2359304 | tf_op jit(solution)/shard_map/ppermute | solution.py:364
  312.0 28.2 %collective-permute-start.44 = (bf16[320,1024]{1,0:T(8,128)(2,1)S(1)}, bf16[320,1024]{1,0:T(8,128)(2,1)S(1)}, u32[]{:S(2)}, u32[]{:S(2)}) collective-permute-start(bf16[320,1024]{1,0:T(8,128)(2,1)S(1)} %pad_maximum_fusion.8), channel_id=1, source_target_pairs={{0,2},{1,3},{2,0},{3,1},{4,6},{5,7},{6,4},{7,5},{8,10},{9,11},{10,... | collective-permute-start | bytes 1966088 | tf_op jit(solution)/shard_map/ppermute | solution.py:364
  340.4 17.8 %collective-permute-start.45 = (bf16[320,1024]{1,0:T(8,128)(2,1)S(1)}, bf16[320,1024]{1,0:T(8,128)(2,1)S(1)}, u32[]{:S(2)}, u32[]{:S(2)}) collective-permute-start(bf16[320,1024]{1,0:T(8,128)(2,1)S(1)} %add_convert_fusion.1), channel_id=1, source_target_pairs={{0,1},{1,0},{2,3},{3,2},{4,5},{5,4},{6,7},{7,6},{8,9},{9,8},{10,11... | collective-permute-start | bytes 1966088 | tf_op jit(solution)/shard_map/ppermute | solution.py:364
  360.8 7.4 %collective-permute-start.31 = (bf16[768,1024]{1,0:T(8,128)(2,1)S(1)}, bf16[768,1024]{1,0:T(8,128)(2,1)S(1)}, u32[]{:S(2)}, u32[]{:S(2)}) collective-permute-start(bf16[768,1024]{1,0:T(8,128)(2,1)S(1)} %fusion.25), channel_id=1, source_target_pairs={{0,4},{4,0},{8,12},{12,8},{16,20},{20,16},{24,28},{28,24},{1,5},{5... | collective-permute-start | bytes 4718600 | tf_op jit(solution)/shard_map/ppermute | solution.py:364
  366.3 14.3 %collective-permute-start.41 = (bf16[256,1024]{0,1:T(8,128)(2,1)S(1)}, bf16[256,1024]{0,1:T(8,128)(2,1)S(1)}, u32[]{:S(2)}, u32[]{:S(2)}) collective-permute-start(bf16[256,1024]{0,1:T(8,128)(2,1)S(1)} %select_convert_fusion), channel_id=1, source_target_pairs={{0,1},{1,0},{2,3},{3,2},{4,5},{5,4},{6,7},{7,6},{8,9},{9,8},{10,11... | collective-permute-start | bytes 1572872 | tf_op jit(solution)/shard_map/ppermute | solution.py:364
  368.8 3.4 collective-permute-start.34
  372.3 9.3 %collective-permute-start.37 = (f32[18,128]{1,0:T(8,128)S(1)}, f32[18,128]{1,0:T(8,128)S(1)}, u32[]{:S(2)}, u32[]{:S(2)}) collective-permute-start(f32[18,128]{1,0:T(8,128)S(1)} %fusion.48), channel_id=1, source_target_pairs={{0,24},{4,28},{8,16},{12,20},{16,8},{20,12},{24,0},{28,4},{1,25},{... | collective-permute-start | bytes 27656 | tf_op jit(solution)/shard_map/ppermute | solution.py:364
  375.6 6.0 %collective-permute-start.36 = (f32[18,128]{1,0:T(8,128)S(1)}, f32[18,128]{1,0:T(8,128)S(1)}, u32[]{:S(2)}, u32[]{:S(2)}) collective-permute-start(f32[18,128]{1,0:T(8,128)S(1)} %fusion.48), channel_id=1, source_target_pairs={{0,16},{4,20},{8,24},{12,28},{16,0},{20,4},{24,8},{28,12},{1,17},{... | collective-permute-start | bytes 27656 | tf_op jit(solution)/shard_map/ppermute | solution.py:364
  375.6 6.0 %collective-permute-start.35 = (f32[18,128]{1,0:T(8,128)S(1)}, f32[18,128]{1,0:T(8,128)S(1)}, u32[]{:S(2)}, u32[]{:S(2)}) collective-permute-start(f32[18,128]{1,0:T(8,128)S(1)} %fusion.48), channel_id=1, source_target_pairs={{0,8},{4,12},{8,0},{12,4},{16,24},{20,28},{24,16},{28,20},{1,9},{5... | collective-permute-start | bytes 27656 | tf_op jit(solution)/shard_map/ppermute | solution.py:364
  380.8 26.9 %collective-permute-start.42 = (bf16[256,1024]{0,1:T(8,128)(2,1)S(1)}, bf16[256,1024]{0,1:T(8,128)(2,1)S(1)}, u32[]{:S(2)}, u32[]{:S(2)}) collective-permute-start(bf16[256,1024]{0,1:T(8,128)(2,1)S(1)} %add_convert_fusion.3), channel_id=1, source_target_pairs={{0,2},{1,3},{2,0},{3,1},{4,6},{5,7},{6,4},{7,5},{8,10},{9,11},{10,... | collective-permute-start | bytes 1572872 | tf_op jit(solution)/shard_map/ppermute | solution.py:364
  381.8 10.8 %collective-permute-start.38 = (f32[4,128]{1,0:T(4,128)S(1)}, f32[4,128]{1,0:T(4,128)S(1)}, u32[]{:S(2)}, u32[]{:S(2)}) collective-permute-start(f32[4,128]{1,0:T(4,128)S(1)} %maximum_bitcast_fusion.1), channel_id=1, source_target_pairs={{0,1},{1,0},{2,3},{3,2},{4,5},{5,4},{6,7},{7,6},{8,9},{9,8},{10,11... | collective-permute-start | bytes 6152 | tf_op jit(solution)/shard_map/ppermute | solution.py:364
  384.0 34.9 %collective-permute-start.32 = (bf16[256,1024]{1,0:T(8,128)(2,1)S(1)}, bf16[256,1024]{1,0:T(8,128)(2,1)S(1)}, u32[]{:S(2)}, u32[]{:S(2)}) collective-permute-start(bf16[256,1024]{1,0:T(8,128)(2,1)S(1)} %slice.534), channel_id=1, source_target_pairs={{1,0},{2,1},{3,2},{5,4},{6,5},{7,6},{9,8},{10,9},{11,10},{13,12},{... | collective-permute-start | bytes 1572872 | tf_op jit(solution)/shard_map/ppermute | solution.py:367
  392.6 25.2 %collective-permute-start.39 = (f32[4,128]{1,0:T(4,128)S(1)}, f32[4,128]{1,0:T(4,128)S(1)}, u32[]{:S(2)}, u32[]{:S(2)}) collective-permute-start(f32[4,128]{1,0:T(4,128)S(1)} %fusion.47), channel_id=1, source_target_pairs={{0,2},{1,3},{2,0},{3,1},{4,6},{5,7},{6,4},{7,5},{8,10},{9,11},{10,... | collective-permute-start | bytes 6152 | tf_op jit(solution)/shard_map/ppermute | solution.py:364
  407.9 13.3 %collective-permute-start.43 = (bf16[256,1024]{0,1:T(8,128)(2,1)S(1)}, bf16[256,1024]{0,1:T(8,128)(2,1)S(1)}, u32[]{:S(2)}, u32[]{:S(2)}) collective-permute-start(bf16[256,1024]{0,1:T(8,128)(2,1)S(1)} %add_convert_fusion.2), channel_id=1, source_target_pairs={{0,1},{1,0},{2,3},{3,2},{4,5},{5,4},{6,7},{7,6},{8,9},{9,8},{10,11... | collective-permute-start | bytes 1572872 | tf_op jit(solution)/shard_map/ppermute | solution.py:364
  419.8 15.8 %collective-permute-start.33 = (bf16[256,1024]{1,0:T(8,128)(2,1)}, bf16[256,1024]{1,0:T(8,128)(2,1)}, u32[]{:S(2)}, u32[]{:S(2)}) collective-permute-start(bf16[256,1024]{1,0:T(8,128)(2,1)} %fusion.32), channel_id=1, source_target_pairs={{1,0},{2,1},{3,2},{5,4},{6,5},{7,6},{9,8},{10,9},{11,10},{13,12},{... | collective-permute-start | bytes 1572872 | tf_op jit(solution)/shard_map/ppermute | solution.py:367
  (60 other events, 221.9 us)
